TPU v7x, 32 devices: a whole 2x2x4 slice. The times are simulated.
32 devices in a mesh: dp: 8 (over z, y), tensor: 4 (over x, core).
Axes of the slice: x: 2, y: 2, z: 4, core: 2. Of those that a mesh axis runs over, the one named last changes fastest.
Arguments:
- tokens: bfloat16 [8192, 1024], P('dp'), may hold values from -6 to 6
- cotangent: bfloat16 [8192, 1024], P('dp'), may hold values from -6 to 6
- norm_params: float32 [4, 1024], replicated, may hold values from 0.25 to 1.75
- attention_weight: bfloat16 [1024, 3, 1024], P('dp', None, 'tensor'), may hold values from -0.1875 to 0.1875
- attention_bias: float32 [3, 1024], P(None, 'tensor'), may hold values from -3 to 3
- merge_weight: bfloat16 [1024, 1024], P('dp', 'tensor'), may hold values from -1.5 to 1.5
- branch_bias: float32 [2, 1024], replicated, may hold values from -3 to 3
- up_weight: bfloat16 [1024, 4096], P('dp', 'tensor'), may hold values from -0.1875 to 0.1875
- up_bias: float32 [4096], P('tensor'), may hold values from -3 to 3
- down_weight: bfloat16 [1024, 4096], P('dp', 'tensor'), may hold values from -0.09375 to 0.09375
- prefix_ids: int32 [10], replicated, may hold values from 0 to 9, each once
- prefix_table: float32 [10, 1024], replicated, may hold values from -1.25 to 1.25
- encoder_weight: float32 [1024, 512], P('dp'), may hold values from -0.625 to 0.625
- encoder_bias: float32 [512], replicated, may hold values from -0.625 to 0.625
- decoder_weight: float32 [512, 2, 1024], P('dp', None, 'tensor'), may hold values from -0.625 to 0.625
- decoder_bias: float32 [2, 1024], P(None, 'tensor'), may hold values from -0.625 to 0.625
- first_table: float32 [10, 1024], replicated, may hold values from -1.9073486e-06 to 1.9073486e-06
- second_table: float32 [10, 1024], replicated, may hold values from 5.3138434e-15 to 8.5369944e-14
- first_encoder: float32 [1024, 512], P('dp'), may hold values from -5.9604645e-07 to 5.9604645e-07
- second_encoder: float32 [1024, 512], P('dp'), may hold values from 3.8329363e-16 to 6.0978533e-15
- first_encoder_bias: float32 [512], replicated, may hold values from -3.33786e-06 to 3.33786e-06
- second_encoder_bias: float32 [512], replicated, may hold values from 1.0540575e-14 to 1.6899766e-13
- first_decoder: float32 [512, 2, 1024], P('dp', None, 'tensor'), may hold values from -4.7683716e-07 to 4.7683716e-07
- second_decoder: float32 [512, 2, 1024], P('dp', None, 'tensor'), may hold values from 2.230072e-16 to 3.5716e-15
- first_decoder_bias: float32 [2, 1024], P(None, 'tensor'), may hold values from -9.536743e-07 to 9.536743e-07
- second_decoder_bias: float32 [2, 1024], P(None, 'tensor'), may hold values from 8.885443e-16 to 1.42864e-14
Outputs:
- output: bfloat16 [8192, 1024], P(('dp', 'tensor'))
- input_grad: bfloat16 [8192, 1024], P(('dp', 'tensor'))
- grad_norm: float32 [], replicated
- new_table: float32 [10, 1024], replicated
- new_first_table: float32 [10, 1024], replicated
- new_second_table: float32 [10, 1024], replicated
- new_encoder: float32 [1024, 512], P('dp')
- new_first_encoder: float32 [1024, 512], P('dp')
- new_second_encoder: float32 [1024, 512], P('dp')
- new_encoder_bias: float32 [512], replicated
- new_first_encoder_bias: float32 [512], replicated
- new_second_encoder_bias: float32 [512], replicated
- new_decoder: float32 [512, 2, 1024], P('dp', None, 'tensor')
- new_first_decoder: float32 [512, 2, 1024], P('dp', None, 'tensor')
- new_second_decoder: float32 [512, 2, 1024], P('dp', None, 'tensor')
- new_decoder_bias: float32 [2, 1024], P(None, 'tensor')
- new_first_decoder_bias: float32 [2, 1024], P(None, 'tensor')
- new_second_decoder_bias: float32 [2, 1024], P(None, 'tensor')
Inputs may be any that keep to these rules, and one draw needn't show every extreme that they name: `prefix_ids`: every table row is used by exactly one prefix position.
All inputs are finite; a program needn't handle non-finite values.
Results may differ from a plain program's by a relative error of at most 0.017.
Values may be sent and summed in bfloat16 or wider, within the bound.
No kernel may reach another device: no remote copies, remote signals or barrier semaphores. Data moves between devices by JAX's collectives and lax.ppermute only.
A program may use at most 128 MiB of HBM per device.

v0:
```python
import functools

import jax
import jax.numpy as jnp
from jax import lax
from jax.experimental import pallas as pl
from jax.experimental.pallas import tpu as pltpu
from jax.sharding import PartitionSpec as P

HD = 64
PRE = 10
PAD = 16
STEP = 10
TILE = 256


NORM_EPS = 1e-05
CLIP_LIMIT = 0.001
LEARN_RATE = 0.05
WEIGHT_DECAY = 0.01
BETA_FIRST = 0.9
BETA_SECOND = 0.999
ADAM_EPS = 1e-08
MASKED = -1e30
GELU_COEF = 0.7978845608028654

NN = ((1,), (0,))
NT = ((1,), (1,))
TN = ((0,), (0,))
OWN, CORE, SIDE, BOTH = 0, 1, 2, 3


def dot(left, right, dims, precision=None):
    return lax.dot_general(
        left, right, (dims, ((), ())), precision=precision, preferred_element_type=jnp.float32
    )


def shaped(shape, dtype):
    return jax.ShapeDtypeStruct(shape, dtype)


def cost(flops, *arrays):
    size = sum(a.size * a.dtype.itemsize for a in arrays)
    return pl.CostEstimate(flops=flops, transcendentals=0, bytes_accessed=size)


def norm_parts(rows):
    offsets = rows - jnp.mean(rows, axis=-1, keepdims=True)
    scale = lax.rsqrt(jnp.mean(offsets * offsets, axis=-1, keepdims=True) + NORM_EPS)
    return offsets * scale, scale


def norm_back(rows, gain, grad):
    unit, scale = norm_parts(rows)
    grad = grad * gain
    mean = jnp.mean(grad, axis=-1, keepdims=True)
    along = jnp.mean(grad * unit, axis=-1, keepdims=True)
    return scale * (grad - mean - unit * along)


def adam_update(weight, grad, first, second, factor):
    clipped = grad * factor
    new_first = BETA_FIRST * first + (1.0 - BETA_FIRST) * clipped
    new_second = BETA_SECOND * second + (1.0 - BETA_SECOND) * clipped * clipped
    fix_first = 1.0 - BETA_FIRST**STEP
    fix_second = 1.0 - BETA_SECOND**STEP
    new_weight = weight * (1.0 - LEARN_RATE * WEIGHT_DECAY) - LEARN_RATE * (
        new_first / fix_first
    ) / (jnp.sqrt(new_second / fix_second) + ADAM_EPS)
    return (new_weight, new_first, new_second)


def swap(values, axis, bits):
    size = lax.axis_size(axis)
    return lax.ppermute(values, axis, [(i, i ^ bits) for i in range(size)])


def after(values, *others):
    return lax.optimization_barrier((values, *others))[0]


def placed(found):
    refs, bits = found
    if bits is None:
        return [(refs[0].at[i], i) for i in range(refs[0].shape[0])]
    here = lax.axis_index("dp")
    return [
        (ref.at[i], lax.bitwise_xor(here, differ))
        for ref, group in zip(refs, bits, strict=True)
        for i, differ in enumerate(group)
    ]


def joined(*pieces):
    return jnp.concatenate(pieces)


def sum_over(values, axis):
    bits = 1
    while bits < lax.axis_size(axis):
        values = values + swap(values, axis, bits)
        bits *= 2
    return values


def assemble_into(outs, found):
    for piece, place in placed(found):
        start = 0
        for out in outs:
            parts, rows = out.shape[0], out.shape[1] // lax.axis_size("dp")
            for part in range(parts):
                where = pl.ds(pl.multiple_of(place * rows, rows), rows)
                out[part, where, :] = piece[start : start + rows, :]
                start += rows


def assemble_kernel(bits, *refs):
    assemble_into(refs[-1:], (refs[:-1], bits))


def assemble(gathered, shape):
    pieces, bits = gathered
    out = shaped(shape, pieces[0].dtype)
    return pl.pallas_call(
        functools.partial(assemble_kernel, bits),
        out_shape=out,
        name="assemble",
        cost_estimate=cost(0, *pieces, out),
    )(*pieces)


def merge_weight_kernel(bits, *refs):
    pieces, (weight, encoded) = refs[:-2], refs[-2:]
    rows = weight.shape[0] // lax.axis_size("dp")
    sums = None
    for piece, place in placed((pieces, bits)):
        weight[pl.ds(pl.multiple_of(place * rows, rows), rows), :] = piece[:rows, :]
        sent = piece[rows:, :].astype(jnp.float32)
        sums = sent if sums is None else sums + sent
    width = weight.shape[1]
    for i in range(encoded.shape[1] // width):
        encoded[:, i * width : (i + 1) * width] = sums[i * PAD : (i + 1) * PAD]


def gather_merge(pieces, bits, rows, hidden):
    outs = (shaped((rows, pieces[0].shape[-1]), jnp.bfloat16), shaped((PAD, hidden), jnp.float32))
    return pl.pallas_call(
        functools.partial(merge_weight_kernel, bits),
        out_shape=outs,
        name="gather_merge",
        cost_estimate=cost(0, *pieces, *outs),
    )(*pieces)


def project_kernel(bits, tokens, norms, bias, *refs):
    pieces, (projected, attend, decoder) = refs[:-3], refs[-3:]
    assemble_into((attend, decoder), (pieces, bits))
    for start in range(0, tokens.shape[0], TILE):
        rows = slice(start, start + TILE)
        unit, _ = norm_parts(tokens[rows, :].astype(jnp.float32))
        normed = (unit * norms[0:1, :] + norms[1:2, :]).astype(jnp.bfloat16)
        for part in range(3):
            total = dot(normed, attend[part], NN) + bias[part : part + 1, :]
            projected[part, rows, :] = total.astype(jnp.bfloat16)


def project(tokens, norms, bias, gathered, hidden):
    pieces, bits = gathered
    rows, width = tokens.shape
    local = bias.shape[1]
    outs = (
        shaped((3, rows, local), jnp.bfloat16),
        shaped((3, width, local), jnp.bfloat16),
        shaped((2, hidden, local), jnp.bfloat16),
    )
    return pl.pallas_call(
        functools.partial(project_kernel, bits),
        out_shape=outs,
        name="project",
        cost_estimate=cost(6 * rows * width * local, tokens, *pieces, *outs),
    )(tokens, norms, bias, *pieces)


def down_kernel(bits, cotangent, *refs):
    pieces, (down, grad) = refs[:-2], refs[-2:]
    assemble_into((down,), (pieces, bits))
    for start in range(0, cotangent.shape[0], TILE):
        rows = slice(start, start + TILE)
        grad[rows, :] = dot(cotangent[rows, :], down[0], NN).astype(jnp.bfloat16)


def down_back(cotangent, gathered):
    pieces, bits = gathered
    rows, width = cotangent.shape
    units = pieces[0].shape[-1]
    outs = (shaped((1, width, units), jnp.bfloat16), shaped((rows, units), jnp.bfloat16))
    return pl.pallas_call(
        functools.partial(down_kernel, bits),
        out_shape=outs,
        name="down_back",
        cost_estimate=cost(2 * rows * width * units, cotangent, *pieces, *outs),
    )(cotangent, *pieces)


def prefix_kernel(encoded, encoder_bias, decoder, decoder_bias, hidden, prefix):
    held = jnp.tanh(encoded[...] + encoder_bias[...])
    hidden[...] = held
    low = held.astype(jnp.bfloat16)
    for part in range(2):
        total = dot(low, decoder[part], NN) + decoder_bias[part : part + 1, :]
        prefix[part] = total.astype(jnp.bfloat16)


def attend_kernel(first, proj, prefix, mix, sums, mixed):
    rows, width = mix.shape
    lane = lax.broadcasted_iota(jnp.int32, (1, width), 1) // HD
    pre_col = lax.broadcasted_iota(jnp.int32, (TILE, PAD), 1)
    below = lax.broadcasted_iota(jnp.int32, (TILE, TILE), 0) >= lax.broadcasted_iota(
        jnp.int32, (TILE, TILE), 1
    )
    sum_col = lax.broadcasted_iota(jnp.int32, (TILE, 128), 1)
    sums[...] = jnp.zeros_like(sums)
    mixed[...] = jnp.zeros_like(mixed)

    def one_head(head, carry):
        mine = lane == head
        for start in range(first, first + rows, TILE):
            here = slice(start, start + TILE)
            there = slice(start - first, start - first + TILE)
            query = proj[0, here, :] * jnp.asarray(HD**-0.5, jnp.bfloat16)
            one = jnp.where(mine, query, jnp.zeros_like(query))
            scores = [
                jnp.where(pre_col < PRE, dot(one, prefix[0], NT), MASKED),
                jnp.where(below, dot(one, proj[1, here, :], NT), MASKED),
            ]
            values = [prefix[1], proj[2, here, :]]
            if start:
                scores.append(dot(one, proj[1, :start, :], NT))
                values.append(proj[2, :start, :])
            top = functools.reduce(jnp.maximum, [jnp.max(s, 1, keepdims=True) for s in scores])
            exps = [jnp.exp(s - top) for s in scores]
            total = sum(jnp.sum(e, 1, keepdims=True) for e in exps)
            inverse = 1.0 / total
            part = sum(
                dot((e * inverse).astype(jnp.bfloat16), v, NN)
                for e, v in zip(exps, values, strict=True)
            )
            mixed[there, :] = jnp.where(mine, part, mixed[there, :])
            sums[there, :] = jnp.where(sum_col == head, top + jnp.log(total), sums[there, :])
        return carry

    lax.fori_loop(0, width // HD, one_head, 0)
    mix[...] = mixed[...].astype(jnp.bfloat16)


def attend_first_kernel(proj, encoded, encoder_bias, decoder, decoder_bias, mix, sums, hidden, prefix, mixed):
    prefix_kernel(encoded, encoder_bias, decoder, decoder_bias, hidden, prefix)
    attend_kernel(0, proj, prefix, mix, sums, mixed)


def attend_shapes(proj):
    _, rows, width = proj.shape
    return shaped((rows // 2, width), jnp.bfloat16), shaped((rows // 2, 128), jnp.float32)


def attend_first(proj, encoded, encoder_bias, decoder, decoder_bias):
    _, rows, width = proj.shape
    outs = (
        *attend_shapes(proj),
        shaped(encoded.shape, jnp.float32),
        shaped((2, PAD, width), jnp.bfloat16),
    )
    return pl.pallas_call(
        attend_first_kernel,
        out_shape=outs,
        scratch_shapes=[pltpu.VMEM((rows // 2, width), jnp.float32)],
        name="attend_first",
        cost_estimate=cost(5 * width // HD * rows * rows * width // 6, proj, *outs),
    )(proj, encoded, encoder_bias, decoder, decoder_bias)


def attend_second(proj, prefix):
    _, rows, width = proj.shape
    outs = attend_shapes(proj)
    return pl.pallas_call(
        functools.partial(attend_kernel, rows // 2),
        out_shape=outs,
        scratch_shapes=[pltpu.VMEM((rows // 2, width), jnp.float32)],
        name="attend_second",
        cost_estimate=cost(5 * width // HD * rows * rows * width // 3, proj, *outs),
    )(proj, prefix)


def attend_back_kernel(
    proj, prefix, mix_first, mix_second, sums_first, sums_second, own, core, side, both, gproj, gprefix, *scratch
):
    gmix, gquery, gkey, gvalue, log_sums, inner, keys_col, pre_col = scratch
    rows, width = gmix.shape
    half = rows // 2
    quarter = own.shape[0]
    me = lax.axis_index("tensor")
    for piece, bits in ((own, OWN), (core, CORE), (side, SIDE), (both, BOTH)):
        place = lax.bitwise_xor(me, bits) * quarter
        gmix[pl.ds(pl.multiple_of(place, quarter), quarter), :] = piece[...]
    lane = lax.broadcasted_iota(jnp.int32, (1, width), 1) // HD
    pre_row = lax.broadcasted_iota(jnp.int32, (PAD, TILE), 0)
    seen = lax.broadcasted_iota(jnp.int32, (TILE, TILE), 0) <= lax.broadcasted_iota(
        jnp.int32, (TILE, TILE), 1
    )
    scale = jnp.asarray(HD**-0.5, jnp.bfloat16)
    head_of = lax.broadcasted_iota(jnp.int32, (8, width), 0) == lax.broadcasted_iota(
        jnp.int32, (8, width), 1
    ) // HD
    for i, (mix, sums) in enumerate(((mix_first, sums_first), (mix_second, sums_second))):
        part = slice(i * half, (i + 1) * half)
        log_sums[:, part] = sums[...].T[:8]
        product = gmix[part, :].astype(jnp.float32) * mix[...].astype(jnp.float32)
        inner[:, part] = dot(head_of.astype(jnp.float32), product, NT, lax.Precision.HIGHEST)
    keys_col[...] = (proj[1] * scale).T
    pre_col[...] = (prefix[0] * scale).T
    gkey[...] = jnp.zeros_like(gkey)
    gvalue[...] = jnp.zeros_like(gvalue)
    gprefix[...] = jnp.zeros_like(gprefix)

    def one_head(head, carry):
        mine = lane == head
        cols = pl.ds(pl.multiple_of(head * HD, HD), HD)
        for start in range(0, rows, TILE):
            here = slice(start, start + TILE)
            query = proj[0, here, :] * scale
            grad = gmix[here, :]
            one = jnp.where(mine, query, jnp.zeros_like(query))
            one_grad = jnp.where(mine, grad, jnp.zeros_like(grad))
            log_sum = log_sums[pl.ds(head, 1), here]
            shared = inner[pl.ds(head, 1), here]

            def block(keys, values, shown):
                scores = dot(keys, one, NT)
                if shown is not None:
                    scores = jnp.where(shown, scores, MASKED)
                prob = jnp.exp(scores - log_sum)
                dscore = (prob * (dot(values, one_grad, NT) - shared)).astype(jnp.bfloat16)
                return dscore, dot(dscore, one, NN), dot(prob.astype(jnp.bfloat16), one_grad, NN)

            dscore, dkey, dvalue = block(prefix[0], prefix[1], pre_row < PRE)
            gprefix[0] += dkey
            gprefix[1] += dvalue
            dquery = dot(pre_col[cols, :], dscore, NN)
            for at in range(0, start + TILE, TILE):
                there = slice(at, at + TILE)
                dscore, dkey, dvalue = block(
                    proj[1, there, :], proj[2, there, :], seen if at == start else None
                )
                gkey[there, :] += dkey
                gvalue[there, :] += dvalue
                dquery = dquery + dot(keys_col[cols, there], dscore, NN)
            gquery[cols, here] = dquery
        return carry

    lax.fori_loop(0, width // HD, one_head, 0)
    gproj[0] = gquery[...].T.astype(jnp.bfloat16)
    gproj[1] = gkey[...].astype(jnp.bfloat16)
    gproj[2] = gvalue[...].astype(jnp.bfloat16)


def attend_back(proj, prefix, mixes, sums, pieces):
    _, rows, width = proj.shape
    outs = (shaped(proj.shape, jnp.bfloat16), shaped(prefix.shape, jnp.float32))
    return pl.pallas_call(
        attend_back_kernel,
        out_shape=outs,
        scratch_shapes=[
            pltpu.VMEM((rows, width), jnp.bfloat16),
            pltpu.VMEM((width, rows), jnp.float32),
            pltpu.VMEM((rows, width), jnp.float32),
            pltpu.VMEM((rows, width), jnp.float32),
            pltpu.VMEM((8, rows), jnp.float32),
            pltpu.VMEM((8, rows), jnp.float32),
            pltpu.VMEM((width, rows), jnp.bfloat16),
            pltpu.VMEM((width, PAD), jnp.bfloat16),
        ],
        name="attend_back",
        cost_estimate=cost(12 * width // HD * rows * rows * width // 2, proj, *mixes, *sums, *outs),
    )(proj, prefix, *mixes, *sums, *pieces)


def merge_kernel(first, tokens, norms, branch, *refs):
    mixes, merges, earlier, (normed, resid_own) = refs[:4], refs[4:8], refs[8:-2], refs[-2:]
    i = pl.program_id(0)
    merged = sum(dot(m[...], w[...], NT) for m, w in zip(mixes, merges, strict=True))
    resid = tokens[...].astype(jnp.float32) + merged + branch[0:1, :]
    unit, _ = norm_parts(resid)
    normed[...] = (unit * norms[2:3, :] + norms[3:4, :]).astype(jnp.bfloat16)
    if earlier:

        @pl.when(i == 0)
        def _():
            resid_own[...] = earlier[1][...]

    @pl.when(i + first == lax.axis_index("tensor"))
    def _():
        resid_own[...] = resid


def merge_half(tokens, norms, branch, mixes, merges, earlier=()):
    rows, width = tokens.shape
    share = rows // lax.axis_size("tensor")
    local = mixes[0].shape[1]
    steps = mixes[0].shape[0] // share
    first = steps if earlier else 0
    whole = lambda a: pl.BlockSpec(a.shape, lambda i: (0,) * a.ndim)
    outs = (shaped((rows, width), jnp.bfloat16), shaped((share, width), jnp.float32))
    return pl.pallas_call(
        functools.partial(merge_kernel, first),
        grid=(steps,),
        in_specs=[pl.BlockSpec((share, width), lambda i: (i + first, 0)), whole(norms), whole(branch)]
        + [pl.BlockSpec((share, local), lambda i: (i, 0))] * 4
        + [whole(w) for w in merges]
        + ([pl.BlockSpec(memory_space=pl.ANY), whole(earlier[1])] if earlier else []),
        out_specs=(
            pl.BlockSpec((share, width), lambda i: (i + first, 0)),
            pl.BlockSpec((share, width), lambda i: (0, 0)),
        ),
        out_shape=outs,
        input_output_aliases={11: 0} if earlier else {},
        name="merge_second" if earlier else "merge_first",
        cost_estimate=cost(4 * rows * width * local, *mixes, *merges, *outs),
    )(tokens, norms, branch, *mixes, *merges, *earlier)


def feed_rows(normed, ghidden, up, bias, act, part, plus=None):
    value = dot(normed[...], up, NN) + bias[...]
    square = value * value
    tanh = jnp.tanh(GELU_COEF * value * (1.0 + 0.044715 * square))
    act[...] = (0.5 * value * (1.0 + tanh)).astype(jnp.bfloat16)
    slope = 0.5 * (1.0 + tanh) + 0.5 * GELU_COEF * value * (1.0 - tanh * tanh) * (
        1.0 + 3.0 * 0.044715 * square
    )
    gpre = (ghidden[...].astype(jnp.float32) * slope).astype(jnp.bfloat16)
    total = dot(gpre, up, NT)
    if plus is not None:
        total = total + plus[...].astype(jnp.float32)
    part[...] = total.astype(jnp.bfloat16)


def feed_first_kernel(bits, normed, ghidden, bias, *refs):
    pieces, (act, part, up) = refs[:-3], refs[-3:]
    assemble_into((up,), (pieces, bits))
    feed_rows(normed, ghidden, up[0], bias, act, part)


def feed_kernel(count, up, bias, *refs):
    rows, plus, outs = refs[: 2 * count], refs[2 * count : -2 * count], refs[-2 * count :]
    for i in range(count):
        feed_rows(rows[2 * i], rows[2 * i + 1], up[0], bias, outs[2 * i], outs[2 * i + 1], *plus)


def block_of(differ):
    return lambda i: (lax.bitwise_xor(lax.axis_index("tensor"), differ), 0)


def whole_spec(a):
    return pl.BlockSpec(a.shape, lambda i: (0,) * a.ndim)


def feed_first(bits, normed, ghidden, gathered, bias):
    pieces, places = gathered
    rows, width = normed.shape
    share = rows // lax.axis_size("tensor")
    units = pieces[0].shape[-1]
    outs = (
        shaped((share, units), jnp.bfloat16),
        shaped((share, width), jnp.bfloat16),
        shaped((1, width, units), jnp.bfloat16),
    )
    return pl.pallas_call(
        functools.partial(feed_first_kernel, places),
        grid=(1,),
        in_specs=[
            pl.BlockSpec((share, width), block_of(bits)),
            pl.BlockSpec((share, units), block_of(bits)),
            whole_spec(bias),
        ]
        + [whole_spec(p) for p in pieces],
        out_specs=[whole_spec(o) for o in outs],
        out_shape=outs,
        name="feed_first",
        cost_estimate=cost(4 * share * width * units, *pieces, *outs),
    )(normed, ghidden, bias, *pieces)


def feed(bits, normed, ghidden, up, bias, *plus):
    rows, width = normed.shape
    share = rows // lax.axis_size("tensor")
    units = up.shape[-1]
    outs = [shaped((share, units), jnp.bfloat16), shaped((share, width), jnp.bfloat16)] * len(bits)
    specs = []
    for differ in bits:
        specs.append(pl.BlockSpec((share, width), block_of(differ)))
        specs.append(pl.BlockSpec((share, units), block_of(differ)))
    return pl.pallas_call(
        functools.partial(feed_kernel, len(bits)),
        grid=(1,),
        in_specs=[whole_spec(up), whole_spec(bias), *specs] + [whole_spec(p) for p in plus],
        out_specs=[whole_spec(o) for o in outs],
        out_shape=outs,
        name="feed",
        cost_estimate=cost(4 * len(bits) * share * width * units, up, *outs),
    )(up, bias, *[normed, ghidden] * len(bits), *plus)


def back_kernel(count, weight, *refs):
    rows, plus, outs = refs[:count], refs[count:-count], refs[-count:]
    for grad, out in zip(rows, outs, strict=True):
        total = sum(dot(grad[i], weight[i], NT) for i in range(weight.shape[0]))
        for one in plus:
            total = total + one[...].astype(jnp.float32)
        out[...] = total.astype(jnp.bfloat16)


def project_back(bits, gproj, attend, *plus):
    _, rows, local = gproj.shape
    width = attend.shape[1]
    share = rows // lax.axis_size("tensor")
    outs = [shaped((share, width), jnp.bfloat16)] * len(bits)
    specs = [
        pl.BlockSpec((3, share, local), lambda i, block=block_of(differ): (0, *block(i)))
        for differ in bits
    ]
    return pl.pallas_call(
        functools.partial(back_kernel, len(bits)),
        grid=(1,),
        in_specs=[whole_spec(attend), *specs] + [whole_spec(p) for p in plus],
        out_specs=[whole_spec(o) for o in outs],
        out_shape=outs,
        name="project_back",
        cost_estimate=cost(6 * len(bits) * share * local * width, attend, *outs),
    )(attend, *[gproj] * len(bits), *plus)


def three(own, core, side):
    return own[...].astype(jnp.float32) + core[...].astype(jnp.float32) + side[...].astype(jnp.float32)


def middle_kernel(own, core, side, cotangent, resid, norms, *refs):
    merges, (gresid, keep, send) = refs[:4], refs[4:]
    total = three(own, core, side)
    grad = cotangent[...].astype(jnp.float32) + norm_back(resid[...], norms[2:3, :], total)
    gresid[...] = grad
    low = grad.astype(jnp.bfloat16)
    keep[0] = dot(low, merges[OWN][...], NN).astype(jnp.bfloat16)
    keep[1] = dot(low, merges[CORE][...], NN).astype(jnp.bfloat16)
    send[0] = dot(low, merges[SIDE][...], NN).astype(jnp.bfloat16)
    send[1] = dot(low, merges[BOTH][...], NN).astype(jnp.bfloat16)


def middle(own, core, side, cotangent, resid, norms, merges):
    share, width = resid.shape
    local = merges[0].shape[1]
    outs = (
        shaped((share, width), jnp.float32),
        shaped((2, share, local), jnp.bfloat16),
        shaped((2, share, local), jnp.bfloat16),
    )
    mine = pl.BlockSpec((share, width), block_of(OWN))
    return pl.pallas_call(
        middle_kernel,
        grid=(1,),
        in_specs=[whole_spec(own), whole_spec(core), whole_spec(side), mine]
        + [whole_spec(a) for a in (resid, norms, *merges)],
        out_specs=[whole_spec(o) for o in outs],
        out_shape=outs,
        name="middle",
        cost_estimate=cost(8 * share * width * local, resid, *merges, *outs),
    )(own, core, side, cotangent, resid, norms, *merges)


def last_kernel(own, core, side, tokens, gresid, norms, out):
    total = three(own, core, side)
    rows = tokens[...].astype(jnp.float32)
    out[...] = (gresid[...] + norm_back(rows, norms[0:1, :], total)).astype(jnp.bfloat16)


def last(own, core, side, tokens, gresid, norms):
    share, width = gresid.shape
    out = shaped((share, width), jnp.bfloat16)
    return pl.pallas_call(
        last_kernel,
        grid=(1,),
        in_specs=[
            whole_spec(own),
            whole_spec(core),
            whole_spec(side),
            pl.BlockSpec((share, width), block_of(OWN)),
            whole_spec(gresid),
            whole_spec(norms),
        ],
        out_specs=whole_spec(out),
        out_shape=out,
        name="last",
        cost_estimate=cost(0, core, side, gresid, out),
    )(own, core, side, tokens, gresid, norms)


def tail_kernel(total, hidden, decoder, joint):
    low = total[...].astype(jnp.bfloat16)
    held = hidden[...].astype(jnp.bfloat16)
    part = jnp.zeros(joint.shape, jnp.float32)
    square = jnp.zeros((1, 1), jnp.float32)
    for i in range(2):
        part = part + dot(low[i], decoder[i], NT)
        grad = dot(held, low[i], TN)
        square = square + jnp.sum(jnp.sum(grad * grad, 0, keepdims=True), 1, keepdims=True)
        bias = jnp.sum(low[i].astype(jnp.float32), 0, keepdims=True)
        square = square + jnp.sum(bias * bias, 1, keepdims=True)
    row = lax.broadcasted_iota(jnp.int32, joint.shape, 0)
    joint[...] = jnp.where(row == PAD - 1, square, part)


def update_kernel(joint, hidden, hidden_own, total, selected, selected_own, onehot, encoder, *refs):
    table, enc, enc_bias, dec, dec_bias = (refs[i : i + 3] for i in range(0, 15, 3))
    norm_out, outs = refs[15], refs[16:]
    held = hidden[...]
    row = lax.broadcasted_iota(jnp.int32, held.shape, 0)
    grad = jnp.where(row < PRE, joint[...], 0.0) * (1.0 - held * held)
    grad = grad.astype(jnp.bfloat16)
    square = joint[PAD - 1 : PAD, 0:1]

    def summed(values):
        return jnp.sum(jnp.sum(values * values, 0, keepdims=True), 1, keepdims=True)

    square = square + summed(dot(selected[...], grad, TN))
    grad_bias = jnp.sum(grad.astype(jnp.float32), 0, keepdims=True)
    square = square + summed(grad_bias)
    grad_selected = dot(grad, encoder[...], NT)
    grad_table = dot(onehot[...], grad_selected, TN, lax.Precision.HIGHEST)[:PRE]
    square = square + summed(grad_table)
    norm = jnp.sqrt(square)
    norm_out[...] = norm
    factor = CLIP_LIMIT / (norm + 1e-06)

    def update(old, grad_of, at, index):
        weight, first, second = (ref[index] for ref in old)
        for out, new in zip(
            outs[at : at + 3], adam_update(weight, grad_of, first, second, factor), strict=True
        ):
            out[index] = new

    update(table, grad_table, 0, ...)
    update(enc, dot(selected_own[...], grad, TN), 3, ...)
    update(enc_bias, grad_bias, 6, ...)
    low = total[...].astype(jnp.bfloat16)
    held_own = hidden_own[...].astype(jnp.bfloat16)
    for i in range(2):
        update(dec, dot(held_own, low[i], TN), 9, (slice(None), i, slice(None)))
        bias = jnp.sum(low[i].astype(jnp.float32), 0, keepdims=True)
        update(dec_bias, bias, 12, (slice(i, i + 1), slice(None)))


def on_device(
    tokens,
    cotangent,
    norm_params,
    attention_weight,
    attention_bias,
    merge_weight,
    branch_bias,
    up_weight,
    up_bias,
    down_weight,
    prefix_ids,
    prefix_table,
    encoder_weight,
    encoder_bias,
    decoder_weight,
    decoder_bias,
    first_table,
    second_table,
    first_encoder,
    second_encoder,
    first_encoder_bias,
    second_encoder_bias,
    first_decoder,
    second_decoder,
    first_decoder_bias,
    second_decoder_bias,
):
    highest = lax.Precision.HIGHEST
    dp_index = lax.axis_index("dp")
    rows, width = tokens.shape
    share = rows // lax.axis_size("tensor")
    local = merge_weight.shape[1]
    units = up_weight.shape[1]
    in_rows = attention_weight.shape[0]
    hidden_size = encoder_weight.shape[1]
    dec_rows = decoder_weight.shape[0]
    halves = hidden_size // local

    decoder_low = decoder_weight.astype(jnp.bfloat16)
    attention = jnp.concatenate(
        [
            attention_weight.transpose(1, 0, 2).reshape(3 * in_rows, local),
            decoder_low.transpose(1, 0, 2).reshape(2 * dec_rows, local),
        ]
    )
    onehot = (
        jnp.pad(prefix_ids, (0, PAD - PRE), constant_values=PAD)[:, None]
        == jnp.arange(PAD, dtype=jnp.int32)[None, :]
    ).astype(jnp.float32)
    selected = jnp.dot(onehot[:, :PRE], prefix_table, precision=highest).astype(jnp.bfloat16)
    selected_own = lax.dynamic_slice_in_dim(selected, dp_index * in_rows, in_rows, 1)
    encoder_low = encoder_weight.astype(jnp.bfloat16)
    encoded_own = jnp.dot(selected_own, encoder_low, preferred_element_type=jnp.float32)
    sent = encoded_own.astype(jnp.bfloat16).reshape(PAD, halves, local).transpose(1, 0, 2)
    merging = jnp.concatenate([merge_weight, sent.reshape(halves * PAD, local)])

    small = lax.axis_size("dp") == 8
    if small:
        y, z, far = 1, 2, 4
        attention_far = swap(attention, "dp", far)
        merging_side = swap(merging, "dp", y)[None]
        down_side = swap(down_weight, "dp", y)[None]
        up_side = swap(up_weight, "dp", y)[None]
        pair = jnp.stack([attention, attention_far])
        near = swap(pair, "dp", z)
        pair_side = swap(pair, "dp", y)
        merging_pair = joined(merging[None], merging_side)
        merging_far = swap(after(merging_pair, attention_far), "dp", far)
        near_side = swap(after(near, merging_far), "dp", y)
        attention = ((pair, near, pair_side, near_side), ((0, 4), (2, 6), (1, 5), (3, 7)))
        merging_quad = joined(merging_pair, merging_far)
        merging_near = swap(merging_quad, "dp", z)
        merging = ((merging_quad, merging_near), ((0, 1, 4, 5), (2, 3, 6, 7)))
        down_far = swap(after(down_weight, near), "dp", far)[None]
    else:
        gathered = lambda shard: ((lax.all_gather(shard, "dp", axis=0),), None)
        attention, merging, down, up, encoder = map(
            gathered, (attention, merging, down_weight, up_weight, encoder_low)
        )

    projected, attend_full, decoder_full = project(
        tokens, norm_params, attention_bias, attention, hidden_size
    )
    if small:
        down_far = after(down_far, projected)
        down_near = swap(joined(down_weight[None], down_far), "dp", z)
        down_far_side = swap(down_far, "dp", y)
        up_far = swap(after(up_weight, down_far), "dp", far)[None]
    merge_own, encoded = gather_merge(after(merging[0], projected), merging[1], width, hidden_size)
    mix_first, sums_first, hidden, prefix = attend_first(
        projected, encoded, encoder_bias[None], decoder_full, decoder_bias
    )

    def from_others(values):
        side = swap(values, "tensor", SIDE)
        return [values, swap(values, "tensor", CORE), side, swap(side, "tensor", CORE)]

    merges = from_others(merge_own)
    mixes_first = from_others(mix_first)
    mix_second, sums_second = attend_second(projected, prefix)
    mixes_second = from_others(mix_second)
    if small:
        down_near = after(down_near, mix_second)
        down_near_side = swap(down_near, "dp", y)
        down = (
            (down_weight[None], down_side, down_far, down_far_side, down_near, down_near_side),
            ((0,), (1,), (4,), (5,), (2, 6), (3, 7)),
        )
        up_far = after(up_far, mix_second)
        up_near = swap(joined(up_weight[None], up_far), "dp", z)
        up_far_side = swap(up_far, "dp", y)
    first_half = merge_half(tokens, norm_params, branch_bias, mixes_first, merges)
    down_full, grad_hidden = down_back(after(cotangent, first_half), down)
    if small:
        up_near_side = swap(up_near, "dp", y)
        up = (
            (up_weight[None], up_side, up_far, up_far_side, up_near, up_near_side),
            ((0,), (1,), (4,), (5,), (2, 6), (3, 7)),
        )
        encoder_far = swap(after(encoder_low, up_near), "dp", far)
        encoder_pair = jnp.stack([encoder_low, encoder_far])
    normed, resid = merge_half(
        tokens, norm_params, branch_bias, mixes_second, merges, after(first_half, grad_hidden)
    )

    def branch(act, *plus):
        part = lax.dot_general(
            act, down_full[0], (((1,), (1,)), ((), ())), preferred_element_type=jnp.float32
        )
        for one in plus:
            part = part + one.astype(jnp.float32)
        return part.astype(jnp.bfloat16)

    bias = up_bias[None]
    act_both, up_both, up_full = feed_first(BOTH, normed, grad_hidden, up, bias)
    up_both = swap(up_both, "tensor", CORE)
    out_both = branch(act_both)
    if small:
        encoder_near = swap(after(encoder_pair, normed), "dp", z)
        up_both = after(up_both, encoder_near)
    act_side, up_send = feed(
        (SIDE,), normed, grad_hidden, up_full, bias, after(up_both, out_both)
    )
    up_from = swap(up_send, "tensor", SIDE)
    out_both = swap(out_both, "tensor", CORE)
    if small:
        encoder_quad = joined(encoder_pair, encoder_near)
        encoder_side = swap(after(encoder_quad, up_send), "dp", y)
        encoder = ((encoder_quad, encoder_side), ((0, 4, 2, 6), (1, 5, 3, 7)))
    act_core, up_core, act_own, up_own = feed(
        (CORE, OWN), after(normed, up_send), grad_hidden, up_full, bias
    )
    up_core = swap(up_core, "tensor", CORE)
    out_core = branch(act_core)
    up_from, up_core = after((up_from, up_core), out_core)
    grad_resid, keep, send = middle(up_own, up_core, up_from, cotangent, resid, norm_params, merges)
    from_side = swap(send, "tensor", SIDE)
    out_core = swap(out_core, "tensor", CORE)
    out_send = branch(after(act_side, send), out_both)
    out_from = swap(out_send, "tensor", SIDE)
    out_own = branch(after(act_own, send))
    from_side = after(from_side, out_own, out_send)
    from_core = swap(jnp.stack([keep[1], from_side[1]]), "tensor", CORE)
    if small:
        from_core = after(from_core, encoder_side)
    grad_projected, grad_prefix = attend_back(
        projected,
        prefix,
        (mix_first, mix_second),
        (sums_first, sums_second),
        [keep[0], from_core[0], from_side[0], from_core[1]],
    )
    (back_both,) = project_back((BOTH,), grad_projected, attend_full)
    back_both = swap(back_both, "tensor", CORE)
    (back_send,) = project_back((SIDE,), grad_projected, attend_full, back_both)
    back_from = swap(back_send, "tensor", SIDE)
    back_core, back_own = project_back(
        (CORE, OWN), after(grad_projected, back_send), attend_full
    )
    back_core = swap(back_core, "tensor", CORE)
    output = (
        resid
        + (
            out_own.astype(jnp.float32)
            + out_core.astype(jnp.float32)
            + out_from.astype(jnp.float32)
        )
        + branch_bias[1]
    )
    input_grad = last(back_own, back_core, back_from, tokens, grad_resid, norm_params)

    prefix_total = sum_over(grad_prefix, "dp")
    joint = pl.pallas_call(
        tail_kernel, out_shape=shaped((PAD, hidden_size), jnp.float32), name="tail"
    )(prefix_total, hidden, decoder_full)
    joint = sum_over(joint, "tensor")
    encoder_full = assemble(encoder, (1, width, hidden_size))
    hidden_own = lax.dynamic_slice_in_dim(hidden, dp_index * dec_rows, dec_rows, 1)
    params = [
        (prefix_table, first_table, second_table),
        (encoder_weight, first_encoder, second_encoder),
        (encoder_bias[None], first_encoder_bias[None], second_encoder_bias[None]),
        (decoder_weight, first_decoder, second_decoder),
        (decoder_bias, first_decoder_bias, second_decoder_bias),
    ]
    params = [array for group in params for array in group]
    grad_norm, *new = pl.pallas_call(
        update_kernel,
        out_shape=[shaped((1, 1), jnp.float32)] + [shaped(p.shape, p.dtype) for p in params],
        name="update",
    )(
        joint,
        hidden,
        hidden_own,
        prefix_total,
        selected,
        selected_own,
        onehot,
        encoder_full[0],
        *params,
    )
    for i in range(6, 9):
        new[i] = new[i][0]
    return (output.astype(jnp.bfloat16), input_grad, grad_norm[0, 0], *new)


def solution(mesh):
    in_specs = (
        P("dp", None),
        P("dp", None),
        P(),
        P("dp", None, "tensor"),
        P(None, "tensor"),
        P("dp", "tensor"),
        P(),
        P("dp", "tensor"),
        P("tensor"),
        P("dp", "tensor"),
        P(),
        P(),
        P("dp", None),
        P(),
        P("dp", None, "tensor"),
        P(None, "tensor"),
        P(),
        P(),
        P("dp", None),
        P("dp", None),
        P(),
        P(),
        P("dp", None, "tensor"),
        P("dp", None, "tensor"),
        P(None, "tensor"),
        P(None, "tensor"),
    )
    out_specs = (
        P(("dp", "tensor"), None),
        P(("dp", "tensor"), None),
        P(),
        P(),
        P(),
        P(),
        P("dp", None),
        P("dp", None),
        P("dp", None),
        P(),
        P(),
        P(),
        P("dp", None, "tensor"),
        P("dp", None, "tensor"),
        P("dp", None, "tensor"),
        P(None, "tensor"),
        P(None, "tensor"),
        P(None, "tensor"),
    )
    return jax.shard_map(
        on_device, mesh=mesh, in_specs=in_specs, out_specs=out_specs, check_vma=False
    )
```

profile of v0, /device:TPU:0, one launch (start us, length us, event | category | flops | bytes accessed | tf_op | source)
XLA Modules:
  0.0 251.2 jit_solution(15516110794217786041)
XLA Ops:
  2.7 4.1 %collective-permute-start = (bf16[512,256]{1,0:T(8,128)(2,1)S(1)}, bf16[512,256]{1,0:T(8,128)(2,1)S(1)}, u32[]{:S(2)}, u32[]{:S(2)}) collective-permute-start(bf16[512,256]{1,0:T(8,128)(2,1)S(1)} %get-tuple-element.173), channel_id=1, source_target_pairs={{0,16},{4,20},{8,24},{12,28},{16,0},{20,4},{24,8},{28,12},{1,17},{... | collective-permute-start | bytes 786440 | tf_op jit(solution)/shard_map/ppermute | solution.py:76
  10.1 8.6 %collective-permute-done = bf16[512,256]{1,0:T(8,128)(2,1)S(1)} collective-permute-done((bf16[512,256]{1,0:T(8,128)(2,1)S(1)}, bf16[512,256]{1,0:T(8,128)(2,1)S(1)}, u32[]{:S(2)}, u32[]{:S(2)}) %collective-permute-start) | collective-permute-done | bytes 262176 | tf_op jit(solution)/shard_map/ppermute | solution.py:76
  29.2 5.2 %collective-permute-done.4 = bf16[2,160,256]{2,1,0:T(8,128)(2,1)S(1)} collective-permute-done((bf16[2,160,256]{2,1,0:T(8,128)(2,1)S(1)}, bf16[2,160,256]{2,1,0:T(8,128)(2,1)S(1)}, u32[]{:S(2)}, u32[]{:S(2)}) %collective-permute-start.4) | collective-permute-done | bytes 163872 | tf_op jit(solution)/shard_map/ppermute | solution.py:76
  42.5 11.3 %collective-permute-done.5.refs_3_ = bf16[2,512,256]{2,1,0:T(8,128)(2,1)} collective-permute-done((bf16[2,512,256]{2,1,0:T(8,128)(2,1)S(1)}, bf16[2,512,256]{2,1,0:T(8,128)(2,1)}, u32[]{:S(2)}, u32[]{:S(2)}) %collective-permute-start.5) | collective-permute-done | bytes 524320 | tf_op jit(solution)/shard_map/ppermute | solution.py:76
  53.8 5.9 %project.1 = (bf16[3,1024,256]{2,1,0:T(8,128)(2,1)}, bf16[3,1024,256]{2,1,0:T(8,128)(2,1)}, bf16[2,512,256]{2,1,0:T(8,128)(2,1)}) custom-call(bf16[1024,1024]{1,0:T(8,128)(2,1)} %tokens.7, f32[4,1024]{1,0:T(4,128)} %norms.9, f32[3,256]{1,0:T(4,128)} %bias.1, bf16[2,512,256]{2,1,0:T(8,128)(2,1)} %copy-done.13, bf16[2,512,256]{2,1,0:T(8,128)(2,1)} %copy-done.37, ...), custom_call_target="tpu_custom_call" | custom-call | flops 1610612736 | bytes 7864320 | tf_op jit(solution)/shard_map/project/pallas_call | solution.py:177
  66.0 7.1 %attend_first.1 = (bf16[512,256]{1,0:T(8,128)(2,1)}, f32[512,128]{1,0:T(8,128)}, f32[16,512]{1,0:T(8,128)}, bf16[2,16,256]{2,1,0:T(8,128)(2,1)}) custom-call(bf16[3,1024,256]{2,1,0:T(8,128)(2,1)} %get-tuple-element.94.proj, f32[16,512]{1,0:T(8,128)} %get-tuple-element.97.encoded, f32[1,512]{1,0:T(1,128)} %bitcast.97, ...), custom_call_target="tpu_custom_call" | custom-call | flops 894784832 | bytes 2146304 | tf_op jit(solution)/shard_map/attend_first/pallas_call | solution.py:274
  73.0 9.0 %attend_second.1 = (bf16[512,256]{1,0:T(8,128)(2,1)}, f32[512,128]{1,0:T(8,128)}) custom-call(bf16[3,1024,256]{2,1,0:T(8,128)(2,1)} %get-tuple-element.94.proj, bf16[2,16,256]{2,1,0:T(8,128)(2,1)} %get-tuple-element.99.prefix), custom_call_target="tpu_custom_call" | custom-call | flops 1789569664 | bytes 2097152 | tf_op jit(solution)/shard_map/attend_second/pallas_call | solution.py:286
  83.2 7.3 %collective-permute-done.8.refs_2_ = bf16[512,256]{1,0:T(8,128)(2,1)} collective-permute-done((bf16[512,256]{1,0:T(8,128)(2,1)}, bf16[512,256]{1,0:T(8,128)(2,1)}, u32[]{:S(2)}, u32[]{:S(2)}) %collective-permute-start.8) | collective-permute-done | bytes 262176 | tf_op jit(solution)/shard_map/ppermute | solution.py:76
  92.6 4.7 %collective-permute-done.14.refs_2_ = bf16[512,256]{1,0:T(8,128)(2,1)S(1)} collective-permute-done((bf16[512,256]{1,0:T(8,128)(2,1)S(1)}, bf16[512,256]{1,0:T(8,128)(2,1)S(1)}, u32[]{:S(2)}, u32[]{:S(2)}) %collective-permute-start.14) | collective-permute-done | bytes 262176 | tf_op jit(solution)/shard_map/ppermute | solution.py:76
  102.7 5.3 %merge_first.1 = (bf16[1024,1024]{1,0:T(8,128)(2,1)}, f32[256,1024]{1,0:T(8,128)}) custom-call(bf16[1024,1024]{1,0:T(8,128)(2,1)} %tokens.7, f32[4,1024]{1,0:T(4,128)} %norms.9, f32[2,1024]{1,0:T(2,128)} %branch.3, bf16[512,256]{1,0:T(8,128)(2,1)} %get-tuple-element.102.refs_0_.mix_first, bf16[512,256]{1,0:T(8,128)(2,1)} %copy-done.22, ...), custom_call_target="tpu_custom_call" | custom-call | flops 1073741824 | bytes 6291456 | tf_op jit(solution)/shard_map/merge_first/pallas_call | solution.py:414
  108.1 3.8 %collective-permute-done.18.refs_3_ = bf16[1,128,1024]{2,1,0:T(8,128)(2,1)} collective-permute-done((bf16[1,128,1024]{2,1,0:T(8,128)(2,1)}, bf16[1,128,1024]{2,1,0:T(8,128)(2,1)}, u32[]{:S(2)}, u32[]{:S(2)}) %collective-permute-start.18) | collective-permute-done | bytes 262176 | tf_op jit(solution)/shard_map/ppermute | solution.py:76
  113.9 6.0 %down_back.1 = (bf16[1,1024,1024]{2,1,0:T(8,128)(2,1)}, bf16[1024,1024]{1,0:T(8,128)(2,1)}) custom-call(bf16[1024,1024]{1,0:T(8,128)(2,1)} %cotangent.2, bf16[1,128,1024]{2,1,0:T(8,128)(2,1)} %bitcast.83, bf16[1,128,1024]{2,1,0:T(8,128)(2,1)} %bitcast.12.refs_1_, bf16[1,128,1024]{2,1,0:T(8,128)(2,1)} %bitcast.87, ...), custom_call_target="tpu_custom_call" | custom-call | flops 2147483648 | bytes 8388608 | tf_op jit(solution)/shard_map/down_back/pallas_call | solution.py:198
  119.9 4.0 %collective-permute-start.27 = (bf16[128,512]{1,0:T(8,128)(2,1)S(1)}, bf16[128,512]{1,0:T(8,128)(2,1)S(1)}, u32[]{:S(2)}, u32[]{:S(2)}) collective-permute-start(bf16[128,512]{1,0:T(8,128)(2,1)S(1)} %convert_element_type.44), channel_id=1, source_target_pairs={{0,16},{4,20},{8,24},{12,28},{16,0},{20,4},{24,8},{28,12},{1,17},{... | collective-permute-start | bytes 393224 | tf_op jit(solution)/shard_map/ppermute | solution.py:76
  123.9 5.7 %merge_second.1 = (bf16[1024,1024]{1,0:T(8,128)(2,1)}, f32[256,1024]{1,0:T(8,128)}) custom-call(bf16[1024,1024]{1,0:T(8,128)(2,1)} %tokens.7, f32[4,1024]{1,0:T(4,128)} %norms.9, f32[2,1024]{1,0:T(2,128)} %branch.3, bf16[512,256]{1,0:T(8,128)(2,1)} %get-tuple-element.100.refs_0_.mix_second, ...), custom_call_target="tpu_custom_call", output_to_operand_aliasing={{0}: (11, {})} | custom-call | flops 1073741824 | bytes 6291456 | tf_op jit(solution)/shard_map/merge_second/pallas_call | solution.py:414
  129.6 4.1 %collective-permute-done.23.refs_3_ = bf16[1,128,1024]{2,1,0:T(8,128)(2,1)S(1)} collective-permute-done((bf16[1,128,1024]{2,1,0:T(8,128)(2,1)S(1)}, bf16[1,128,1024]{2,1,0:T(8,128)(2,1)S(1)}, u32[]{:S(2)}, u32[]{:S(2)}) %collective-permute-start.23) | collective-permute-done | bytes 262176 | tf_op jit(solution)/shard_map/ppermute | solution.py:76
  134.6 5.3 %feed_first.1 = (bf16[256,1024]{1,0:T(8,128)(2,1)}, bf16[256,1024]{1,0:T(8,128)(2,1)}, bf16[1,1024,1024]{2,1,0:T(8,128)(2,1)}) custom-call(bf16[1024,1024]{1,0:T(8,128)(2,1)} %get-tuple-element.125.normed.refs_0_.refs_2_, bf16[1024,1024]{1,0:T(8,128)(2,1)} %get-tuple-element.109.ghidden.refs_1_.refs_3_, f32[1,1024]{1,0:T(1,128)} %bitcast.93, ...), custom_call_target="tpu_custom_call" | custom-call | flops 1073741824 | bytes 5242880 | tf_op jit(solution)/shard_map/feed_first/pallas_call | solution.py:477
  144.2 4.6 %collective-permute-done.28 = bf16[2,128,512]{2,1,0:T(8,128)(2,1)S(1)} collective-permute-done((bf16[2,128,512]{2,1,0:T(8,128)(2,1)S(1)}, bf16[2,128,512]{2,1,0:T(8,128)(2,1)S(1)}, u32[]{:S(2)}, u32[]{:S(2)}) %collective-permute-start.28) | collective-permute-done | bytes 262176 | tf_op jit(solution)/shard_map/ppermute | solution.py:76
  149.6 4.6 %feed.2 = (bf16[256,1024]{1,0:T(8,128)(2,1)}, bf16[256,1024]{1,0:T(8,128)(2,1)}) custom-call(bf16[1,1024,1024]{2,1,0:T(8,128)(2,1)} %get-tuple-element.116.up, f32[1,1024]{1,0:T(1,128)} %bitcast.94, bf16[1024,1024]{1,0:T(8,128)(2,1)} %get-tuple-element.125.normed.refs_0_.refs_2_, bf16[1024,1024]{1,0:T(8,128)(2,1)} %get-tuple-element.109.ghidden.refs_1_.refs_3_, ...), custom_call_target="tpu_custom_call" | custom-call | flops 1073741824 | bytes 3145728 | tf_op jit(solution)/shard_map/feed/pallas_call | solution.py:502
  156.1 6.2 %feed.3 = (bf16[256,1024]{1,0:T(8,128)(2,1)}, bf16[256,1024]{1,0:T(8,128)(2,1)}, bf16[256,1024]{1,0:T(8,128)(2,1)}, bf16[256,1024]{1,0:T(8,128)(2,1)}) custom-call(bf16[1,1024,1024]{2,1,0:T(8,128)(2,1)} %get-tuple-element.116.up, f32[1,1024]{1,0:T(1,128)} %bitcast.95, bf16[1024,1024]{1,0:T(8,128)(2,1)} %get-tuple-element.125.normed.refs_0_.refs_2_, ...), custom_call_target="tpu_custom_call" | custom-call | flops 2147483648 | bytes 4194304 | tf_op jit(solution)/shard_map/feed/pallas_call | solution.py:502
  169.0 4.7 %middle.1 = (f32[256,1024]{1,0:T(8,128)}, bf16[2,256,256]{2,1,0:T(8,128)(2,1)}, bf16[2,256,256]{2,1,0:T(8,128)(2,1)}) custom-call(bf16[256,1024]{1,0:T(8,128)(2,1)} %get-tuple-element.127.own, bf16[256,1024]{1,0:T(8,128)(2,1)} %copy-done.18, bf16[256,1024]{1,0:T(8,128)(2,1)} %copy-done.17, bf16[1024,1024]{1,0:T(8,128)(2,1)} %cotangent.2, ...), custom_call_target="tpu_custom_call" | custom-call | flops 536870912 | bytes 4718592 | tf_op jit(solution)/shard_map/middle/pallas_call | solution.py:567
  184.7 19.2 %attend_back.1 = (bf16[3,1024,256]{2,1,0:T(8,128)(2,1)}, f32[2,16,256]{2,1,0:T(8,128)}) custom-call(bf16[3,1024,256]{2,1,0:T(8,128)(2,1)} %get-tuple-element.94.proj, bf16[2,16,256]{2,1,0:T(8,128)(2,1)} %get-tuple-element.99.prefix, bf16[512,256]{1,0:T(8,128)(2,1)} %get-tuple-element.102.refs_0_.mix_first, ...), custom_call_target="tpu_custom_call" | custom-call | flops 6442450944 | bytes 4227072 | tf_op jit(solution)/shard_map/attend_back/pallas_call | solution.py:370
  225.2 3.9 %collective-permute-start.42 = (f32[2,16,256]{2,1,0:T(8,128)S(1)}, f32[2,16,256]{2,1,0:T(8,128)S(1)}, u32[]{:S(2)}, u32[]{:S(2)}) collective-permute-start(f32[2,16,256]{2,1,0:T(8,128)S(1)} %add.54), channel_id=1, source_target_pairs={{0,16},{4,20},{8,24},{12,28},{16,0},{20,4},{24,8},{28,12},{1,17},{... | collective-permute-start | bytes 98312 | tf_op jit(solution)/shard_map/ppermute | solution.py:76
  242.5 4.3 %update.1 = (f32[1,1]{1,0:T(1,128)}, f32[10,1024]{1,0:T(8,128)}, f32[10,1024]{1,0:T(8,128)}, f32[10,1024]{1,0:T(8,128)}, f32[128,512]{1,0:T(8,128)}, /*index=5*/...) custom-call(f32[16,512]{1,0:T(8,128)} %add.57.joint, ...), custom_call_target="tpu_custom_call" | custom-call | tf_op jit(solution)/shard_map/update/pallas_call | solution.py:868
  247.7 3.5 %last.1 = bf16[256,1024]{1,0:T(8,128)(2,1)} custom-call(bf16[256,1024]{1,0:T(8,128)(2,1)} %get-tuple-element.145.own, bf16[256,1024]{1,0:T(8,128)(2,1)} %copy-done.10, bf16[256,1024]{1,0:T(8,128)(2,1)} %copy-done.11, bf16[1024,1024]{1,0:T(8,128)(2,1)} %tokens.7, f32[256,1024]{1,0:T(8,128)} %get-tuple-element.147.gresid, f32[4,1024]{1,0:T(4,128)} %norms.9), custom_call_target="tpu_custom_call" | custom-call | bytes 2621440 | tf_op jit(solution)/shard_map/last/pallas_call | solution.py:588
  (204 shorter events, 101.8 us)
Async XLA Ops:
  2.7 16.1 %collective-permute-start = (bf16[512,256]{1,0:T(8,128)(2,1)S(1)}, bf16[512,256]{1,0:T(8,128)(2,1)S(1)}, u32[]{:S(2)}, u32[]{:S(2)}) collective-permute-start(bf16[512,256]{1,0:T(8,128)(2,1)S(1)} %get-tuple-element.173), channel_id=1, source_target_pairs={{0,16},{4,20},{8,24},{12,28},{16,0},{20,4},{24,8},{28,12},{1,17},{... | collective-permute-start | bytes 786440 | tf_op jit(solution)/shard_map/ppermute | solution.py:76
  18.8 16.7 %collective-permute-start.1 = (bf16[2,512,256]{2,1,0:T(8,128)(2,1)S(1)}, bf16[2,512,256]{2,1,0:T(8,128)(2,1)S(1)}, u32[]{:S(2)}, u32[]{:S(2)}) collective-permute-start(bf16[2,512,256]{2,1,0:T(8,128)(2,1)S(1)} %pad_maximum_fusion.refs_0_), channel_id=1, source_target_pairs={{0,8},{4,12},{8,0},{12,4},{16,24},{20,28},{24,16},{28,20},{1,9},{5... | collective-permute-start | bytes 1572872 | tf_op jit(solution)/shard_map/ppermute | solution.py:76
  27.7 14.8 %collective-permute-start.2 = (bf16[2,512,256]{2,1,0:T(8,128)(2,1)S(1)}, bf16[2,512,256]{2,1,0:T(8,128)(2,1)S(1)}, u32[]{:S(2)}, u32[]{:S(2)}) collective-permute-start(bf16[2,512,256]{2,1,0:T(8,128)(2,1)S(1)} %pad_maximum_fusion.refs_0_), channel_id=1, source_target_pairs={{0,4},{4,0},{8,12},{12,8},{16,20},{20,16},{24,28},{28,24},{1,5},{5... | collective-permute-start | bytes 1572872 | tf_op jit(solution)/shard_map/ppermute | solution.py:76
  35.5 18.4 %collective-permute-start.5 = (bf16[2,512,256]{2,1,0:T(8,128)(2,1)S(1)}, bf16[2,512,256]{2,1,0:T(8,128)(2,1)}, u32[]{:S(2)}, u32[]{:S(2)}) collective-permute-start(bf16[2,512,256]{2,1,0:T(8,128)(2,1)S(1)} %collective-permute-done.1.refs_1_), channel_id=1, source_target_pairs={{0,4},{4,0},{8,12},{12,8},{16,20},{20,16},{24,28},{28,24},{1,5},{5... | collective-permute-start | bytes 1572872 | tf_op jit(solution)/shard_map/ppermute | solution.py:76
  36.8 22.9 %collective-permute-start.6 = (bf16[4,160,256]{2,1,0:T(8,128)(2,1)S(1)}, bf16[4,160,256]{2,1,0:T(8,128)(2,1)S(1)}, u32[]{:S(2)}, u32[]{:S(2)}) collective-permute-start(bf16[4,160,256]{2,1,0:T(8,128)(2,1)S(1)} %pad_maximum_fusion.4.refs_0_), channel_id=1, source_target_pairs={{0,8},{4,12},{8,0},{12,4},{16,24},{20,28},{24,16},{28,20},{1,9},{5... | collective-permute-start | bytes 983048 | tf_op jit(solution)/shard_map/ppermute | solution.py:76
  40.3 23.6 %collective-permute-start.17 = (bf16[128,1024]{1,0:T(8,128)(2,1)S(1)}, bf16[128,1024]{1,0:T(8,128)(2,1)S(1)}, u32[]{:S(2)}, u32[]{:S(2)}) collective-permute-start(bf16[128,1024]{1,0:T(8,128)(2,1)S(1)} %copy-done.27), channel_id=1, source_target_pairs={{0,16},{4,20},{8,24},{12,28},{16,0},{20,4},{24,8},{28,12},{1,17},{... | collective-permute-start | bytes 786440 | tf_op jit(solution)/shard_map/ppermute | solution.py:76
  42.0 40.7 %collective-permute-start.16 = (bf16[128,1024]{1,0:T(8,128)(2,1)S(1)}, bf16[128,1024]{1,0:T(8,128)(2,1)}, u32[]{:S(2)}, u32[]{:S(2)}) collective-permute-start(bf16[128,1024]{1,0:T(8,128)(2,1)S(1)} %copy-done.27), channel_id=1, source_target_pairs={{0,4},{4,0},{8,12},{12,8},{16,20},{20,16},{24,28},{28,24},{1,5},{5... | collective-permute-start | bytes 786440 | tf_op jit(solution)/shard_map/ppermute | solution.py:76
  62.4 28.6 %collective-permute-start.11 = (bf16[1024,256]{1,0:T(8,128)(2,1)}, bf16[1024,256]{1,0:T(8,128)(2,1)S(1)}, u32[]{:S(2)}, u32[]{:S(2)}) collective-permute-start(bf16[1024,256]{1,0:T(8,128)(2,1)} %get-tuple-element.101.refs_4_.refs_0_), channel_id=1, source_target_pairs={{0,2},{1,3},{2,0},{3,1},{4,6},{5,7},{6,4},{7,5},{8,10},{9,11},{10,... | collective-permute-start | bytes 1572872 | tf_op jit(solution)/shard_map/ppermute | solution.py:76
  64.6 26.4 %collective-permute-start.19 = (bf16[2,128,1024]{2,1,0:T(8,128)(2,1)S(1)}, bf16[2,128,1024]{2,1,0:T(8,128)(2,1)}, u32[]{:S(2)}, u32[]{:S(2)}) collective-permute-start(bf16[2,128,1024]{2,1,0:T(8,128)(2,1)S(1)} %pad_maximum_fusion.1), channel_id=1, source_target_pairs={{0,8},{4,12},{8,0},{12,4},{16,24},{20,28},{24,16},{28,20},{1,9},{5... | collective-permute-start | bytes 1572872 | tf_op jit(solution)/shard_map/ppermute | solution.py:76
  64.6 18.0 %collective-permute-start.22 = (bf16[128,1024]{1,0:T(8,128)(2,1)S(1)}, bf16[128,1024]{1,0:T(8,128)(2,1)S(1)}, u32[]{:S(2)}, u32[]{:S(2)}) collective-permute-start(bf16[128,1024]{1,0:T(8,128)(2,1)S(1)} %copy-done.8), channel_id=1, source_target_pairs={{0,16},{4,20},{8,24},{12,28},{16,0},{20,4},{24,8},{28,12},{1,17},{... | collective-permute-start | bytes 786440 | tf_op jit(solution)/shard_map/ppermute | solution.py:76
  82.6 14.7 %collective-permute-start.10 = (bf16[1024,256]{1,0:T(8,128)(2,1)S(1)}, bf16[1024,256]{1,0:T(8,128)(2,1)S(1)}, u32[]{:S(2)}, u32[]{:S(2)}) collective-permute-start(bf16[1024,256]{1,0:T(8,128)(2,1)S(1)} %copy-done), channel_id=1, source_target_pairs={{0,1},{1,0},{2,3},{3,2},{4,5},{5,4},{6,7},{7,6},{8,9},{9,8},{10,11... | collective-permute-start | bytes 1572872 | tf_op jit(solution)/shard_map/ppermute | solution.py:76
  91.1 22.3 %collective-permute-start.20 = (bf16[2,128,1024]{2,1,0:T(8,128)(2,1)}, bf16[2,128,1024]{2,1,0:T(8,128)(2,1)}, u32[]{:S(2)}, u32[]{:S(2)}) collective-permute-start(bf16[2,128,1024]{2,1,0:T(8,128)(2,1)} %collective-permute-done.19.refs_4_), channel_id=1, source_target_pairs={{0,4},{4,0},{8,12},{12,8},{16,20},{20,16},{24,28},{28,24},{1,5},{5... | collective-permute-start | bytes 1572872 | tf_op jit(solution)/shard_map/ppermute | solution.py:76
  97.3 14.5 %collective-permute-start.18 = (bf16[1,128,1024]{2,1,0:T(8,128)(2,1)}, bf16[1,128,1024]{2,1,0:T(8,128)(2,1)}, u32[]{:S(2)}, u32[]{:S(2)}) collective-permute-start(bf16[1,128,1024]{2,1,0:T(8,128)(2,1)} %bitcast.86), channel_id=1, source_target_pairs={{0,4},{4,0},{8,12},{12,8},{16,20},{20,16},{24,28},{28,24},{1,5},{5... | collective-permute-start | bytes 786440 | tf_op jit(solution)/shard_map/ppermute | solution.py:76
  99.7 34.0 %collective-permute-start.25 = (bf16[2,128,1024]{2,1,0:T(8,128)(2,1)S(1)}, bf16[2,128,1024]{2,1,0:T(8,128)(2,1)S(1)}, u32[]{:S(2)}, u32[]{:S(2)}) collective-permute-start(bf16[2,128,1024]{2,1,0:T(8,128)(2,1)S(1)} %collective-permute-done.24.refs_4_), channel_id=1, source_target_pairs={{0,4},{4,0},{8,12},{12,8},{16,20},{20,16},{24,28},{28,24},{1,5},{5... | collective-permute-start | bytes 1572872 | tf_op jit(solution)/shard_map/ppermute | solution.py:76
  101.2 18.6 %collective-permute-start.7 = (bf16[512,256]{1,0:T(8,128)(2,1)}, bf16[512,256]{1,0:T(8,128)(2,1)S(1)}, u32[]{:S(2)}, u32[]{:S(2)}) collective-permute-start(bf16[512,256]{1,0:T(8,128)(2,1)} %get-tuple-element.100.refs_0_.mix_second), channel_id=1, source_target_pairs={{0,1},{1,0},{2,3},{3,2},{4,5},{5,4},{6,7},{7,6},{8,9},{9,8},{10,11... | collective-permute-start | bytes 786440 | tf_op jit(solution)/shard_map/ppermute | solution.py:76
  101.9 21.9 %collective-permute-start.9 = (bf16[512,256]{1,0:T(8,128)(2,1)}, bf16[512,256]{1,0:T(8,128)(2,1)}, u32[]{:S(2)}, u32[]{:S(2)}) collective-permute-start(bf16[512,256]{1,0:T(8,128)(2,1)} %collective-permute-done.8.refs_2_), channel_id=1, source_target_pairs={{0,1},{1,0},{2,3},{3,2},{4,5},{5,4},{6,7},{7,6},{8,9},{9,8},{10,11... | collective-permute-start | bytes 786440 | tf_op jit(solution)/shard_map/ppermute | solution.py:76
  111.9 17.7 %collective-permute-start.21 = (bf16[128,1024]{1,0:T(8,128)(2,1)S(1)}, bf16[128,1024]{1,0:T(8,128)(2,1)S(1)}, u32[]{:S(2)}, u32[]{:S(2)}) collective-permute-start(bf16[128,1024]{1,0:T(8,128)(2,1)S(1)} %copy-done.8), channel_id=1, source_target_pairs={{0,4},{4,0},{8,12},{12,8},{16,20},{20,16},{24,28},{28,24},{1,5},{5... | collective-permute-start | bytes 786440 | tf_op jit(solution)/shard_map/ppermute | solution.py:76
  113.4 20.3 %collective-permute-start.23 = (bf16[1,128,1024]{2,1,0:T(8,128)(2,1)S(1)}, bf16[1,128,1024]{2,1,0:T(8,128)(2,1)S(1)}, u32[]{:S(2)}, u32[]{:S(2)}) collective-permute-start(bf16[1,128,1024]{2,1,0:T(8,128)(2,1)S(1)} %bitcast.76), channel_id=1, source_target_pairs={{0,4},{4,0},{8,12},{12,8},{16,20},{20,16},{24,28},{28,24},{1,5},{5... | collective-permute-start | bytes 786440 | tf_op jit(solution)/shard_map/ppermute | solution.py:76
  119.9 20.1 %collective-permute-start.27 = (bf16[128,512]{1,0:T(8,128)(2,1)S(1)}, bf16[128,512]{1,0:T(8,128)(2,1)S(1)}, u32[]{:S(2)}, u32[]{:S(2)}) collective-permute-start(bf16[128,512]{1,0:T(8,128)(2,1)S(1)} %convert_element_type.44), channel_id=1, source_target_pairs={{0,16},{4,20},{8,24},{12,28},{16,0},{20,4},{24,8},{28,12},{1,17},{... | collective-permute-start | bytes 393224 | tf_op jit(solution)/shard_map/ppermute | solution.py:76
  162.9 19.6 %collective-permute-start.36 = (bf16[4,128,512]{2,1,0:T(8,128)(2,1)S(1)}, bf16[4,128,512]{2,1,0:T(8,128)(2,1)S(1)}, u32[]{:S(2)}, u32[]{:S(2)}) collective-permute-start(bf16[4,128,512]{2,1,0:T(8,128)(2,1)S(1)} %pad_maximum_fusion.3.refs_0_), channel_id=1, source_target_pairs={{0,4},{4,0},{8,12},{12,8},{16,20},{20,16},{24,28},{28,24},{1,5},{5... | collective-permute-start | bytes 1572872 | tf_op jit(solution)/shard_map/ppermute | solution.py:76
  206.9 32.0 %collective-permute-start.31 = (bf16[256,1024]{1,0:T(8,128)(2,1)}, bf16[256,1024]{1,0:T(8,128)(2,1)S(1)}, u32[]{:S(2)}, u32[]{:S(2)}) collective-permute-start(bf16[256,1024]{1,0:T(8,128)(2,1)} %fusion.14), channel_id=1, source_target_pairs={{0,1},{1,0},{2,3},{3,2},{4,5},{5,4},{6,7},{7,6},{8,9},{9,8},{10,11... | collective-permute-start | bytes 1572872 | tf_op jit(solution)/shard_map/ppermute | solution.py:76
  207.3 31.6 %collective-permute-start.33 = (bf16[256,1024]{1,0:T(8,128)(2,1)}, bf16[256,1024]{1,0:T(8,128)(2,1)}, u32[]{:S(2)}, u32[]{:S(2)}) collective-permute-start(bf16[256,1024]{1,0:T(8,128)(2,1)} %fusion.20), channel_id=1, source_target_pairs={{0,2},{1,3},{2,0},{3,1},{4,6},{5,7},{6,4},{7,5},{8,10},{9,11},{10,... | collective-permute-start | bytes 1572872 | tf_op jit(solution)/shard_map/ppermute | solution.py:76
  216.1 30.6 %collective-permute-start.38 = (bf16[256,1024]{1,0:T(8,128)(2,1)}, bf16[256,1024]{1,0:T(8,128)(2,1)S(1)}, u32[]{:S(2)}, u32[]{:S(2)}) collective-permute-start(bf16[256,1024]{1,0:T(8,128)(2,1)} %get-tuple-element.146), channel_id=1, source_target_pairs={{0,1},{1,0},{2,3},{3,2},{4,5},{5,4},{6,7},{7,6},{8,9},{9,8},{10,11... | collective-permute-start | bytes 1572872 | tf_op jit(solution)/shard_map/ppermute | solution.py:76
  216.3 30.5 %collective-permute-start.39 = (bf16[256,1024]{1,0:T(8,128)(2,1)}, bf16[256,1024]{1,0:T(8,128)(2,1)S(1)}, u32[]{:S(2)}, u32[]{:S(2)}) collective-permute-start(bf16[256,1024]{1,0:T(8,128)(2,1)} %project_back.4), channel_id=1, source_target_pairs={{0,2},{1,3},{2,0},{3,1},{4,6},{5,7},{6,4},{7,5},{8,10},{9,11},{10,... | collective-permute-start | bytes 1572872 | tf_op jit(solution)/shard_map/ppermute | solution.py:76
  (63 other events, 614.4 us)
where the time goes:
time: 252 us; the launch traced here: 251 us
  Pallas kernels  102 us (40%)
  waiting for transfers between devices  65.6 us (26%)
  starting transfers between devices  52 us (21%)
  local copies, waits for them, and re-layouts  11.6 us (5%)
  matrix products  10.9 us (4%)
  other arithmetic  7.35 us (3%)
    ppermute x45, waiting for transfers between devices, swap(): return lax.ppermute(values, axis, [(i, i ^ bits) for i in range(size)])  65.6 us
    ppermute x45, starting transfers between devices, swap(): return lax.ppermute(values, axis, [(i, i ^ bits) for i in range(size)])  52 us
    pallas_call x1, Pallas kernels, attend_back(): pl.pallas_call(attend_back_kernel, out_shape=outs, scratch_shapes=[pltpu....  19.2 us
    pallas_call x2, Pallas kernels, merge_half(): pl.pallas_call(functools.partial(merge_kernel, first), grid=(steps,), in_...  11.1 us
    pallas_call x2, Pallas kernels, feed(): pl.pallas_call(functools.partial(feed_kernel, len(bits)), grid=(1,), in_s...  10.8 us
    dot_general x4, matrix products, branch(): lax.dot_general(act, down_full[0], (((1,), (1,)), ((), ())), preferred_el...  9.82 us
    pallas_call x3, Pallas kernels, project_back(): pl.pallas_call(functools.partial(back_kernel, len(bits)), grid=(1,), in_s...  9.31 us
    pallas_call x1, Pallas kernels, attend_second(): pl.pallas_call(functools.partial(attend_kernel, rows // 2), out_shape=out...  9 us
  transfers between devices with their start and end apart: 45, of which 19 were waited for; matrix products, arithmetic and copies ran while one was open for 8% of the time, Pallas kernels for 29%

commit v1 on v0

--- a/solution.py
+++ b/solution.py
@@ -40,9 +40,17 @@
     return jax.ShapeDtypeStruct(shape, dtype)
 
 
+def limited():
+    return pltpu.CompilerParams(vmem_limit_bytes=24 * 2**20)
+
+
 def cost(flops, *arrays):
     size = sum(a.size * a.dtype.itemsize for a in arrays)
     return pl.CostEstimate(flops=flops, transcendentals=0, bytes_accessed=size)
+
+
+def brief():
+    return pl.CostEstimate(flops=0, transcendentals=0, bytes_accessed=0)
 
 
 def norm_parts(rows):
@@ -125,8 +133,9 @@
     return pl.pallas_call(
         functools.partial(assemble_kernel, bits),
         out_shape=out,
+        compiler_params=limited(),
         name="assemble",
-        cost_estimate=cost(0, *pieces, out),
+        cost_estimate=brief(),
     )(*pieces)
 
 
@@ -148,8 +157,9 @@
     return pl.pallas_call(
         functools.partial(merge_weight_kernel, bits),
         out_shape=outs,
+        compiler_params=limited(),
         name="gather_merge",
-        cost_estimate=cost(0, *pieces, *outs),
+        cost_estimate=brief(),
     )(*pieces)
 
 
@@ -177,8 +187,9 @@
     return pl.pallas_call(
         functools.partial(project_kernel, bits),
         out_shape=outs,
+        compiler_params=limited(),
         name="project",
-        cost_estimate=cost(6 * rows * width * local, tokens, *pieces, *outs),
+        cost_estimate=brief(),
     )(tokens, norms, bias, *pieces)
 
 
@@ -198,8 +209,9 @@
     return pl.pallas_call(
         functools.partial(down_kernel, bits),
         out_shape=outs,
+        compiler_params=limited(),
         name="down_back",
-        cost_estimate=cost(2 * rows * width * units, cotangent, *pieces, *outs),
+        cost_estimate=brief(),
     )(cotangent, *pieces)
 
 
@@ -275,8 +287,9 @@
         attend_first_kernel,
         out_shape=outs,
         scratch_shapes=[pltpu.VMEM((rows // 2, width), jnp.float32)],
+        compiler_params=limited(),
         name="attend_first",
-        cost_estimate=cost(5 * width // HD * rows * rows * width // 6, proj, *outs),
+        cost_estimate=brief(),
     )(proj, encoded, encoder_bias, decoder, decoder_bias)
 
 
@@ -287,28 +300,24 @@
         functools.partial(attend_kernel, rows // 2),
         out_shape=outs,
         scratch_shapes=[pltpu.VMEM((rows // 2, width), jnp.float32)],
+        compiler_params=limited(),
         name="attend_second",
-        cost_estimate=cost(5 * width // HD * rows * rows * width // 3, proj, *outs),
+        cost_estimate=brief(),
     )(proj, prefix)
 
 
-def attend_back_kernel(
-    proj, prefix, mix_first, mix_second, sums_first, sums_second, own, core, side, both, gproj, gprefix, *scratch
+def prefix_back_kernel(
+    query, prefix, mix_first, mix_second, sums_first, sums_second, keep, side, core_keep, core_side, *refs
 ):
-    gmix, gquery, gkey, gvalue, log_sums, inner, keys_col, pre_col = scratch
+    gprefix, gmix, log_sums, inner, gquery = refs
     rows, width = gmix.shape
     half = rows // 2
-    quarter = own.shape[0]
+    quarter = keep.shape[1]
+    heads = width // HD
     me = lax.axis_index("tensor")
-    for piece, bits in ((own, OWN), (core, CORE), (side, SIDE), (both, BOTH)):
+    for piece, bits in ((keep.at[0], OWN), (core_keep.at[1], CORE), (side.at[0], SIDE), (core_side.at[1], BOTH)):
         place = lax.bitwise_xor(me, bits) * quarter
         gmix[pl.ds(pl.multiple_of(place, quarter), quarter), :] = piece[...]
-    lane = lax.broadcasted_iota(jnp.int32, (1, width), 1) // HD
-    pre_row = lax.broadcasted_iota(jnp.int32, (PAD, TILE), 0)
-    seen = lax.broadcasted_iota(jnp.int32, (TILE, TILE), 0) <= lax.broadcasted_iota(
-        jnp.int32, (TILE, TILE), 1
-    )
-    scale = jnp.asarray(HD**-0.5, jnp.bfloat16)
     head_of = lax.broadcasted_iota(jnp.int32, (8, width), 0) == lax.broadcasted_iota(
         jnp.int32, (8, width), 1
     ) // HD
@@ -317,43 +326,91 @@
         log_sums[:, part] = sums[...].T[:8]
         product = gmix[part, :].astype(jnp.float32) * mix[...].astype(jnp.float32)
         inner[:, part] = dot(head_of.astype(jnp.float32), product, NT, lax.Precision.HIGHEST)
+    lane = lax.broadcasted_iota(jnp.int32, (PAD, width), 1) // HD
+    zero = jnp.zeros((PAD, width), jnp.bfloat16)
+    keys, values = (
+        jnp.concatenate([jnp.where(lane == head, prefix[i], zero) for head in range(heads)])
+        for i in range(2)
+    )
+    scale = jnp.asarray(HD**-0.5, jnp.bfloat16)
+
+    def spread(of_heads):
+        return jnp.concatenate(
+            [jnp.broadcast_to(of_heads[head : head + 1, :], (PAD, rows)) for head in range(heads)]
+        )
+
+    scaled = query[0] * scale
+    grad = gmix[...]
+    position = lax.broadcasted_iota(jnp.int32, (heads * PAD, rows), 0) % PAD
+    scores = jnp.where(position < PRE, dot(keys, scaled, NT), MASKED)
+    prob = jnp.exp(scores - spread(log_sums))
+    dscore = (prob * (dot(values, grad, NT) - spread(inner))).astype(jnp.bfloat16)
+    dkeys = dot(dscore, scaled, NN)
+    dvalues = dot(prob.astype(jnp.bfloat16), grad, NN)
+    for i, found in enumerate((dkeys, dvalues)):
+        gprefix[i] = sum(
+            jnp.where(lane == head, found[head * PAD : (head + 1) * PAD], 0.0)
+            for head in range(heads)
+        )
+    gquery[...] = dot(keys * scale, dscore, TN)
+
+
+def prefix_back(proj, prefix, mixes, sums, pieces):
+    _, rows, width = proj.shape
+    outs = (
+        shaped(prefix.shape, jnp.float32),
+        shaped((rows, width), jnp.bfloat16),
+        shaped((8, rows), jnp.float32),
+        shaped((8, rows), jnp.float32),
+        shaped((width, rows), jnp.float32),
+    )
+    return pl.pallas_call(
+        prefix_back_kernel,
+        grid=(1,),
+        in_specs=[pl.BlockSpec((1, rows, width), lambda i: (0, 0, 0))]
+        + [whole_spec(a) for a in (prefix, *mixes, *sums, *pieces)],
+        out_specs=[whole_spec(o) for o in outs],
+        out_shape=outs,
+        compiler_params=limited(),
+        name="prefix_back",
+        cost_estimate=brief(),
+    )(proj, prefix, *mixes, *sums, *pieces)
+
+
+def attend_back_kernel(pair, proj, gmix, log_sums, inner, gquery_prefix, gproj, gquery, gkey, gvalue, keys_col):
+    rows, width = gmix.shape
+    lane = lax.broadcasted_iota(jnp.int32, (1, width), 1) // HD
+    seen = lax.broadcasted_iota(jnp.int32, (TILE, TILE), 0) <= lax.broadcasted_iota(
+        jnp.int32, (TILE, TILE), 1
+    )
+    scale = jnp.asarray(HD**-0.5, jnp.bfloat16)
     keys_col[...] = (proj[1] * scale).T
-    pre_col[...] = (prefix[0] * scale).T
     gkey[...] = jnp.zeros_like(gkey)
     gvalue[...] = jnp.zeros_like(gvalue)
-    gprefix[...] = jnp.zeros_like(gprefix)
 
     def one_head(head, carry):
         mine = lane == head
         cols = pl.ds(pl.multiple_of(head * HD, HD), HD)
+        row = pl.ds(pair * (width // HD) + head, 1)
         for start in range(0, rows, TILE):
             here = slice(start, start + TILE)
             query = proj[0, here, :] * scale
             grad = gmix[here, :]
             one = jnp.where(mine, query, jnp.zeros_like(query))
             one_grad = jnp.where(mine, grad, jnp.zeros_like(grad))
-            log_sum = log_sums[pl.ds(head, 1), here]
-            shared = inner[pl.ds(head, 1), here]
-
-            def block(keys, values, shown):
-                scores = dot(keys, one, NT)
-                if shown is not None:
-                    scores = jnp.where(shown, scores, MASKED)
-                prob = jnp.exp(scores - log_sum)
-                dscore = (prob * (dot(values, one_grad, NT) - shared)).astype(jnp.bfloat16)
-                return dscore, dot(dscore, one, NN), dot(prob.astype(jnp.bfloat16), one_grad, NN)
-
-            dscore, dkey, dvalue = block(prefix[0], prefix[1], pre_row < PRE)
-            gprefix[0] += dkey
-            gprefix[1] += dvalue
-            dquery = dot(pre_col[cols, :], dscore, NN)
+            log_sum = log_sums[row, here]
+            shared = inner[row, here]
+            dquery = gquery_prefix[cols, here]
             for at in range(0, start + TILE, TILE):
                 there = slice(at, at + TILE)
-                dscore, dkey, dvalue = block(
-                    proj[1, there, :], proj[2, there, :], seen if at == start else None
-                )
-                gkey[there, :] += dkey
-                gvalue[there, :] += dvalue
+                scores = dot(proj[1, there, :], one, NT)
+                if at == start:
+                    scores = jnp.where(seen, scores, MASKED)
+                prob = jnp.exp(scores - log_sum)
+                dscore = prob * (dot(proj[2, there, :], one_grad, NT) - shared)
+                dscore = dscore.astype(jnp.bfloat16)
+                gkey[there, :] += dot(dscore, one, NN)
+                gvalue[there, :] += dot(prob.astype(jnp.bfloat16), one_grad, NN)
                 dquery = dquery + dot(keys_col[cols, there], dscore, NN)
             gquery[cols, here] = dquery
         return carry
@@ -364,31 +421,43 @@
     gproj[2] = gvalue[...].astype(jnp.bfloat16)
 
 
-def attend_back(proj, prefix, mixes, sums, pieces):
-    _, rows, width = proj.shape
-    outs = (shaped(proj.shape, jnp.bfloat16), shaped(prefix.shape, jnp.float32))
-    return pl.pallas_call(
-        attend_back_kernel,
-        out_shape=outs,
+def attend_back(pair, proj, gmix, log_sums, inner, gquery):
+    _, rows, local = proj.shape
+    width = 2 * HD
+    out = shaped((3, rows, width), jnp.bfloat16)
+    return pl.pallas_call(
+        functools.partial(attend_back_kernel, pair),
+        grid=(1,),
+        in_specs=[
+            pl.BlockSpec((3, rows, width), lambda i: (0, 0, pair)),
+            pl.BlockSpec((rows, width), lambda i: (0, pair)),
+            whole_spec(log_sums),
+            whole_spec(inner),
+            pl.BlockSpec((width, rows), lambda i: (pair, 0)),
+        ],
+        out_specs=whole_spec(out),
+        out_shape=out,
         scratch_shapes=[
-            pltpu.VMEM((rows, width), jnp.bfloat16),
             pltpu.VMEM((width, rows), jnp.float32),
             pltpu.VMEM((rows, width), jnp.float32),
             pltpu.VMEM((rows, width), jnp.float32),
-            pltpu.VMEM((8, rows), jnp.float32),
-            pltpu.VMEM((8, rows), jnp.float32),
             pltpu.VMEM((width, rows), jnp.bfloat16),
-            pltpu.VMEM((width, PAD), jnp.bfloat16),
         ],
+        compiler_params=limited(),
         name="attend_back",
-        cost_estimate=cost(12 * width // HD * rows * rows * width // 2, proj, *mixes, *sums, *outs),
-    )(proj, prefix, *mixes, *sums, *pieces)
+        cost_estimate=cost(12 * rows * rows * width, proj, gmix, gquery, out),
+    )(proj, gmix, log_sums, inner, gquery)
+
+
+def four(refs):
+    own, side, other = refs
+    return own, other.at[0], side, other.at[1]
 
 
 def merge_kernel(first, tokens, norms, branch, *refs):
-    mixes, merges, earlier, (normed, resid_own) = refs[:4], refs[4:8], refs[8:-2], refs[-2:]
+    mixes, merges, earlier, (normed, resid_own) = refs[:3], refs[3:6], refs[6:-2], refs[-2:]
     i = pl.program_id(0)
-    merged = sum(dot(m[...], w[...], NT) for m, w in zip(mixes, merges, strict=True))
+    merged = sum(dot(m[...], w[...], NT) for m, w in zip(four(mixes), four(merges), strict=True))
     resid = tokens[...].astype(jnp.float32) + merged + branch[0:1, :]
     unit, _ = norm_parts(resid)
     normed[...] = (unit * norms[2:3, :] + norms[3:4, :]).astype(jnp.bfloat16)
@@ -415,7 +484,8 @@
         functools.partial(merge_kernel, first),
         grid=(steps,),
         in_specs=[pl.BlockSpec((share, width), lambda i: (i + first, 0)), whole(norms), whole(branch)]
-        + [pl.BlockSpec((share, local), lambda i: (i, 0))] * 4
+        + [pl.BlockSpec((share, local), lambda i: (i, 0))] * 2
+        + [pl.BlockSpec((2, share, local), lambda i: (0, i, 0))]
         + [whole(w) for w in merges]
         + ([pl.BlockSpec(memory_space=pl.ANY), whole(earlier[1])] if earlier else []),
         out_specs=(
@@ -423,9 +493,10 @@
             pl.BlockSpec((share, width), lambda i: (0, 0)),
         ),
         out_shape=outs,
-        input_output_aliases={11: 0} if earlier else {},
+        input_output_aliases={9: 0} if earlier else {},
+        compiler_params=limited(),
         name="merge_second" if earlier else "merge_first",
-        cost_estimate=cost(4 * rows * width * local, *mixes, *merges, *outs),
+        cost_estimate=brief(),
     )(tokens, norms, branch, *mixes, *merges, *earlier)
 
 
@@ -450,14 +521,13 @@
     feed_rows(normed, ghidden, up[0], bias, act, part)
 
 
-def feed_kernel(count, up, bias, *refs):
-    rows, plus, outs = refs[: 2 * count], refs[2 * count : -2 * count], refs[-2 * count :]
-    for i in range(count):
-        feed_rows(rows[2 * i], rows[2 * i + 1], up[0], bias, outs[2 * i], outs[2 * i + 1], *plus)
-
-
-def block_of(differ):
-    return lambda i: (lax.bitwise_xor(lax.axis_index("tensor"), differ), 0)
+def feed_kernel(up, bias, normed, ghidden, *refs):
+    feed_rows(normed, ghidden, up[0], bias, *refs[-2:], *refs[:-2])
+
+
+def block_of(*bits):
+    last = len(bits) - 1
+    return lambda i: (lax.bitwise_xor(lax.axis_index("tensor"), bits[0] if not last else last - i), 0)
 
 
 def whole_spec(a):
@@ -485,8 +555,9 @@
         + [whole_spec(p) for p in pieces],
         out_specs=[whole_spec(o) for o in outs],
         out_shape=outs,
+        compiler_params=limited(),
         name="feed_first",
-        cost_estimate=cost(4 * share * width * units, *pieces, *outs),
+        cost_estimate=brief(),
     )(normed, ghidden, bias, *pieces)
 
 
@@ -494,49 +565,60 @@
     rows, width = normed.shape
     share = rows // lax.axis_size("tensor")
     units = up.shape[-1]
-    outs = [shaped((share, units), jnp.bfloat16), shaped((share, width), jnp.bfloat16)] * len(bits)
-    specs = []
-    for differ in bits:
-        specs.append(pl.BlockSpec((share, width), block_of(differ)))
-        specs.append(pl.BlockSpec((share, units), block_of(differ)))
-    return pl.pallas_call(
-        functools.partial(feed_kernel, len(bits)),
-        grid=(1,),
-        in_specs=[whole_spec(up), whole_spec(bias), *specs] + [whole_spec(p) for p in plus],
-        out_specs=[whole_spec(o) for o in outs],
+    steps = len(bits)
+    outs = (
+        shaped((steps * share, units), jnp.bfloat16),
+        shaped((steps * share, width), jnp.bfloat16),
+    )
+    return pl.pallas_call(
+        feed_kernel,
+        grid=(steps,),
+        in_specs=[
+            whole_spec(up),
+            whole_spec(bias),
+            pl.BlockSpec((share, width), block_of(*bits)),
+            pl.BlockSpec((share, units), block_of(*bits)),
+        ]
+        + [whole_spec(p) for p in plus],
+        out_specs=[
+            pl.BlockSpec((share, units), lambda i: (i, 0)),
+            pl.BlockSpec((share, width), lambda i: (i, 0)),
+        ],
         out_shape=outs,
+        compiler_params=limited(),
         name="feed",
-        cost_estimate=cost(4 * len(bits) * share * width * units, up, *outs),
-    )(up, bias, *[normed, ghidden] * len(bits), *plus)
-
-
-def back_kernel(count, weight, *refs):
-    rows, plus, outs = refs[:count], refs[count:-count], refs[-count:]
-    for grad, out in zip(rows, outs, strict=True):
-        total = sum(dot(grad[i], weight[i], NT) for i in range(weight.shape[0]))
-        for one in plus:
-            total = total + one[...].astype(jnp.float32)
-        out[...] = total.astype(jnp.bfloat16)
-
-
-def project_back(bits, gproj, attend, *plus):
-    _, rows, local = gproj.shape
+        cost_estimate=brief(),
+    )(up, bias, normed, ghidden, *plus)
+
+
+def back_kernel(weight, one, two, *refs):
+    total = sum(
+        dot(jnp.concatenate([one[i], two[i]], axis=1), weight[i], NT) for i in range(weight.shape[0])
+    )
+    for plus in refs[:-1]:
+        total = total + plus[...].astype(jnp.float32)
+    refs[-1][...] = total.astype(jnp.bfloat16)
+
+
+def project_back(bits, gprojs, attend, *plus):
+    _, rows, local = gprojs[0].shape
     width = attend.shape[1]
     share = rows // lax.axis_size("tensor")
-    outs = [shaped((share, width), jnp.bfloat16)] * len(bits)
-    specs = [
-        pl.BlockSpec((3, share, local), lambda i, block=block_of(differ): (0, *block(i)))
-        for differ in bits
-    ]
-    return pl.pallas_call(
-        functools.partial(back_kernel, len(bits)),
-        grid=(1,),
-        in_specs=[whole_spec(attend), *specs] + [whole_spec(p) for p in plus],
-        out_specs=[whole_spec(o) for o in outs],
-        out_shape=outs,
+    steps = len(bits)
+    block = block_of(*bits)
+    out = shaped((steps * share, width), jnp.bfloat16)
+    return pl.pallas_call(
+        back_kernel,
+        grid=(steps,),
+        in_specs=[whole_spec(attend)]
+        + [pl.BlockSpec((3, share, local), lambda i: (0, *block(i)))] * 2
+        + [whole_spec(p) for p in plus],
+        out_specs=pl.BlockSpec((share, width), lambda i: (i, 0)),
+        out_shape=out,
+        compiler_params=limited(),
         name="project_back",
-        cost_estimate=cost(6 * len(bits) * share * local * width, attend, *outs),
-    )(attend, *[gproj] * len(bits), *plus)
+        cost_estimate=brief(),
+    )(attend, *gprojs, *plus)
 
 
 def three(own, core, side):
@@ -544,7 +626,7 @@
 
 
 def middle_kernel(own, core, side, cotangent, resid, norms, *refs):
-    merges, (gresid, keep, send) = refs[:4], refs[4:]
+    merges, (gresid, keep, send) = four(refs[:3]), refs[3:]
     total = three(own, core, side)
     grad = cotangent[...].astype(jnp.float32) + norm_back(resid[...], norms[2:3, :], total)
     gresid[...] = grad
@@ -555,6 +637,10 @@
     send[1] = dot(low, merges[BOTH][...], NN).astype(jnp.bfloat16)
 
 
+def row_of(share, width, step):
+    return pl.BlockSpec((share, width), lambda i: (step, 0))
+
+
 def middle(own, core, side, cotangent, resid, norms, merges):
     share, width = resid.shape
     local = merges[0].shape[1]
@@ -567,12 +653,13 @@
     return pl.pallas_call(
         middle_kernel,
         grid=(1,),
-        in_specs=[whole_spec(own), whole_spec(core), whole_spec(side), mine]
+        in_specs=[row_of(share, width, 1), row_of(share, width, 0), whole_spec(side), mine]
         + [whole_spec(a) for a in (resid, norms, *merges)],
         out_specs=[whole_spec(o) for o in outs],
         out_shape=outs,
+        compiler_params=limited(),
         name="middle",
-        cost_estimate=cost(8 * share * width * local, resid, *merges, *outs),
+        cost_estimate=brief(),
     )(own, core, side, cotangent, resid, norms, *merges)
 
 
@@ -589,8 +676,8 @@
         last_kernel,
         grid=(1,),
         in_specs=[
-            whole_spec(own),
-            whole_spec(core),
+            row_of(share, width, 1),
+            row_of(share, width, 0),
             whole_spec(side),
             pl.BlockSpec((share, width), block_of(OWN)),
             whole_spec(gresid),
@@ -598,8 +685,9 @@
         ],
         out_specs=whole_spec(out),
         out_shape=out,
+        compiler_params=limited(),
         name="last",
-        cost_estimate=cost(0, core, side, gresid, out),
+        cost_estimate=brief(),
     )(own, core, side, tokens, gresid, norms)
 
 
@@ -720,14 +808,13 @@
         y, z, far = 1, 2, 4
         attention_far = swap(attention, "dp", far)
         merging_side = swap(merging, "dp", y)[None]
-        down_side = swap(down_weight, "dp", y)[None]
         up_side = swap(up_weight, "dp", y)[None]
-        pair = jnp.stack([attention, attention_far])
+        pair = jnp.stack([attention, after(attention_far, merging_side)])
         near = swap(pair, "dp", z)
         pair_side = swap(pair, "dp", y)
         merging_pair = joined(merging[None], merging_side)
         merging_far = swap(after(merging_pair, attention_far), "dp", far)
-        near_side = swap(after(near, merging_far), "dp", y)
+        near_side = swap(near, "dp", y)
         attention = ((pair, near, pair_side, near_side), ((0, 4), (2, 6), (1, 5), (3, 7)))
         merging_quad = joined(merging_pair, merging_far)
         merging_near = swap(merging_quad, "dp", z)
@@ -743,43 +830,51 @@
         tokens, norm_params, attention_bias, attention, hidden_size
     )
     if small:
-        down_far = after(down_far, projected)
-        down_near = swap(joined(down_weight[None], down_far), "dp", z)
-        down_far_side = swap(down_far, "dp", y)
+        down_far = after(down_far, projected, up_side)
+        down_pair = joined(down_weight[None], down_far)
+        down_near = swap(down_pair, "dp", z)
+        down_pair_side = swap(down_pair, "dp", y)
         up_far = swap(after(up_weight, down_far), "dp", far)[None]
-    merge_own, encoded = gather_merge(after(merging[0], projected), merging[1], width, hidden_size)
+    pieces, places = merging
+    pieces = after(pieces, projected)
+    if small:
+        pieces = after(pieces, down_far, up_side)
+    merge_own, encoded = gather_merge(pieces, places, width, hidden_size)
     mix_first, sums_first, hidden, prefix = attend_first(
         projected, encoded, encoder_bias[None], decoder_full, decoder_bias
     )
 
-    def from_others(values):
-        side = swap(values, "tensor", SIDE)
-        return [values, swap(values, "tensor", CORE), side, swap(side, "tensor", CORE)]
-
-    merges = from_others(merge_own)
-    mixes_first = from_others(mix_first)
+    def from_others(values, side):
+        return values, side, swap(jnp.stack([values, side]), "tensor", CORE)
+
+    merges = from_others(merge_own, after(swap(merge_own, "tensor", SIDE), mix_first))
+    mixes_first = from_others(mix_first, swap(mix_first, "tensor", SIDE))
     mix_second, sums_second = attend_second(projected, prefix)
-    mixes_second = from_others(mix_second)
+    mix_side = swap(mix_second, "tensor", SIDE)
     if small:
-        down_near = after(down_near, mix_second)
+        down_near, down_pair_side, up_far = after((down_near, down_pair_side, up_far), mix_second)
         down_near_side = swap(down_near, "dp", y)
         down = (
-            (down_weight[None], down_side, down_far, down_far_side, down_near, down_near_side),
-            ((0,), (1,), (4,), (5,), (2, 6), (3, 7)),
+            (down_pair, down_pair_side, down_near, down_near_side),
+            ((0, 4), (1, 5), (2, 6), (3, 7)),
         )
-        up_far = after(up_far, mix_second)
+        up_far = after(up_far, mixes_first[1])
         up_near = swap(joined(up_weight[None], up_far), "dp", z)
         up_far_side = swap(up_far, "dp", y)
     first_half = merge_half(tokens, norm_params, branch_bias, mixes_first, merges)
-    down_full, grad_hidden = down_back(after(cotangent, first_half), down)
+    mixes_second = from_others(mix_second, after(mix_side, first_half))
+    cotangent_late = after(cotangent, first_half)
     if small:
+        up_near = after(up_near, first_half)
+        cotangent_late = after(cotangent_late, up_near)
         up_near_side = swap(up_near, "dp", y)
         up = (
             (up_weight[None], up_side, up_far, up_far_side, up_near, up_near_side),
             ((0,), (1,), (4,), (5,), (2, 6), (3, 7)),
         )
-        encoder_far = swap(after(encoder_low, up_near), "dp", far)
-        encoder_pair = jnp.stack([encoder_low, encoder_far])
+    down_full, grad_hidden = down_back(cotangent_late, down)
+    if small:
+        encoder_far = swap(after(encoder_low, grad_hidden), "dp", far)
     normed, resid = merge_half(
         tokens, norm_params, branch_bias, mixes_second, merges, after(first_half, grad_hidden)
     )
@@ -793,52 +888,71 @@
         return part.astype(jnp.bfloat16)
 
     bias = up_bias[None]
+    if small:
+        normed = after(normed, encoder_far)
     act_both, up_both, up_full = feed_first(BOTH, normed, grad_hidden, up, bias)
     up_both = swap(up_both, "tensor", CORE)
-    out_both = branch(act_both)
     if small:
-        encoder_near = swap(after(encoder_pair, normed), "dp", z)
-        up_both = after(up_both, encoder_near)
-    act_side, up_send = feed(
-        (SIDE,), normed, grad_hidden, up_full, bias, after(up_both, out_both)
-    )
+        encoder_pair = jnp.stack([encoder_low, encoder_far])
+        encoder_near = swap(encoder_pair, "dp", z)
+    act_side, up_send = feed((SIDE,), normed, grad_hidden, up_full, bias, up_both)
     up_from = swap(up_send, "tensor", SIDE)
+    normed = after(normed, up_send)
+    if small:
+        normed = after(normed, encoder_near)
+        encoder_quad = joined(encoder_pair, encoder_near)
+        encoder_side = swap(encoder_quad, "dp", y)
+        encoder = ((encoder_quad, encoder_side), ((0, 4, 2, 6), (1, 5, 3, 7)))
+    act_rest, up_rest = feed((CORE, OWN), normed, grad_hidden, up_full, bias)
+    up_core = swap(up_rest, "tensor", CORE)
+    out_both = branch(after(act_both, act_rest))
+    out_core = branch(act_rest[:share])
+    up_from = after(up_from, out_both, out_core)
+    out_own = branch(after(act_rest, up_from)[share:])
+    up_core = after(up_core, out_own)
+    grad_resid, keep, send = middle(up_rest, up_core, up_from, cotangent, resid, norm_params, merges)
     out_both = swap(out_both, "tensor", CORE)
-    if small:
-        encoder_quad = joined(encoder_pair, encoder_near)
-        encoder_side = swap(after(encoder_quad, up_send), "dp", y)
-        encoder = ((encoder_quad, encoder_side), ((0, 4, 2, 6), (1, 5, 3, 7)))
-    act_core, up_core, act_own, up_own = feed(
-        (CORE, OWN), after(normed, up_send), grad_hidden, up_full, bias
-    )
-    up_core = swap(up_core, "tensor", CORE)
-    out_core = branch(act_core)
-    up_from, up_core = after((up_from, up_core), out_core)
-    grad_resid, keep, send = middle(up_own, up_core, up_from, cotangent, resid, norm_params, merges)
     from_side = swap(send, "tensor", SIDE)
+    core_keep = swap(keep, "tensor", CORE)
     out_core = swap(out_core, "tensor", CORE)
     out_send = branch(after(act_side, send), out_both)
     out_from = swap(out_send, "tensor", SIDE)
-    out_own = branch(after(act_own, send))
-    from_side = after(from_side, out_own, out_send)
-    from_core = swap(jnp.stack([keep[1], from_side[1]]), "tensor", CORE)
-    if small:
-        from_core = after(from_core, encoder_side)
-    grad_projected, grad_prefix = attend_back(
+    encoder_full = assemble((after(encoder[0], send), encoder[1]), (1, width, hidden_size))
+    hidden_own = lax.dynamic_slice_in_dim(after(hidden, send), dp_index * dec_rows, dec_rows, 1)
+    from_side = after(from_side, out_send, encoder_full, hidden_own)
+    core_side = swap(from_side, "tensor", CORE)
+    grad_prefix, grad_mix, log_sums, inner, grad_query = prefix_back(
         projected,
         prefix,
         (mix_first, mix_second),
         (sums_first, sums_second),
-        [keep[0], from_core[0], from_side[0], from_core[1]],
-    )
-    (back_both,) = project_back((BOTH,), grad_projected, attend_full)
-    back_both = swap(back_both, "tensor", CORE)
-    (back_send,) = project_back((SIDE,), grad_projected, attend_full, back_both)
+        (keep, from_side, core_keep, core_side),
+    )
+    grad_first = attend_back(0, projected, grad_mix, log_sums, inner, grad_query)
+    prefix_total = grad_prefix + swap(grad_prefix, "dp", 1)
+    grad_second = attend_back(
+        1, projected, after(grad_mix, prefix_total), log_sums, inner, grad_query
+    )
+    prefix_total = prefix_total + swap(prefix_total, "dp", 2)
+    gprojs = after((grad_first, grad_second), prefix_total, out_from, out_core)
+    bits = 4
+    while bits < lax.axis_size("dp"):
+        prefix_total = prefix_total + swap(prefix_total, "dp", bits)
+        bits *= 2
+    back_both = swap(project_back((BOTH,), gprojs, attend_full), "tensor", CORE)
+    back_send = project_back((SIDE,), gprojs, attend_full, after(back_both, prefix_total))
     back_from = swap(back_send, "tensor", SIDE)
-    back_core, back_own = project_back(
-        (CORE, OWN), after(grad_projected, back_send), attend_full
-    )
-    back_core = swap(back_core, "tensor", CORE)
+    joint = pl.pallas_call(
+        tail_kernel,
+        out_shape=shaped((PAD, hidden_size), jnp.float32),
+        compiler_params=limited(),
+        name="tail",
+        cost_estimate=brief(),
+    )(prefix_total, hidden, decoder_full)
+    joint = joint + swap(joint, "tensor", CORE)
+    back_rest = project_back((CORE, OWN), after(gprojs, back_send), attend_full)
+    joint = joint + swap(joint, "tensor", SIDE)
+    back_core = swap(back_rest, "tensor", CORE)
     output = (
         resid
         + (
@@ -848,15 +962,8 @@
         )
         + branch_bias[1]
     )
-    input_grad = last(back_own, back_core, back_from, tokens, grad_resid, norm_params)
-
-    prefix_total = sum_over(grad_prefix, "dp")
-    joint = pl.pallas_call(
-        tail_kernel, out_shape=shaped((PAD, hidden_size), jnp.float32), name="tail"
-    )(prefix_total, hidden, decoder_full)
-    joint = sum_over(joint, "tensor")
-    encoder_full = assemble(encoder, (1, width, hidden_size))
-    hidden_own = lax.dynamic_slice_in_dim(hidden, dp_index * dec_rows, dec_rows, 1)
+    input_grad = last(back_rest, back_core, back_from, tokens, grad_resid, norm_params)
+
     params = [
         (prefix_table, first_table, second_table),
         (encoder_weight, first_encoder, second_encoder),
@@ -868,6 +975,7 @@
     grad_norm, *new = pl.pallas_call(
         update_kernel,
         out_shape=[shaped((1, 1), jnp.float32)] + [shaped(p.shape, p.dtype) for p in params],
+        compiler_params=limited(),
         name="update",
     )(
         joint,

time: 252 us -> 213 us (0.85)
  Pallas kernels: 102 us -> 53.3 us
  waiting for transfers between devices: 65.6 us -> 87.7 us
  local copies, waits for them, and re-layouts: 11.6 us -> 4.44 us
  matrix products: 10.9 us -> 5.92 us
    pallas_call x11 -> x13, Pallas kernels: 61.6 us -> 31.8 us  [the longest x2 11.7 us: attend_back(): pl.pallas_call(functools.partial(attend_back_kernel, pair), grid=(1,), in...]
    ppermute x45 -> x42, waiting for transfers between devices: 65.6 us -> 87.7 us  [swap(): return lax.ppermute(values, axis, [(i, i ^ bits) for i in range(size)])]
    pallas_call x2, Pallas kernels: 11.1 us -> 4.48 us  [merge_half(): pl.pallas_call(functools.partial(merge_kernel, first), grid=(steps,), in_...]
    dot_general x4, matrix products: 9.82 us -> 4.75 us  [branch(): lax.dot_general(act, down_full[0], (((1,), (1,)), ((), ())), preferred_el...]
    unnamed x84 -> x116, local copies, waits for them, and re-layouts: 7.53 us -> 3.67 us
    pallas_call x1, Pallas kernels: 5.32 us -> 1.99 us  [feed_first(): pl.pallas_call(functools.partial(feed_first_kernel, places), grid=(1,), i...]
    ppermute x45 -> x42, starting transfers between devices: 52 us -> 51.8 us  [swap(): return lax.ppermute(values, axis, [(i, i ^ bits) for i in range(size)])]
  transfers between devices with their start and end apart: 45 -> 42, of which waited for: 19 -> 23; matrix products, arithmetic and copies ran while one was open for 8% -> 5% of each run, Pallas kernels for 29% -> 20%
where the time goes in v1:
time: 213 us
  waiting for transfers between devices  87.7 us (41%)
  Pallas kernels  53.3 us (25%)
  starting transfers between devices  51.8 us (24%)
  other arithmetic  7.81 us (4%)
  matrix products  5.92 us (3%)
  local copies, waits for them, and re-layouts  4.44 us (2%)
    ppermute x42, waiting for transfers between devices, swap(): return lax.ppermute(values, axis, [(i, i ^ bits) for i in range(size)])  87.7 us
    ppermute x42, starting transfers between devices, swap(): return lax.ppermute(values, axis, [(i, i ^ bits) for i in range(size)])  51.8 us
    pallas_call x2, Pallas kernels, attend_back(): pl.pallas_call(functools.partial(attend_back_kernel, pair), grid=(1,), in...  11.7 us
    pallas_call x1, Pallas kernels, attend_second(): pl.pallas_call(functools.partial(attend_kernel, rows // 2), out_shape=out...  6.89 us
    pallas_call x2, Pallas kernels, feed(): pl.pallas_call(feed_kernel, grid=(steps,), in_specs=[whole_spec(up), whol...  6.34 us
    pallas_call x1, Pallas kernels, attend_first(): pl.pallas_call(attend_first_kernel, out_shape=outs, scratch_shapes=[pltpu...  4.89 us
    dot_general x4, matrix products, branch(): lax.dot_general(act, down_full[0], (((1,), (1,)), ((), ())), preferred_el...  4.75 us
    pallas_call x2, Pallas kernels, merge_half(): pl.pallas_call(functools.partial(merge_kernel, first), grid=(steps,), in_...  4.48 us
  transfers between devices with their start and end apart: 42, of which 23 were waited for; matrix products, arithmetic and copies ran while one was open for 5% of the time, Pallas kernels for 20%

profile of v1, /device:TPU:0, one launch (start us, length us, event | category | flops | bytes accessed | tf_op | source)
XLA Modules:
  0.0 212.7 jit_solution(15229943040735967303)
XLA Ops:
  2.8 4.1 %collective-permute-start = (bf16[512,256]{1,0:T(8,128)(2,1)S(1)}, bf16[512,256]{1,0:T(8,128)(2,1)}, u32[]{:S(2)}, u32[]{:S(2)}) collective-permute-start(bf16[512,256]{1,0:T(8,128)(2,1)S(1)} %get-tuple-element.193), channel_id=1, source_target_pairs={{0,16},{4,20},{8,24},{12,28},{16,0},{20,4},{24,8},{28,12},{1,17},{... | collective-permute-start | bytes 786440 | tf_op jit(solution)/shard_map/ppermute | solution.py:84
  12.3 2.9 %collective-permute-done.1 = bf16[160,256]{1,0:T(8,128)(2,1)S(1)} collective-permute-done((bf16[160,256]{1,0:T(8,128)(2,1)S(1)}, bf16[160,256]{1,0:T(8,128)(2,1)S(1)}, u32[]{:S(2)}, u32[]{:S(2)}) %collective-permute-start.1) | collective-permute-done | bytes 81952 | tf_op jit(solution)/shard_map/ppermute | solution.py:84
  15.2 3.7 %collective-permute-done = bf16[512,256]{1,0:T(8,128)(2,1)} collective-permute-done((bf16[512,256]{1,0:T(8,128)(2,1)S(1)}, bf16[512,256]{1,0:T(8,128)(2,1)}, u32[]{:S(2)}, u32[]{:S(2)}) %collective-permute-start) | collective-permute-done | bytes 262176 | tf_op jit(solution)/shard_map/ppermute | solution.py:84
  20.7 3.6 %collective-permute-start.5 = (bf16[2,160,256]{2,1,0:T(8,128)(2,1)S(1)}, bf16[2,160,256]{2,1,0:T(8,128)(2,1)S(1)}, u32[]{:S(2)}, u32[]{:S(2)}) collective-permute-start(bf16[2,160,256]{2,1,0:T(8,128)(2,1)S(1)} %pad_maximum_fusion.10), channel_id=1, source_target_pairs={{0,16},{4,20},{8,24},{12,28},{16,0},{20,4},{24,8},{28,12},{1,17},{... | collective-permute-start | bytes 491528 | tf_op jit(solution)/shard_map/ppermute | solution.py:84
  25.7 10.9 %collective-permute-done.2.refs_1_ = bf16[2,512,256]{2,1,0:T(8,128)(2,1)S(1)} collective-permute-done((bf16[2,512,256]{2,1,0:T(8,128)(2,1)S(1)}, bf16[2,512,256]{2,1,0:T(8,128)(2,1)S(1)}, u32[]{:S(2)}, u32[]{:S(2)}) %collective-permute-start.2) | collective-permute-done | bytes 524320 | tf_op jit(solution)/shard_map/ppermute | solution.py:84
  43.7 7.8 %collective-permute-done.4.refs_3_ = bf16[2,512,256]{2,1,0:T(8,128)(2,1)S(1)} collective-permute-done((bf16[2,512,256]{2,1,0:T(8,128)(2,1)S(1)}, bf16[2,512,256]{2,1,0:T(8,128)(2,1)S(1)}, u32[]{:S(2)}, u32[]{:S(2)}) %collective-permute-start.4) | collective-permute-done | bytes 524320 | tf_op jit(solution)/shard_map/ppermute | solution.py:84
  56.7 4.9 %attend_first.1 = (bf16[512,256]{1,0:T(8,128)(2,1)S(1)}, f32[512,128]{1,0:T(8,128)S(1)}, f32[16,512]{1,0:T(8,128)S(1)}, bf16[2,16,256]{2,1,0:T(8,128)(2,1)S(1)}) custom-call(bf16[3,1024,256]{2,1,0:T(8,128)(2,1)S(1)} %get-tuple-element.106.proj.query, f32[16,512]{1,0:T(8,128)S(1)} %get-tuple-element.114.encoded, f32[1,512]{1,0:T(1,128)S(1)} %bitcast.83, ...), custom_call_target="tpu_custom_call" | custom-call | tf_op jit(solution)/shard_map/attend_first/pallas_call | solution.py:286
  61.6 4.4 %collective-permute-done.12.refs_4_.refs_1_ = bf16[1024,256]{1,0:T(8,128)(2,1)S(1)} collective-permute-done((bf16[1024,256]{1,0:T(8,128)(2,1)S(1)}, bf16[1024,256]{1,0:T(8,128)(2,1)S(1)}, u32[]{:S(2)}, u32[]{:S(2)}) %collective-permute-start.12) | collective-permute-done | bytes 524320 | tf_op jit(solution)/shard_map/ppermute | solution.py:84
  70.4 5.4 %collective-permute-start.17 = (bf16[128,1024]{1,0:T(8,128)(2,1)S(1)}, bf16[128,1024]{1,0:T(8,128)(2,1)S(1)}, u32[]{:S(2)}, u32[]{:S(2)}) collective-permute-start(bf16[128,1024]{1,0:T(8,128)(2,1)S(1)} %copy-done.20), channel_id=1, source_target_pairs={{0,16},{4,20},{8,24},{12,28},{16,0},{20,4},{24,8},{28,12},{1,17},{... | collective-permute-start | bytes 786440 | tf_op jit(solution)/shard_map/ppermute | solution.py:84
  77.2 6.9 %attend_second.1 = (bf16[512,256]{1,0:T(8,128)(2,1)S(1)}, f32[512,128]{1,0:T(8,128)S(1)}) custom-call(bf16[3,1024,256]{2,1,0:T(8,128)(2,1)S(1)} %get-tuple-element.106.proj.query, bf16[2,16,256]{2,1,0:T(8,128)(2,1)S(1)} %get-tuple-element.116.prefix), custom_call_target="tpu_custom_call" | custom-call | tf_op jit(solution)/shard_map/attend_second/pallas_call | solution.py:299
  86.4 4.6 %collective-permute-start.18 = (bf16[2,128,1024]{2,1,0:T(8,128)(2,1)S(1)}, bf16[2,128,1024]{2,1,0:T(8,128)(2,1)S(1)}, u32[]{:S(2)}, u32[]{:S(2)}) collective-permute-start(bf16[2,128,1024]{2,1,0:T(8,128)(2,1)S(1)} %pad_maximum_fusion.5), channel_id=1, source_target_pairs={{0,8},{4,12},{8,0},{12,4},{16,24},{20,28},{24,16},{28,20},{1,9},{5... | collective-permute-start | bytes 1572872 | tf_op jit(solution)/shard_map/ppermute | solution.py:84
  99.0 4.0 %collective-permute-done.18.refs_4_ = bf16[2,128,1024]{2,1,0:T(8,128)(2,1)S(1)} collective-permute-done((bf16[2,128,1024]{2,1,0:T(8,128)(2,1)S(1)}, bf16[2,128,1024]{2,1,0:T(8,128)(2,1)S(1)}, u32[]{:S(2)}, u32[]{:S(2)}) %collective-permute-start.18) | collective-permute-done | bytes 524320 | tf_op jit(solution)/shard_map/ppermute | solution.py:84
  113.1 3.0 %collective-permute-done.20 = bf16[128,512]{1,0:T(8,128)(2,1)S(1)} collective-permute-done((bf16[128,512]{1,0:T(8,128)(2,1)S(1)}, bf16[128,512]{1,0:T(8,128)(2,1)S(1)}, u32[]{:S(2)}, u32[]{:S(2)}) %collective-permute-start.20) | collective-permute-done | bytes 131104 | tf_op jit(solution)/shard_map/ppermute | solution.py:84
  116.1 6.4 %collective-permute-done.21.refs_3_ = bf16[1,128,1024]{2,1,0:T(8,128)(2,1)S(1)} collective-permute-done((bf16[1,128,1024]{2,1,0:T(8,128)(2,1)S(1)}, bf16[1,128,1024]{2,1,0:T(8,128)(2,1)S(1)}, u32[]{:S(2)}, u32[]{:S(2)}) %collective-permute-start.21) | collective-permute-done | bytes 262176 | tf_op jit(solution)/shard_map/ppermute | solution.py:84
  130.8 3.5 %collective-permute-done.24 = bf16[2,128,512]{2,1,0:T(8,128)(2,1)S(1)} collective-permute-done((bf16[2,128,512]{2,1,0:T(8,128)(2,1)S(1)}, bf16[2,128,512]{2,1,0:T(8,128)(2,1)S(1)}, u32[]{:S(2)}, u32[]{:S(2)}) %collective-permute-start.24) | collective-permute-done | bytes 262176 | tf_op jit(solution)/shard_map/ppermute | solution.py:84
  134.3 4.5 %feed.3 = (bf16[512,1024]{1,0:T(8,128)(2,1)S(1)}, bf16[512,1024]{1,0:T(8,128)(2,1)}) custom-call(bf16[1,1024,1024]{2,1,0:T(8,128)(2,1)S(1)} %get-tuple-element.139.up, f32[1,1024]{1,0:T(1,128)S(1)} %bitcast.82, bf16[1024,1024]{1,0:T(8,128)(2,1)S(1)} %get-tuple-element.143.normed, bf16[1024,1024]{1,0:T(8,128)(2,1)S(1)} %get-tuple-element.132.ghidden), custom_call_target="tpu_custom_call" | custom-call | tf_op jit(solution)/shard_map/feed/pallas_call | solution.py:573
  146.7 10.1 %collective-permute-done.25.side = bf16[256,1024]{1,0:T(8,128)(2,1)S(1)} collective-permute-done((bf16[256,1024]{1,0:T(8,128)(2,1)}, bf16[256,1024]{1,0:T(8,128)(2,1)S(1)}, u32[]{:S(2)}, u32[]{:S(2)}) %collective-permute-start.25) | collective-permute-done | bytes 524320 | tf_op jit(solution)/shard_map/ppermute | solution.py:84
  157.7 2.7 %middle.1 = (f32[256,1024]{1,0:T(8,128)S(1)}, bf16[2,256,256]{2,1,0:T(8,128)(2,1)S(1)}, bf16[2,256,256]{2,1,0:T(8,128)(2,1)S(1)}) custom-call(bf16[512,1024]{1,0:T(8,128)(2,1)} %get-tuple-element.151.own, bf16[512,1024]{1,0:T(8,128)(2,1)} %collective-permute-done.27.core, bf16[256,1024]{1,0:T(8,128)(2,1)S(1)} %collective-permute-done.25.side, ...), custom_call_target="tpu_custom_call" | custom-call | tf_op jit(solution)/shard_map/middle/pallas_call | solution.py:653
  162.1 5.9 %collective-permute-done.30.side = bf16[2,256,256]{2,1,0:T(8,128)(2,1)S(1)} collective-permute-done((bf16[2,256,256]{2,1,0:T(8,128)(2,1)S(1)}, bf16[2,256,256]{2,1,0:T(8,128)(2,1)S(1)}, u32[]{:S(2)}, u32[]{:S(2)}) %collective-permute-start.30) | collective-permute-done | bytes 262176 | tf_op jit(solution)/shard_map/ppermute | solution.py:84
  171.8 5.7 %attend_back.2.one = bf16[3,1024,128]{2,1,0:T(8,128)(2,1)S(1)} custom-call(bf16[3,1024,256]{2,1,0:T(8,128)(2,1)S(1)} %copy-done.2, bf16[1024,256]{1,0:T(8,128)(2,1)S(1)} %get-tuple-element.169.gmix, f32[8,1024]{1,0:T(8,128)S(1)} %get-tuple-element.165.log_sums, f32[8,1024]{1,0:T(8,128)S(1)} %get-tuple-element.166.inner, ...), custom_call_target="tpu_custom_call" | custom-call | flops 1610612736 | bytes 3932160 | tf_op jit(solution)/shard_map/attend_back/pallas_call | solution.py:428
  178.8 6.0 %attend_back.3.two = bf16[3,1024,128]{2,1,0:T(8,128)(2,1)S(1)} custom-call(bf16[3,1024,256]{2,1,0:T(8,128)(2,1)S(1)} %copy-done.2, bf16[1024,256]{1,0:T(8,128)(2,1)S(1)} %get-tuple-element.169.gmix, f32[8,1024]{1,0:T(8,128)S(1)} %get-tuple-element.165.log_sums, f32[8,1024]{1,0:T(8,128)S(1)} %get-tuple-element.166.inner, ...), custom_call_target="tpu_custom_call" | custom-call | flops 1610612736 | bytes 3932160 | tf_op jit(solution)/shard_map/attend_back/pallas_call | solution.py:428
  186.7 4.2 %collective-permute-done.37 = f32[2,16,256]{2,1,0:T(8,128)S(1)} collective-permute-done((f32[2,16,256]{2,1,0:T(8,128)S(1)}, f32[2,16,256]{2,1,0:T(8,128)S(1)}, u32[]{:S(2)}, u32[]{:S(2)}) %collective-permute-start.37) | collective-permute-done | bytes 32800 | tf_op jit(solution)/shard_map/ppermute | solution.py:84
  198.2 10.0 %collective-permute-done.41 = f32[16,512]{1,0:T(8,128)S(1)} collective-permute-done((f32[16,512]{1,0:T(8,128)S(1)}, f32[16,512]{1,0:T(8,128)S(1)}, u32[]{:S(2)}, u32[]{:S(2)}) %collective-permute-start.41) | collective-permute-done | bytes 32800 | tf_op jit(solution)/shard_map/ppermute | solution.py:84
  208.3 2.7 %update.1 = (f32[1,1]{1,0:T(1,128)}, f32[10,1024]{1,0:T(8,128)}, f32[10,1024]{1,0:T(8,128)}, f32[10,1024]{1,0:T(8,128)}, f32[128,512]{1,0:T(8,128)}, /*index=5*/...) custom-call(f32[16,512]{1,0:T(8,128)S(1)} %add.58.joint, ...), custom_call_target="tpu_custom_call" | custom-call | tf_op jit(solution)/shard_map/update/pallas_call | solution.py:975
  (231 shorter events, 83.2 us)
Async XLA Ops:
  2.8 16.2 %collective-permute-start = (bf16[512,256]{1,0:T(8,128)(2,1)S(1)}, bf16[512,256]{1,0:T(8,128)(2,1)}, u32[]{:S(2)}, u32[]{:S(2)}) collective-permute-start(bf16[512,256]{1,0:T(8,128)(2,1)S(1)} %get-tuple-element.193), channel_id=1, source_target_pairs={{0,16},{4,20},{8,24},{12,28},{16,0},{20,4},{24,8},{28,12},{1,17},{... | collective-permute-start | bytes 786440 | tf_op jit(solution)/shard_map/ppermute | solution.py:84
  20.0 16.7 %collective-permute-start.2 = (bf16[2,512,256]{2,1,0:T(8,128)(2,1)S(1)}, bf16[2,512,256]{2,1,0:T(8,128)(2,1)S(1)}, u32[]{:S(2)}, u32[]{:S(2)}) collective-permute-start(bf16[2,512,256]{2,1,0:T(8,128)(2,1)S(1)} %pad_maximum_fusion.1.refs_0_), channel_id=1, source_target_pairs={{0,8},{4,12},{8,0},{12,4},{16,24},{20,28},{24,16},{28,20},{1,9},{5... | collective-permute-start | bytes 1572872 | tf_op jit(solution)/shard_map/ppermute | solution.py:84
  20.7 17.3 %collective-permute-start.5 = (bf16[2,160,256]{2,1,0:T(8,128)(2,1)S(1)}, bf16[2,160,256]{2,1,0:T(8,128)(2,1)S(1)}, u32[]{:S(2)}, u32[]{:S(2)}) collective-permute-start(bf16[2,160,256]{2,1,0:T(8,128)(2,1)S(1)} %pad_maximum_fusion.10), channel_id=1, source_target_pairs={{0,16},{4,20},{8,24},{12,28},{16,0},{20,4},{24,8},{28,12},{1,17},{... | collective-permute-start | bytes 491528 | tf_op jit(solution)/shard_map/ppermute | solution.py:84
  24.2 19.4 %collective-permute-start.3 = (bf16[2,512,256]{2,1,0:T(8,128)(2,1)S(1)}, bf16[2,512,256]{2,1,0:T(8,128)(2,1)S(1)}, u32[]{:S(2)}, u32[]{:S(2)}) collective-permute-start(bf16[2,512,256]{2,1,0:T(8,128)(2,1)S(1)} %pad_maximum_fusion.1.refs_0_), channel_id=1, source_target_pairs={{0,4},{4,0},{8,12},{12,8},{16,20},{20,16},{24,28},{28,24},{1,5},{5... | collective-permute-start | bytes 1572872 | tf_op jit(solution)/shard_map/ppermute | solution.py:84
  36.6 14.8 %collective-permute-start.4 = (bf16[2,512,256]{2,1,0:T(8,128)(2,1)S(1)}, bf16[2,512,256]{2,1,0:T(8,128)(2,1)S(1)}, u32[]{:S(2)}, u32[]{:S(2)}) collective-permute-start(bf16[2,512,256]{2,1,0:T(8,128)(2,1)S(1)} %collective-permute-done.2.refs_1_), channel_id=1, source_target_pairs={{0,4},{4,0},{8,12},{12,8},{16,20},{20,16},{24,28},{28,24},{1,5},{5... | collective-permute-start | bytes 1572872 | tf_op jit(solution)/shard_map/ppermute | solution.py:84
  38.0 16.1 %collective-permute-start.6 = (bf16[4,160,256]{2,1,0:T(8,128)(2,1)S(1)}, bf16[4,160,256]{2,1,0:T(8,128)(2,1)S(1)}, u32[]{:S(2)}, u32[]{:S(2)}) collective-permute-start(bf16[4,160,256]{2,1,0:T(8,128)(2,1)S(1)} %pad_maximum_fusion.7.refs_0_), channel_id=1, source_target_pairs={{0,8},{4,12},{8,0},{12,4},{16,24},{20,28},{24,16},{28,20},{1,9},{5... | collective-permute-start | bytes 983048 | tf_op jit(solution)/shard_map/ppermute | solution.py:84
  39.9 14.6 %collective-permute-start.8 = (bf16[128,1024]{1,0:T(8,128)(2,1)S(1)}, bf16[128,1024]{1,0:T(8,128)(2,1)S(1)}, u32[]{:S(2)}, u32[]{:S(2)}) collective-permute-start(bf16[128,1024]{1,0:T(8,128)(2,1)S(1)} %copy-done.19), channel_id=1, source_target_pairs={{0,4},{4,0},{8,12},{12,8},{16,20},{20,16},{24,28},{28,24},{1,5},{5... | collective-permute-start | bytes 786440 | tf_op jit(solution)/shard_map/ppermute | solution.py:84
  66.1 27.9 %collective-permute-start.13 = (bf16[2,1024,256]{2,1,0:T(8,128)(2,1)S(1)}, bf16[2,1024,256]{2,1,0:T(8,128)(2,1)S(1)}, u32[]{:S(2)}, u32[]{:S(2)}) collective-permute-start(bf16[2,1024,256]{2,1,0:T(8,128)(2,1)S(1)} %pad_maximum_fusion), channel_id=1, source_target_pairs={{0,1},{1,0},{2,3},{3,2},{4,5},{5,4},{6,7},{7,6},{8,9},{9,8},{10,11... | collective-permute-start | bytes 3145736 | tf_op jit(solution)/shard_map/ppermute | solution.py:84
  66.3 20.1 %collective-permute-start.15 = (bf16[2,128,1024]{2,1,0:T(8,128)(2,1)S(1)}, bf16[2,128,1024]{2,1,0:T(8,128)(2,1)S(1)}, u32[]{:S(2)}, u32[]{:S(2)}) collective-permute-start(bf16[2,128,1024]{2,1,0:T(8,128)(2,1)S(1)} %pad_maximum_fusion.4.refs_0_), channel_id=1, source_target_pairs={{0,8},{4,12},{8,0},{12,4},{16,24},{20,28},{24,16},{28,20},{1,9},{5... | collective-permute-start | bytes 1572872 | tf_op jit(solution)/shard_map/ppermute | solution.py:84
  68.2 18.2 %collective-permute-start.16 = (bf16[2,128,1024]{2,1,0:T(8,128)(2,1)S(1)}, bf16[2,128,1024]{2,1,0:T(8,128)(2,1)S(1)}, u32[]{:S(2)}, u32[]{:S(2)}) collective-permute-start(bf16[2,128,1024]{2,1,0:T(8,128)(2,1)S(1)} %pad_maximum_fusion.4.refs_0_), channel_id=1, source_target_pairs={{0,4},{4,0},{8,12},{12,8},{16,20},{20,16},{24,28},{28,24},{1,5},{5... | collective-permute-start | bytes 1572872 | tf_op jit(solution)/shard_map/ppermute | solution.py:84
  70.4 15.3 %collective-permute-start.17 = (bf16[128,1024]{1,0:T(8,128)(2,1)S(1)}, bf16[128,1024]{1,0:T(8,128)(2,1)S(1)}, u32[]{:S(2)}, u32[]{:S(2)}) collective-permute-start(bf16[128,1024]{1,0:T(8,128)(2,1)S(1)} %copy-done.20), channel_id=1, source_target_pairs={{0,16},{4,20},{8,24},{12,28},{16,0},{20,4},{24,8},{28,12},{1,17},{... | collective-permute-start | bytes 786440 | tf_op jit(solution)/shard_map/ppermute | solution.py:84
  77.1 17.0 %collective-permute-start.11 = (bf16[2,512,256]{2,1,0:T(8,128)(2,1)S(1)}, bf16[2,512,256]{2,1,0:T(8,128)(2,1)S(1)}, u32[]{:S(2)}, u32[]{:S(2)}) collective-permute-start(bf16[2,512,256]{2,1,0:T(8,128)(2,1)S(1)} %pad_maximum_fusion.2), channel_id=1, source_target_pairs={{0,1},{1,0},{2,3},{3,2},{4,5},{5,4},{6,7},{7,6},{8,9},{9,8},{10,11... | collective-permute-start | bytes 1572872 | tf_op jit(solution)/shard_map/ppermute | solution.py:84
  86.4 16.6 %collective-permute-start.18 = (bf16[2,128,1024]{2,1,0:T(8,128)(2,1)S(1)}, bf16[2,128,1024]{2,1,0:T(8,128)(2,1)S(1)}, u32[]{:S(2)}, u32[]{:S(2)}) collective-permute-start(bf16[2,128,1024]{2,1,0:T(8,128)(2,1)S(1)} %pad_maximum_fusion.5), channel_id=1, source_target_pairs={{0,8},{4,12},{8,0},{12,4},{16,24},{20,28},{24,16},{28,20},{1,9},{5... | collective-permute-start | bytes 1572872 | tf_op jit(solution)/shard_map/ppermute | solution.py:84
  92.5 13.9 %collective-permute-start.19 = (bf16[2,128,1024]{2,1,0:T(8,128)(2,1)S(1)}, bf16[2,128,1024]{2,1,0:T(8,128)(2,1)S(1)}, u32[]{:S(2)}, u32[]{:S(2)}) collective-permute-start(bf16[2,128,1024]{2,1,0:T(8,128)(2,1)S(1)} %collective-permute-done.15.refs_2_), channel_id=1, source_target_pairs={{0,4},{4,0},{8,12},{12,8},{16,20},{20,16},{24,28},{28,24},{1,5},{5... | collective-permute-start | bytes 1572872 | tf_op jit(solution)/shard_map/ppermute | solution.py:84
  103.0 19.5 %collective-permute-start.22 = (bf16[2,128,1024]{2,1,0:T(8,128)(2,1)S(1)}, bf16[2,128,1024]{2,1,0:T(8,128)(2,1)S(1)}, u32[]{:S(2)}, u32[]{:S(2)}) collective-permute-start(bf16[2,128,1024]{2,1,0:T(8,128)(2,1)S(1)} %collective-permute-done.18.refs_4_), channel_id=1, source_target_pairs={{0,4},{4,0},{8,12},{12,8},{16,20},{20,16},{24,28},{28,24},{1,5},{5... | collective-permute-start | bytes 1572872 | tf_op jit(solution)/shard_map/ppermute | solution.py:84
  104.6 18.0 %collective-permute-start.21 = (bf16[1,128,1024]{2,1,0:T(8,128)(2,1)S(1)}, bf16[1,128,1024]{2,1,0:T(8,128)(2,1)S(1)}, u32[]{:S(2)}, u32[]{:S(2)}) collective-permute-start(bf16[1,128,1024]{2,1,0:T(8,128)(2,1)S(1)} %bitcast.77), channel_id=1, source_target_pairs={{0,4},{4,0},{8,12},{12,8},{16,20},{20,16},{24,28},{28,24},{1,5},{5... | collective-permute-start | bytes 786440 | tf_op jit(solution)/shard_map/ppermute | solution.py:84
  139.7 17.9 %collective-permute-start.27 = (bf16[512,1024]{1,0:T(8,128)(2,1)}, bf16[512,1024]{1,0:T(8,128)(2,1)}, u32[]{:S(2)}, u32[]{:S(2)}) collective-permute-start(bf16[512,1024]{1,0:T(8,128)(2,1)} %get-tuple-element.151.own), channel_id=1, source_target_pairs={{0,1},{1,0},{2,3},{3,2},{4,5},{5,4},{6,7},{7,6},{8,9},{9,8},{10,11... | collective-permute-start | bytes 3145736 | tf_op jit(solution)/shard_map/ppermute | solution.py:84
  141.0 20.2 %collective-permute-start.31 = (bf16[4,128,512]{2,1,0:T(8,128)(2,1)S(1)}, bf16[4,128,512]{2,1,0:T(8,128)(2,1)S(1)}, u32[]{:S(2)}, u32[]{:S(2)}) collective-permute-start(bf16[4,128,512]{2,1,0:T(8,128)(2,1)S(1)} %pad_maximum_fusion.6.refs_0_), channel_id=1, source_target_pairs={{0,4},{4,0},{8,12},{12,8},{16,20},{20,16},{24,28},{28,24},{1,5},{5... | collective-permute-start | bytes 1572872 | tf_op jit(solution)/shard_map/ppermute | solution.py:84
  142.6 14.3 %collective-permute-start.25 = (bf16[256,1024]{1,0:T(8,128)(2,1)}, bf16[256,1024]{1,0:T(8,128)(2,1)S(1)}, u32[]{:S(2)}, u32[]{:S(2)}) collective-permute-start(bf16[256,1024]{1,0:T(8,128)(2,1)} %copy-done.50), channel_id=1, source_target_pairs={{0,2},{1,3},{2,0},{3,1},{4,6},{5,7},{6,4},{7,5},{8,10},{9,11},{10,... | collective-permute-start | bytes 1572872 | tf_op jit(solution)/shard_map/ppermute | solution.py:84
  145.8 15.5 %collective-permute-start.28 = (bf16[256,1024]{1,0:T(8,128)(2,1)S(1)}, bf16[256,1024]{1,0:T(8,128)(2,1)S(1)}, u32[]{:S(2)}, u32[]{:S(2)}) collective-permute-start(bf16[256,1024]{1,0:T(8,128)(2,1)S(1)} %fusion.11), channel_id=1, source_target_pairs={{0,1},{1,0},{2,3},{3,2},{4,5},{5,4},{6,7},{7,6},{8,9},{9,8},{10,11... | collective-permute-start | bytes 1572872 | tf_op jit(solution)/shard_map/ppermute | solution.py:84
  168.0 16.8 %collective-permute-start.26 = (bf16[256,1024]{1,0:T(8,128)(2,1)S(1)}, bf16[256,1024]{1,0:T(8,128)(2,1)S(1)}, u32[]{:S(2)}, u32[]{:S(2)}) collective-permute-start(bf16[256,1024]{1,0:T(8,128)(2,1)S(1)} %fusion.14), channel_id=1, source_target_pairs={{0,1},{1,0},{2,3},{3,2},{4,5},{5,4},{6,7},{7,6},{8,9},{9,8},{10,11... | collective-permute-start | bytes 1572872 | tf_op jit(solution)/shard_map/ppermute | solution.py:84
  168.5 16.3 %collective-permute-start.29 = (bf16[256,1024]{1,0:T(8,128)(2,1)S(1)}, bf16[256,1024]{1,0:T(8,128)(2,1)S(1)}, u32[]{:S(2)}, u32[]{:S(2)}) collective-permute-start(bf16[256,1024]{1,0:T(8,128)(2,1)S(1)} %fusion.20), channel_id=1, source_target_pairs={{0,2},{1,3},{2,0},{3,1},{4,6},{5,7},{6,4},{7,5},{8,10},{9,11},{10,... | collective-permute-start | bytes 1572872 | tf_op jit(solution)/shard_map/ppermute | solution.py:84
  193.1 17.9 %collective-permute-start.38 = (bf16[512,1024]{1,0:T(8,128)(2,1)S(1)}, bf16[512,1024]{1,0:T(8,128)(2,1)S(1)}, u32[]{:S(2)}, u32[]{:S(2)}) collective-permute-start(bf16[512,1024]{1,0:T(8,128)(2,1)S(1)} %project_back.5.own), channel_id=1, source_target_pairs={{0,1},{1,0},{2,3},{3,2},{4,5},{5,4},{6,7},{7,6},{8,9},{9,8},{10,11... | collective-permute-start | bytes 3145736 | tf_op jit(solution)/shard_map/ppermute | solution.py:84
  193.2 17.8 %collective-permute-start.39 = (bf16[256,1024]{1,0:T(8,128)(2,1)S(1)}, bf16[256,1024]{1,0:T(8,128)(2,1)S(1)}, u32[]{:S(2)}, u32[]{:S(2)}) collective-permute-start(bf16[256,1024]{1,0:T(8,128)(2,1)S(1)} %project_back.4), channel_id=1, source_target_pairs={{0,2},{1,3},{2,0},{3,1},{4,6},{5,7},{6,4},{7,5},{8,10},{9,11},{10,... | collective-permute-start | bytes 1572872 | tf_op jit(solution)/shard_map/ppermute | solution.py:84
  (76 other events, 1075.3 us)

commit v2 on v1

--- a/solution.py
+++ b/solution.py
@@ -561,29 +561,22 @@
     )(normed, ghidden, bias, *pieces)
 
 
-def feed(bits, normed, ghidden, up, bias, *plus):
+def feed(differ, normed, ghidden, up, bias, *plus):
     rows, width = normed.shape
     share = rows // lax.axis_size("tensor")
     units = up.shape[-1]
-    steps = len(bits)
-    outs = (
-        shaped((steps * share, units), jnp.bfloat16),
-        shaped((steps * share, width), jnp.bfloat16),
-    )
+    outs = (shaped((share, units), jnp.bfloat16), shaped((share, width), jnp.bfloat16))
     return pl.pallas_call(
         feed_kernel,
-        grid=(steps,),
+        grid=(1,),
         in_specs=[
             whole_spec(up),
             whole_spec(bias),
-            pl.BlockSpec((share, width), block_of(*bits)),
-            pl.BlockSpec((share, units), block_of(*bits)),
+            pl.BlockSpec((share, width), block_of(differ)),
+            pl.BlockSpec((share, units), block_of(differ)),
         ]
         + [whole_spec(p) for p in plus],
-        out_specs=[
-            pl.BlockSpec((share, units), lambda i: (i, 0)),
-            pl.BlockSpec((share, width), lambda i: (i, 0)),
-        ],
+        out_specs=[whole_spec(o) for o in outs],
         out_shape=outs,
         compiler_params=limited(),
         name="feed",
@@ -653,7 +646,7 @@
     return pl.pallas_call(
         middle_kernel,
         grid=(1,),
-        in_specs=[row_of(share, width, 1), row_of(share, width, 0), whole_spec(side), mine]
+        in_specs=[whole_spec(own), whole_spec(core), whole_spec(side), mine]
         + [whole_spec(a) for a in (resid, norms, *merges)],
         out_specs=[whole_spec(o) for o in outs],
         out_shape=outs,
@@ -803,13 +796,15 @@
     sent = encoded_own.astype(jnp.bfloat16).reshape(PAD, halves, local).transpose(1, 0, 2)
     merging = jnp.concatenate([merge_weight, sent.reshape(halves * PAD, local)])
 
+    own_start = dp_index.astype(jnp.uint32) * dec_rows
     small = lax.axis_size("dp") == 8
     if small:
         y, z, far = 1, 2, 4
         attention_far = swap(attention, "dp", far)
         merging_side = swap(merging, "dp", y)[None]
         up_side = swap(up_weight, "dp", y)[None]
-        pair = jnp.stack([attention, after(attention_far, merging_side)])
+        attention_far, own_start = after((attention_far, own_start), merging_side, up_side)
+        pair = jnp.stack([attention, attention_far])
         near = swap(pair, "dp", z)
         pair_side = swap(pair, "dp", y)
         merging_pair = joined(merging[None], merging_side)
@@ -830,7 +825,7 @@
         tokens, norm_params, attention_bias, attention, hidden_size
     )
     if small:
-        down_far = after(down_far, projected, up_side)
+        down_far = after(down_far, projected)
         down_pair = joined(down_weight[None], down_far)
         down_near = swap(down_pair, "dp", z)
         down_pair_side = swap(down_pair, "dp", y)
@@ -838,7 +833,7 @@
     pieces, places = merging
     pieces = after(pieces, projected)
     if small:
-        pieces = after(pieces, down_far, up_side)
+        pieces = after(pieces, down_far)
     merge_own, encoded = gather_merge(pieces, places, width, hidden_size)
     mix_first, sums_first, hidden, prefix = attend_first(
         projected, encoded, encoder_bias[None], decoder_full, decoder_bias
@@ -847,37 +842,45 @@
     def from_others(values, side):
         return values, side, swap(jnp.stack([values, side]), "tensor", CORE)
 
-    merges = from_others(merge_own, after(swap(merge_own, "tensor", SIDE), mix_first))
+    merge_side = after(swap(merge_own, "tensor", SIDE), mix_first)
+    if small:
+        merge_side, up_far = after((merge_side, up_far))
+    merges = from_others(merge_own, merge_side)
     mixes_first = from_others(mix_first, swap(mix_first, "tensor", SIDE))
-    mix_second, sums_second = attend_second(projected, prefix)
+    proj_late = after(projected, mixes_first[1])
+    if small:
+        proj_late, down_near, down_pair_side, up_far = after(
+            (proj_late, down_near, down_pair_side, up_far)
+        )
+        down_near_side = swap(down_near, "dp", y)
+        up_near = swap(joined(up_weight[None], up_far), "dp", z)
+        up_far_side = swap(up_far, "dp", y)
+    mix_second, sums_second = attend_second(proj_late, prefix)
     mix_side = swap(mix_second, "tensor", SIDE)
+    branch_late = branch_bias
     if small:
-        down_near, down_pair_side, up_far = after((down_near, down_pair_side, up_far), mix_second)
-        down_near_side = swap(down_near, "dp", y)
+        branch_late, down_near_side, up_near = after((branch_bias, down_near_side, up_near), mix_second)
         down = (
             (down_pair, down_pair_side, down_near, down_near_side),
             ((0, 4), (1, 5), (2, 6), (3, 7)),
         )
-        up_far = after(up_far, mixes_first[1])
-        up_near = swap(joined(up_weight[None], up_far), "dp", z)
-        up_far_side = swap(up_far, "dp", y)
-    first_half = merge_half(tokens, norm_params, branch_bias, mixes_first, merges)
+        up_near_side = swap(up_near, "dp", y)
+    first_half = merge_half(tokens, norm_params, branch_late, mixes_first, merges)
     mixes_second = from_others(mix_second, after(mix_side, first_half))
-    cotangent_late = after(cotangent, first_half)
+    down_full, grad_hidden = down_back(after(cotangent, first_half), down)
+    branch_late = after(branch_bias, grad_hidden)
     if small:
-        up_near = after(up_near, first_half)
-        cotangent_late = after(cotangent_late, up_near)
-        up_near_side = swap(up_near, "dp", y)
+        encoder_far = swap(after(encoder_low, first_half), "dp", far)
+        branch_late, up_far_side = after((branch_late, up_far_side))
         up = (
             (up_weight[None], up_side, up_far, up_far_side, up_near, up_near_side),
             ((0,), (1,), (4,), (5,), (2, 6), (3, 7)),
         )
-    down_full, grad_hidden = down_back(cotangent_late, down)
+    normed, resid = merge_half(
+        tokens, norm_params, branch_late, mixes_second, merges, after(first_half, grad_hidden)
+    )
     if small:
-        encoder_far = swap(after(encoder_low, grad_hidden), "dp", far)
-    normed, resid = merge_half(
-        tokens, norm_params, branch_bias, mixes_second, merges, after(first_half, grad_hidden)
-    )
+        normed = after(normed, encoder_far)
 
     def branch(act, *plus):
         part = lax.dot_general(
@@ -893,24 +896,25 @@
     act_both, up_both, up_full = feed_first(BOTH, normed, grad_hidden, up, bias)
     up_both = swap(up_both, "tensor", CORE)
     if small:
-        encoder_pair = jnp.stack([encoder_low, encoder_far])
+        encoder_pair = jnp.stack([encoder_low, after(encoder_far, act_both)])
         encoder_near = swap(encoder_pair, "dp", z)
-    act_side, up_send = feed((SIDE,), normed, grad_hidden, up_full, bias, up_both)
+    act_side, up_send = feed(SIDE, normed, grad_hidden, up_full, bias, up_both)
     up_from = swap(up_send, "tensor", SIDE)
-    normed = after(normed, up_send)
+    act_core, up_core = feed(CORE, after(normed, up_send), grad_hidden, up_full, bias)
+    up_core = swap(up_core, "tensor", CORE)
+    act_own, up_own = feed(OWN, after(normed, act_core), grad_hidden, up_full, bias)
+    out_both = branch(after(act_both, act_own))
+    up_from = after(up_from, out_both)
     if small:
-        normed = after(normed, encoder_near)
+        encoder_near = after(encoder_near, act_own)
         encoder_quad = joined(encoder_pair, encoder_near)
         encoder_side = swap(encoder_quad, "dp", y)
         encoder = ((encoder_quad, encoder_side), ((0, 4, 2, 6), (1, 5, 3, 7)))
-    act_rest, up_rest = feed((CORE, OWN), normed, grad_hidden, up_full, bias)
-    up_core = swap(up_rest, "tensor", CORE)
-    out_both = branch(after(act_both, act_rest))
-    out_core = branch(act_rest[:share])
-    up_from = after(up_from, out_both, out_core)
-    out_own = branch(after(act_rest, up_from)[share:])
-    up_core = after(up_core, out_own)
-    grad_resid, keep, send = middle(up_rest, up_core, up_from, cotangent, resid, norm_params, merges)
+        up_from = after(up_from, encoder_near)
+    out_core = branch(after(act_core, up_from))
+    out_own = branch(after(act_own, up_from))
+    up_core = after(up_core, out_own, out_core)
+    grad_resid, keep, send = middle(up_own, up_core, up_from, cotangent, resid, norm_params, merges)
     out_both = swap(out_both, "tensor", CORE)
     from_side = swap(send, "tensor", SIDE)
     core_keep = swap(keep, "tensor", CORE)
@@ -918,7 +922,9 @@
     out_send = branch(after(act_side, send), out_both)
     out_from = swap(out_send, "tensor", SIDE)
     encoder_full = assemble((after(encoder[0], send), encoder[1]), (1, width, hidden_size))
-    hidden_own = lax.dynamic_slice_in_dim(after(hidden, send), dp_index * dec_rows, dec_rows, 1)
+    hidden_own = lax.dynamic_slice(
+        after(hidden, send), (jnp.uint32(0), own_start), (hidden.shape[0], dec_rows)
+    )
     from_side = after(from_side, out_send, encoder_full, hidden_own)
     core_side = swap(from_side, "tensor", CORE)
     grad_prefix, grad_mix, log_sums, inner, grad_query = prefix_back(
@@ -935,13 +941,13 @@
     )
     prefix_total = prefix_total + swap(prefix_total, "dp", 2)
     gprojs = after((grad_first, grad_second), prefix_total, out_from, out_core)
+    back_both = swap(project_back((BOTH,), gprojs, attend_full), "tensor", CORE)
+    back_send = project_back((SIDE,), gprojs, attend_full, back_both)
+    back_from = swap(back_send, "tensor", SIDE)
     bits = 4
     while bits < lax.axis_size("dp"):
-        prefix_total = prefix_total + swap(prefix_total, "dp", bits)
+        prefix_total = prefix_total + after(swap(prefix_total, "dp", bits), back_send)
         bits *= 2
-    back_both = swap(project_back((BOTH,), gprojs, attend_full), "tensor", CORE)
-    back_send = project_back((SIDE,), gprojs, attend_full, after(back_both, prefix_total))
-    back_from = swap(back_send, "tensor", SIDE)
     joint = pl.pallas_call(
         tail_kernel,
         out_shape=shaped((PAD, hidden_size), jnp.float32),
@@ -950,8 +956,8 @@
         cost_estimate=brief(),
     )(prefix_total, hidden, decoder_full)
     joint = joint + swap(joint, "tensor", CORE)
-    back_rest = project_back((CORE, OWN), after(gprojs, back_send), attend_full)
-    joint = joint + swap(joint, "tensor", SIDE)
+    back_rest = project_back((CORE, OWN), after(gprojs, back_send, prefix_total), attend_full)
+    joint_side = swap(joint, "tensor", SIDE)
     back_core = swap(back_rest, "tensor", CORE)
     output = (
         resid
@@ -963,6 +969,7 @@
         + branch_bias[1]
     )
     input_grad = last(back_rest, back_core, back_from, tokens, grad_resid, norm_params)
+    joint = joint + after(joint_side, input_grad)
 
     params = [
         (prefix_table, first_table, second_table),

time: 213 us -> 191 us (0.90)
  waiting for transfers between devices: 87.7 us -> 78.8 us
  starting transfers between devices: 51.8 us -> 47.1 us
  local copies, waits for them, and re-layouts: 4.44 us -> 0.9 us
    ppermute x42, waiting for transfers between devices: 87.7 us -> 78.8 us  [swap(): return lax.ppermute(values, axis, [(i, i ^ bits) for i in range(size)])]
    ppermute x42, starting transfers between devices: 51.8 us -> 47.1 us  [swap(): return lax.ppermute(values, axis, [(i, i ^ bits) for i in range(size)])]
    unnamed x116 -> x46, local copies, waits for them, and re-layouts: 3.67 us -> 0.13 us
    pallas_call x3 -> x4, Pallas kernels: 9.01 us -> 6.98 us  [the longest x3 5.49 us: feed(): pl.pallas_call(feed_kernel, grid=(1,), in_specs=[whole_spec(up), whole_sp...]
  transfers between devices with their start and end apart: 42 -> 42, of which waited for: 23 -> 21; matrix products, arithmetic and copies ran while one was open for 5% -> 5% of each run, Pallas kernels for 20% -> 22%
where the time goes in v2:
time: 191 us
  waiting for transfers between devices  78.8 us (41%)
  Pallas kernels  51.4 us (27%)
  starting transfers between devices  47.1 us (25%)
  other arithmetic  7.22 us (4%)
  matrix products  4.14 us (2%)
    ppermute x42, waiting for transfers between devices, swap(): return lax.ppermute(values, axis, [(i, i ^ bits) for i in range(size)])  78.8 us
    ppermute x42, starting transfers between devices, swap(): return lax.ppermute(values, axis, [(i, i ^ bits) for i in range(size)])  47.1 us
    pallas_call x2, Pallas kernels, attend_back(): pl.pallas_call(functools.partial(attend_back_kernel, pair), grid=(1,), in...  11.4 us
    pallas_call x1, Pallas kernels, attend_second(): pl.pallas_call(functools.partial(attend_kernel, rows // 2), out_shape=out...  6.96 us
    pallas_call x3, Pallas kernels, feed(): pl.pallas_call(feed_kernel, grid=(1,), in_specs=[whole_spec(up), whole_sp...  5.49 us
    pallas_call x1, Pallas kernels, attend_first(): pl.pallas_call(attend_first_kernel, out_shape=outs, scratch_shapes=[pltpu...  4.79 us
    pallas_call x2, Pallas kernels, merge_half(): pl.pallas_call(functools.partial(merge_kernel, first), grid=(steps,), in_...  4.65 us
  transfers between devices with their start and end apart: 42, of which 21 were waited for; matrix products, arithmetic and copies ran while one was open for 5% of the time, Pallas kernels for 22%

profile of v2, /device:TPU:0, one launch (start us, length us, event | category | flops | bytes accessed | tf_op | source)
XLA Modules:
  0.0 191.1 jit_solution(7843320844531504287)
XLA Ops:
  2.8 4.1 %collective-permute-start = (bf16[512,256]{1,0:T(8,128)(2,1)S(1)}, bf16[512,256]{1,0:T(8,128)(2,1)}, u32[]{:S(2)}, u32[]{:S(2)}) collective-permute-start(bf16[512,256]{1,0:T(8,128)(2,1)S(1)} %get-tuple-element.225), channel_id=1, source_target_pairs={{0,16},{4,20},{8,24},{12,28},{16,0},{20,4},{24,8},{28,12},{1,17},{... | collective-permute-start | bytes 786440 | tf_op jit(solution)/shard_map/ppermute | solution.py:84
  13.3 4.1 %collective-permute-done.1 = bf16[160,256]{1,0:T(8,128)(2,1)S(1)} collective-permute-done((bf16[160,256]{1,0:T(8,128)(2,1)}, bf16[160,256]{1,0:T(8,128)(2,1)S(1)}, u32[]{:S(2)}, u32[]{:S(2)}) %collective-permute-start.1) | collective-permute-done | bytes 81952 | tf_op jit(solution)/shard_map/ppermute | solution.py:84
  20.7 3.6 %collective-permute-start.6 = (bf16[2,160,256]{2,1,0:T(8,128)(2,1)S(1)}, bf16[2,160,256]{2,1,0:T(8,128)(2,1)S(1)}, u32[]{:S(2)}, u32[]{:S(2)}) collective-permute-start(bf16[2,160,256]{2,1,0:T(8,128)(2,1)S(1)} %pad_maximum_fusion.10), channel_id=1, source_target_pairs={{0,16},{4,20},{8,24},{12,28},{16,0},{20,4},{24,8},{28,12},{1,17},{... | collective-permute-start | bytes 491528 | tf_op jit(solution)/shard_map/ppermute | solution.py:84
  25.7 10.9 %collective-permute-done.3.refs_1_ = bf16[2,512,256]{2,1,0:T(8,128)(2,1)S(1)} collective-permute-done((bf16[2,512,256]{2,1,0:T(8,128)(2,1)S(1)}, bf16[2,512,256]{2,1,0:T(8,128)(2,1)S(1)}, u32[]{:S(2)}, u32[]{:S(2)}) %collective-permute-start.3) | collective-permute-done | bytes 524320 | tf_op jit(solution)/shard_map/ppermute | solution.py:84
  39.9 3.3 %collective-permute-start.8 = (bf16[128,1024]{1,0:T(8,128)(2,1)S(1)}, bf16[128,1024]{1,0:T(8,128)(2,1)S(1)}, u32[]{:S(2)}, u32[]{:S(2)}) collective-permute-start(bf16[128,1024]{1,0:T(8,128)(2,1)S(1)} %copy-done.22), channel_id=1, source_target_pairs={{0,16},{4,20},{8,24},{12,28},{16,0},{20,4},{24,8},{28,12},{1,17},{... | collective-permute-start | bytes 786440 | tf_op jit(solution)/shard_map/ppermute | solution.py:84
  43.1 5.7 %collective-permute-done.5.refs_3_ = bf16[2,512,256]{2,1,0:T(8,128)(2,1)S(1)} collective-permute-done((bf16[2,512,256]{2,1,0:T(8,128)(2,1)S(1)}, bf16[2,512,256]{2,1,0:T(8,128)(2,1)S(1)}, u32[]{:S(2)}, u32[]{:S(2)}) %collective-permute-start.5) | collective-permute-done | bytes 524320 | tf_op jit(solution)/shard_map/ppermute | solution.py:84
  48.9 2.7 %project.1 = (bf16[3,1024,256]{2,1,0:T(8,128)(2,1)S(1)}, bf16[3,1024,256]{2,1,0:T(8,128)(2,1)S(1)}, bf16[2,512,256]{2,1,0:T(8,128)(2,1)S(1)}) custom-call(bf16[1024,1024]{1,0:T(8,128)(2,1)S(1)} %copy-done, f32[4,1024]{1,0:T(4,128)S(1)} %copy-done.5, f32[3,256]{1,0:T(4,128)S(1)} %copy-done.17, bf16[2,512,256]{2,1,0:T(8,128)(2,1)S(1)} %pad_maximum_fusion.1.refs_0_, ...), custom_call_target="tpu_custom_call" | custom-call | tf_op jit(solution)/shard_map/project/pallas_call | solution.py:187
  54.4 2.6 %collective-permute-start.13 = (bf16[128,1024]{1,0:T(8,128)(2,1)S(1)}, bf16[128,1024]{1,0:T(8,128)(2,1)S(1)}, u32[]{:S(2)}, u32[]{:S(2)}) collective-permute-start(bf16[128,1024]{1,0:T(8,128)(2,1)S(1)} %copy-done.3), channel_id=1, source_target_pairs={{0,16},{4,20},{8,24},{12,28},{16,0},{20,4},{24,8},{28,12},{1,17},{... | collective-permute-start | bytes 786440 | tf_op jit(solution)/shard_map/ppermute | solution.py:84
  60.5 4.8 %attend_first.1 = (bf16[512,256]{1,0:T(8,128)(2,1)S(1)}, f32[512,128]{1,0:T(8,128)S(1)}, f32[16,512]{1,0:T(8,128)S(1)}, bf16[2,16,256]{2,1,0:T(8,128)(2,1)S(1)}) custom-call(bf16[3,1024,256]{2,1,0:T(8,128)(2,1)S(1)} %get-tuple-element.140.proj.query, f32[16,512]{1,0:T(8,128)S(1)} %get-tuple-element.130.encoded, f32[1,512]{1,0:T(1,128)S(1)} %bitcast.84, ...), custom_call_target="tpu_custom_call" | custom-call | tf_op jit(solution)/shard_map/attend_first/pallas_call | solution.py:286
  68.3 8.1 %collective-permute-done.9.refs_1_ = bf16[512,256]{1,0:T(8,128)(2,1)S(1)} collective-permute-done((bf16[512,256]{1,0:T(8,128)(2,1)S(1)}, bf16[512,256]{1,0:T(8,128)(2,1)S(1)}, u32[]{:S(2)}, u32[]{:S(2)}) %collective-permute-start.9) | collective-permute-done | bytes 262176 | tf_op jit(solution)/shard_map/ppermute | solution.py:84
  78.9 7.0 %attend_second.1 = (bf16[512,256]{1,0:T(8,128)(2,1)S(1)}, f32[512,128]{1,0:T(8,128)S(1)}) custom-call(bf16[3,1024,256]{2,1,0:T(8,128)(2,1)S(1)} %get-tuple-element.140.proj.query, bf16[2,16,256]{2,1,0:T(8,128)(2,1)S(1)} %get-tuple-element.141.prefix), custom_call_target="tpu_custom_call" | custom-call | tf_op jit(solution)/shard_map/attend_second/pallas_call | solution.py:299
  86.5 3.5 %collective-permute-done.14.refs_3_ = bf16[2,128,1024]{2,1,0:T(8,128)(2,1)S(1)} collective-permute-done((bf16[2,128,1024]{2,1,0:T(8,128)(2,1)S(1)}, bf16[2,128,1024]{2,1,0:T(8,128)(2,1)S(1)}, u32[]{:S(2)}, u32[]{:S(2)}) %collective-permute-start.14) | collective-permute-done | bytes 524320 | tf_op jit(solution)/shard_map/ppermute | solution.py:84
  91.5 2.2 %merge_first.1 = (bf16[1024,1024]{1,0:T(8,128)(2,1)S(1)}, f32[256,1024]{1,0:T(8,128)S(1)}) custom-call(bf16[1024,1024]{1,0:T(8,128)(2,1)S(1)} %copy-done, f32[4,1024]{1,0:T(4,128)S(1)} %copy-done.5, f32[2,1024]{1,0:T(2,128)S(1)} %copy-done.14, bf16[512,256]{1,0:T(8,128)(2,1)S(1)} %get-tuple-element.132.refs_0_.mix_first, ...), custom_call_target="tpu_custom_call" | custom-call | tf_op jit(solution)/shard_map/merge_first/pallas_call | solution.py:483
  96.9 3.4 %collective-permute-start.21 = (bf16[128,512]{1,0:T(8,128)(2,1)S(1)}, bf16[128,512]{1,0:T(8,128)(2,1)S(1)}, u32[]{:S(2)}, u32[]{:S(2)}) collective-permute-start(bf16[128,512]{1,0:T(8,128)(2,1)S(1)} %convert_element_type.48), channel_id=1, source_target_pairs={{0,16},{4,20},{8,24},{12,28},{16,0},{20,4},{24,8},{28,12},{1,17},{... | collective-permute-start | bytes 393224 | tf_op jit(solution)/shard_map/ppermute | solution.py:84
  100.3 2.5 %down_back.1 = (bf16[1,1024,1024]{2,1,0:T(8,128)(2,1)S(1)}, bf16[1024,1024]{1,0:T(8,128)(2,1)S(1)}) custom-call(bf16[1024,1024]{1,0:T(8,128)(2,1)S(1)} %copy-done.1, bf16[2,128,1024]{2,1,0:T(8,128)(2,1)S(1)} %pad_maximum_fusion.2.refs_0_, bf16[2,128,1024]{2,1,0:T(8,128)(2,1)S(1)} %collective-permute-done.11.refs_1_, ...), custom_call_target="tpu_custom_call" | custom-call | tf_op jit(solution)/shard_map/down_back/pallas_call | solution.py:209
  102.8 11.9 %collective-permute-done.18.refs_3_ = bf16[1,128,1024]{2,1,0:T(8,128)(2,1)S(1)} collective-permute-done((bf16[1,128,1024]{2,1,0:T(8,128)(2,1)S(1)}, bf16[1,128,1024]{2,1,0:T(8,128)(2,1)S(1)}, u32[]{:S(2)}, u32[]{:S(2)}) %collective-permute-start.18) | collective-permute-done | bytes 262176 | tf_op jit(solution)/shard_map/ppermute | solution.py:84
  114.7 2.4 %merge_second.1 = (bf16[1024,1024]{1,0:T(8,128)(2,1)S(1)}, f32[256,1024]{1,0:T(8,128)S(1)}) custom-call(bf16[1024,1024]{1,0:T(8,128)(2,1)S(1)} %copy-done, f32[4,1024]{1,0:T(4,128)S(1)} %copy-done.5, f32[2,1024]{1,0:T(2,128)S(1)} %copy-done.14, bf16[512,256]{1,0:T(8,128)(2,1)S(1)} %get-tuple-element.142.refs_0_.mix_second, ...), custom_call_target="tpu_custom_call", output_to_operand_aliasing={{0}: (9, {})} | custom-call | tf_op jit(solution)/shard_map/merge_second/pallas_call | solution.py:483
  133.0 4.1 %collective-permute-done.24.side = bf16[256,1024]{1,0:T(8,128)(2,1)S(1)} collective-permute-done((bf16[256,1024]{1,0:T(8,128)(2,1)S(1)}, bf16[256,1024]{1,0:T(8,128)(2,1)S(1)}, u32[]{:S(2)}, u32[]{:S(2)}) %collective-permute-start.24) | collective-permute-done | bytes 524320 | tf_op jit(solution)/shard_map/ppermute | solution.py:84
  140.8 4.0 %collective-permute-done.31.refs_1_ = bf16[4,128,512]{2,1,0:T(8,128)(2,1)S(1)} collective-permute-done((bf16[4,128,512]{2,1,0:T(8,128)(2,1)S(1)}, bf16[4,128,512]{2,1,0:T(8,128)(2,1)S(1)}, u32[]{:S(2)}, u32[]{:S(2)}) %collective-permute-start.31) | collective-permute-done | bytes 524320 | tf_op jit(solution)/shard_map/ppermute | solution.py:84
  151.6 5.7 %attend_back.2.one = bf16[3,1024,128]{2,1,0:T(8,128)(2,1)S(1)} custom-call(bf16[3,1024,256]{2,1,0:T(8,128)(2,1)S(1)} %get-tuple-element.140.proj.query, bf16[1024,256]{1,0:T(8,128)(2,1)S(1)} %get-tuple-element.200.gmix, f32[8,1024]{1,0:T(8,128)S(1)} %get-tuple-element.196.log_sums, f32[8,1024]{1,0:T(8,128)S(1)} %get-tuple-element.197.inner, ...), custom_call_target="tpu_custom_call" | custom-call | flops 1610612736 | bytes 3932160 | tf_op jit(solution)/shard_map/attend_back/pallas_call | solution.py:428
  158.8 5.7 %attend_back.3.two = bf16[3,1024,128]{2,1,0:T(8,128)(2,1)S(1)} custom-call(bf16[3,1024,256]{2,1,0:T(8,128)(2,1)S(1)} %get-tuple-element.140.proj.query, bf16[1024,256]{1,0:T(8,128)(2,1)S(1)} %get-tuple-element.200.gmix, f32[8,1024]{1,0:T(8,128)S(1)} %get-tuple-element.196.log_sums, f32[8,1024]{1,0:T(8,128)S(1)} %get-tuple-element.197.inner, ...), custom_call_target="tpu_custom_call" | custom-call | flops 1610612736 | bytes 3932160 | tf_op jit(solution)/shard_map/attend_back/pallas_call | solution.py:428
  168.0 2.2 %collective-permute-done.37 = f32[2,16,256]{2,1,0:T(8,128)S(1)} collective-permute-done((f32[2,16,256]{2,1,0:T(8,128)S(1)}, f32[2,16,256]{2,1,0:T(8,128)S(1)}, u32[]{:S(2)}, u32[]{:S(2)}) %collective-permute-start.37) | collective-permute-done | bytes 32800 | tf_op jit(solution)/shard_map/ppermute | solution.py:84
  176.6 9.7 %collective-permute-done.39.side = bf16[256,1024]{1,0:T(8,128)(2,1)S(1)} collective-permute-done((bf16[256,1024]{1,0:T(8,128)(2,1)S(1)}, bf16[256,1024]{1,0:T(8,128)(2,1)S(1)}, u32[]{:S(2)}, u32[]{:S(2)}) %collective-permute-start.39) | collective-permute-done | bytes 524320 | tf_op jit(solution)/shard_map/ppermute | solution.py:84
  188.2 2.7 %update.1 = (f32[1,1]{1,0:T(1,128)}, f32[10,1024]{1,0:T(8,128)}, f32[10,1024]{1,0:T(8,128)}, f32[10,1024]{1,0:T(8,128)}, f32[128,512]{1,0:T(8,128)}, /*index=5*/...) custom-call(f32[16,512]{1,0:T(8,128)S(1)} %add.54.joint, ...), custom_call_target="tpu_custom_call" | custom-call | tf_op jit(solution)/shard_map/update/pallas_call | solution.py:982
  (162 shorter events, 72.7 us)
Async XLA Ops:
  2.8 16.2 %collective-permute-start = (bf16[512,256]{1,0:T(8,128)(2,1)S(1)}, bf16[512,256]{1,0:T(8,128)(2,1)}, u32[]{:S(2)}, u32[]{:S(2)}) collective-permute-start(bf16[512,256]{1,0:T(8,128)(2,1)S(1)} %get-tuple-element.225), channel_id=1, source_target_pairs={{0,16},{4,20},{8,24},{12,28},{16,0},{20,4},{24,8},{28,12},{1,17},{... | collective-permute-start | bytes 786440 | tf_op jit(solution)/shard_map/ppermute | solution.py:84
  20.0 16.7 %collective-permute-start.3 = (bf16[2,512,256]{2,1,0:T(8,128)(2,1)S(1)}, bf16[2,512,256]{2,1,0:T(8,128)(2,1)S(1)}, u32[]{:S(2)}, u32[]{:S(2)}) collective-permute-start(bf16[2,512,256]{2,1,0:T(8,128)(2,1)S(1)} %pad_maximum_fusion.1.refs_0_), channel_id=1, source_target_pairs={{0,8},{4,12},{8,0},{12,4},{16,24},{20,28},{24,16},{28,20},{1,9},{5... | collective-permute-start | bytes 1572872 | tf_op jit(solution)/shard_map/ppermute | solution.py:84
  20.7 17.3 %collective-permute-start.6 = (bf16[2,160,256]{2,1,0:T(8,128)(2,1)S(1)}, bf16[2,160,256]{2,1,0:T(8,128)(2,1)S(1)}, u32[]{:S(2)}, u32[]{:S(2)}) collective-permute-start(bf16[2,160,256]{2,1,0:T(8,128)(2,1)S(1)} %pad_maximum_fusion.10), channel_id=1, source_target_pairs={{0,16},{4,20},{8,24},{12,28},{16,0},{20,4},{24,8},{28,12},{1,17},{... | collective-permute-start | bytes 491528 | tf_op jit(solution)/shard_map/ppermute | solution.py:84
  24.2 18.9 %collective-permute-start.4 = (bf16[2,512,256]{2,1,0:T(8,128)(2,1)S(1)}, bf16[2,512,256]{2,1,0:T(8,128)(2,1)S(1)}, u32[]{:S(2)}, u32[]{:S(2)}) collective-permute-start(bf16[2,512,256]{2,1,0:T(8,128)(2,1)S(1)} %pad_maximum_fusion.1.refs_0_), channel_id=1, source_target_pairs={{0,4},{4,0},{8,12},{12,8},{16,20},{20,16},{24,28},{28,24},{1,5},{5... | collective-permute-start | bytes 1572872 | tf_op jit(solution)/shard_map/ppermute | solution.py:84
  38.0 14.8 %collective-permute-start.7 = (bf16[4,160,256]{2,1,0:T(8,128)(2,1)S(1)}, bf16[4,160,256]{2,1,0:T(8,128)(2,1)S(1)}, u32[]{:S(2)}, u32[]{:S(2)}) collective-permute-start(bf16[4,160,256]{2,1,0:T(8,128)(2,1)S(1)} %pad_maximum_fusion.7.refs_0_), channel_id=1, source_target_pairs={{0,8},{4,12},{8,0},{12,4},{16,24},{20,28},{24,16},{28,20},{1,9},{5... | collective-permute-start | bytes 983048 | tf_op jit(solution)/shard_map/ppermute | solution.py:84
  39.9 12.9 %collective-permute-start.8 = (bf16[128,1024]{1,0:T(8,128)(2,1)S(1)}, bf16[128,1024]{1,0:T(8,128)(2,1)S(1)}, u32[]{:S(2)}, u32[]{:S(2)}) collective-permute-start(bf16[128,1024]{1,0:T(8,128)(2,1)S(1)} %copy-done.22), channel_id=1, source_target_pairs={{0,16},{4,20},{8,24},{12,28},{16,0},{20,4},{24,8},{28,12},{1,17},{... | collective-permute-start | bytes 786440 | tf_op jit(solution)/shard_map/ppermute | solution.py:84
  54.4 13.1 %collective-permute-start.13 = (bf16[128,1024]{1,0:T(8,128)(2,1)S(1)}, bf16[128,1024]{1,0:T(8,128)(2,1)S(1)}, u32[]{:S(2)}, u32[]{:S(2)}) collective-permute-start(bf16[128,1024]{1,0:T(8,128)(2,1)S(1)} %copy-done.3), channel_id=1, source_target_pairs={{0,16},{4,20},{8,24},{12,28},{16,0},{20,4},{24,8},{28,12},{1,17},{... | collective-permute-start | bytes 786440 | tf_op jit(solution)/shard_map/ppermute | solution.py:84
  57.1 19.3 %collective-permute-start.10 = (bf16[2,128,1024]{2,1,0:T(8,128)(2,1)S(1)}, bf16[2,128,1024]{2,1,0:T(8,128)(2,1)S(1)}, u32[]{:S(2)}, u32[]{:S(2)}) collective-permute-start(bf16[2,128,1024]{2,1,0:T(8,128)(2,1)S(1)} %pad_maximum_fusion.2.refs_0_), channel_id=1, source_target_pairs={{0,8},{4,12},{8,0},{12,4},{16,24},{20,28},{24,16},{28,20},{1,9},{5... | collective-permute-start | bytes 1572872 | tf_op jit(solution)/shard_map/ppermute | solution.py:84
  59.0 17.4 %collective-permute-start.11 = (bf16[2,128,1024]{2,1,0:T(8,128)(2,1)S(1)}, bf16[2,128,1024]{2,1,0:T(8,128)(2,1)S(1)}, u32[]{:S(2)}, u32[]{:S(2)}) collective-permute-start(bf16[2,128,1024]{2,1,0:T(8,128)(2,1)S(1)} %pad_maximum_fusion.2.refs_0_), channel_id=1, source_target_pairs={{0,4},{4,0},{8,12},{12,8},{16,20},{20,16},{24,28},{28,24},{1,5},{5... | collective-permute-start | bytes 1572872 | tf_op jit(solution)/shard_map/ppermute | solution.py:84
  67.6 23.9 %collective-permute-start.17 = (bf16[2,1024,256]{2,1,0:T(8,128)(2,1)S(1)}, bf16[2,1024,256]{2,1,0:T(8,128)(2,1)S(1)}, u32[]{:S(2)}, u32[]{:S(2)}) collective-permute-start(bf16[2,1024,256]{2,1,0:T(8,128)(2,1)S(1)} %pad_maximum_fusion), channel_id=1, source_target_pairs={{0,1},{1,0},{2,3},{3,2},{4,5},{5,4},{6,7},{7,6},{8,9},{9,8},{10,11... | collective-permute-start | bytes 3145736 | tf_op jit(solution)/shard_map/ppermute | solution.py:84
  76.4 13.5 %collective-permute-start.14 = (bf16[2,128,1024]{2,1,0:T(8,128)(2,1)S(1)}, bf16[2,128,1024]{2,1,0:T(8,128)(2,1)S(1)}, u32[]{:S(2)}, u32[]{:S(2)}) collective-permute-start(bf16[2,128,1024]{2,1,0:T(8,128)(2,1)S(1)} %collective-permute-done.10.refs_2_), channel_id=1, source_target_pairs={{0,4},{4,0},{8,12},{12,8},{16,20},{20,16},{24,28},{28,24},{1,5},{5... | collective-permute-start | bytes 1572872 | tf_op jit(solution)/shard_map/ppermute | solution.py:84
  78.3 13.2 %collective-permute-start.15 = (bf16[2,128,1024]{2,1,0:T(8,128)(2,1)S(1)}, bf16[2,128,1024]{2,1,0:T(8,128)(2,1)S(1)}, u32[]{:S(2)}, u32[]{:S(2)}) collective-permute-start(bf16[2,128,1024]{2,1,0:T(8,128)(2,1)S(1)} %pad_maximum_fusion.3), channel_id=1, source_target_pairs={{0,8},{4,12},{8,0},{12,4},{16,24},{20,28},{24,16},{28,20},{1,9},{5... | collective-permute-start | bytes 1572872 | tf_op jit(solution)/shard_map/ppermute | solution.py:84
  94.7 20.0 %collective-permute-start.20 = (bf16[2,512,256]{2,1,0:T(8,128)(2,1)S(1)}, bf16[2,512,256]{2,1,0:T(8,128)(2,1)S(1)}, u32[]{:S(2)}, u32[]{:S(2)}) collective-permute-start(bf16[2,512,256]{2,1,0:T(8,128)(2,1)S(1)} %pad_maximum_fusion.5), channel_id=1, source_target_pairs={{0,1},{1,0},{2,3},{3,2},{4,5},{5,4},{6,7},{7,6},{8,9},{9,8},{10,11... | collective-permute-start | bytes 1572872 | tf_op jit(solution)/shard_map/ppermute | solution.py:84
  94.8 22.4 %collective-permute-start.22 = (bf16[2,128,1024]{2,1,0:T(8,128)(2,1)S(1)}, bf16[2,128,1024]{2,1,0:T(8,128)(2,1)S(1)}, u32[]{:S(2)}, u32[]{:S(2)}) collective-permute-start(bf16[2,128,1024]{2,1,0:T(8,128)(2,1)S(1)} %collective-permute-done.15.refs_4_), channel_id=1, source_target_pairs={{0,4},{4,0},{8,12},{12,8},{16,20},{20,16},{24,28},{28,24},{1,5},{5... | collective-permute-start | bytes 1572872 | tf_op jit(solution)/shard_map/ppermute | solution.py:84
  95.4 19.4 %collective-permute-start.18 = (bf16[1,128,1024]{2,1,0:T(8,128)(2,1)S(1)}, bf16[1,128,1024]{2,1,0:T(8,128)(2,1)S(1)}, u32[]{:S(2)}, u32[]{:S(2)}) collective-permute-start(bf16[1,128,1024]{2,1,0:T(8,128)(2,1)S(1)} %bitcast.77), channel_id=1, source_target_pairs={{0,4},{4,0},{8,12},{12,8},{16,20},{20,16},{24,28},{28,24},{1,5},{5... | collective-permute-start | bytes 786440 | tf_op jit(solution)/shard_map/ppermute | solution.py:84
  96.9 20.3 %collective-permute-start.21 = (bf16[128,512]{1,0:T(8,128)(2,1)S(1)}, bf16[128,512]{1,0:T(8,128)(2,1)S(1)}, u32[]{:S(2)}, u32[]{:S(2)}) collective-permute-start(bf16[128,512]{1,0:T(8,128)(2,1)S(1)} %convert_element_type.48), channel_id=1, source_target_pairs={{0,16},{4,20},{8,24},{12,28},{16,0},{20,4},{24,8},{28,12},{1,17},{... | collective-permute-start | bytes 393224 | tf_op jit(solution)/shard_map/ppermute | solution.py:84
  123.0 14.0 %collective-permute-start.24 = (bf16[256,1024]{1,0:T(8,128)(2,1)S(1)}, bf16[256,1024]{1,0:T(8,128)(2,1)S(1)}, u32[]{:S(2)}, u32[]{:S(2)}) collective-permute-start(bf16[256,1024]{1,0:T(8,128)(2,1)S(1)} %get-tuple-element.165), channel_id=1, source_target_pairs={{0,2},{1,3},{2,0},{3,1},{4,6},{5,7},{6,4},{7,5},{8,10},{9,11},{10,... | collective-permute-start | bytes 1572872 | tf_op jit(solution)/shard_map/ppermute | solution.py:84
  129.8 15.1 %collective-permute-start.28 = (bf16[256,1024]{1,0:T(8,128)(2,1)S(1)}, bf16[256,1024]{1,0:T(8,128)(2,1)S(1)}, u32[]{:S(2)}, u32[]{:S(2)}) collective-permute-start(bf16[256,1024]{1,0:T(8,128)(2,1)S(1)} %fusion.8), channel_id=1, source_target_pairs={{0,1},{1,0},{2,3},{3,2},{4,5},{5,4},{6,7},{7,6},{8,9},{9,8},{10,11... | collective-permute-start | bytes 1572872 | tf_op jit(solution)/shard_map/ppermute | solution.py:84
  131.9 12.9 %collective-permute-start.31 = (bf16[4,128,512]{2,1,0:T(8,128)(2,1)S(1)}, bf16[4,128,512]{2,1,0:T(8,128)(2,1)S(1)}, u32[]{:S(2)}, u32[]{:S(2)}) collective-permute-start(bf16[4,128,512]{2,1,0:T(8,128)(2,1)S(1)} %pad_maximum_fusion.6.refs_0_), channel_id=1, source_target_pairs={{0,4},{4,0},{8,12},{12,8},{16,20},{20,16},{24,28},{28,24},{1,5},{5... | collective-permute-start | bytes 1572872 | tf_op jit(solution)/shard_map/ppermute | solution.py:84
  147.6 16.9 %collective-permute-start.29 = (bf16[256,1024]{1,0:T(8,128)(2,1)S(1)}, bf16[256,1024]{1,0:T(8,128)(2,1)S(1)}, u32[]{:S(2)}, u32[]{:S(2)}) collective-permute-start(bf16[256,1024]{1,0:T(8,128)(2,1)S(1)} %add_convert_fusion.1), channel_id=1, source_target_pairs={{0,2},{1,3},{2,0},{3,1},{4,6},{5,7},{6,4},{7,5},{8,10},{9,11},{10,... | collective-permute-start | bytes 1572872 | tf_op jit(solution)/shard_map/ppermute | solution.py:84
  148.3 16.3 %collective-permute-start.26 = (bf16[256,1024]{1,0:T(8,128)(2,1)S(1)}, bf16[256,1024]{1,0:T(8,128)(2,1)S(1)}, u32[]{:S(2)}, u32[]{:S(2)}) collective-permute-start(bf16[256,1024]{1,0:T(8,128)(2,1)S(1)} %fusion.14), channel_id=1, source_target_pairs={{0,1},{1,0},{2,3},{3,2},{4,5},{5,4},{6,7},{7,6},{8,9},{9,8},{10,11... | collective-permute-start | bytes 1572872 | tf_op jit(solution)/shard_map/ppermute | solution.py:84
  171.5 14.8 %collective-permute-start.38 = (bf16[512,1024]{1,0:T(8,128)(2,1)S(1)}, bf16[512,1024]{1,0:T(8,128)(2,1)S(1)}, u32[]{:S(2)}, u32[]{:S(2)}) collective-permute-start(bf16[512,1024]{1,0:T(8,128)(2,1)S(1)} %project_back.5.own), channel_id=1, source_target_pairs={{0,1},{1,0},{2,3},{3,2},{4,5},{5,4},{6,7},{7,6},{8,9},{9,8},{10,11... | collective-permute-start | bytes 3145736 | tf_op jit(solution)/shard_map/ppermute | solution.py:84
  171.6 14.7 %collective-permute-start.39 = (bf16[256,1024]{1,0:T(8,128)(2,1)S(1)}, bf16[256,1024]{1,0:T(8,128)(2,1)S(1)}, u32[]{:S(2)}, u32[]{:S(2)}) collective-permute-start(bf16[256,1024]{1,0:T(8,128)(2,1)S(1)} %project_back.4), channel_id=1, source_target_pairs={{0,2},{1,3},{2,0},{3,1},{4,6},{5,7},{6,4},{7,5},{8,10},{9,11},{10,... | collective-permute-start | bytes 1572872 | tf_op jit(solution)/shard_map/ppermute | solution.py:84
  174.3 13.8 %collective-permute-start.41 = (f32[16,512]{1,0:T(8,128)S(1)}, f32[16,512]{1,0:T(8,128)S(1)}, u32[]{:S(2)}, u32[]{:S(2)}) collective-permute-start(f32[16,512]{1,0:T(8,128)S(1)} %add.53), channel_id=1, source_target_pairs={{0,2},{1,3},{2,0},{3,1},{4,6},{5,7},{6,4},{7,5},{8,10},{9,11},{10,... | collective-permute-start | bytes 98312 | tf_op jit(solution)/shard_map/ppermute | solution.py:84
  (41 other events, 446.9 us)

commit v3 on v2

--- a/solution.py
+++ b/solution.py
@@ -262,7 +262,7 @@
             sums[there, :] = jnp.where(sum_col == head, top + jnp.log(total), sums[there, :])
         return carry
 
-    lax.fori_loop(0, width // HD, one_head, 0)
+    lax.fori_loop(0, width // HD, one_head, 0, unroll=2 if first else 1)
     mix[...] = mixed[...].astype(jnp.bfloat16)
 
 
@@ -449,15 +449,10 @@
     )(proj, gmix, log_sums, inner, gquery)
 
 
-def four(refs):
-    own, side, other = refs
-    return own, other.at[0], side, other.at[1]
-
-
 def merge_kernel(first, tokens, norms, branch, *refs):
-    mixes, merges, earlier, (normed, resid_own) = refs[:3], refs[3:6], refs[6:-2], refs[-2:]
+    mixes, merges, earlier, (normed, resid_own) = refs[:4], refs[4:8], refs[8:-2], refs[-2:]
     i = pl.program_id(0)
-    merged = sum(dot(m[...], w[...], NT) for m, w in zip(four(mixes), four(merges), strict=True))
+    merged = sum(dot(m[...], w[...], NT) for m, w in zip(mixes, merges, strict=True))
     resid = tokens[...].astype(jnp.float32) + merged + branch[0:1, :]
     unit, _ = norm_parts(resid)
     normed[...] = (unit * norms[2:3, :] + norms[3:4, :]).astype(jnp.bfloat16)
@@ -472,11 +467,19 @@
         resid_own[...] = resid
 
 
+def part_spec(shape, first):
+    return pl.BlockSpec(shape, lambda i: (first // shape[0] + i, 0))
+
+
+def fixed_spec(shape, first):
+    return pl.BlockSpec(shape, lambda i: (first // shape[0], 0))
+
+
 def merge_half(tokens, norms, branch, mixes, merges, earlier=()):
     rows, width = tokens.shape
     share = rows // lax.axis_size("tensor")
-    local = mixes[0].shape[1]
-    steps = mixes[0].shape[0] // share
+    local = mixes[0][0].shape[1]
+    steps = rows // 2 // share
     first = steps if earlier else 0
     whole = lambda a: pl.BlockSpec(a.shape, lambda i: (0,) * a.ndim)
     outs = (shaped((rows, width), jnp.bfloat16), shaped((share, width), jnp.float32))
@@ -484,20 +487,19 @@
         functools.partial(merge_kernel, first),
         grid=(steps,),
         in_specs=[pl.BlockSpec((share, width), lambda i: (i + first, 0)), whole(norms), whole(branch)]
-        + [pl.BlockSpec((share, local), lambda i: (i, 0))] * 2
-        + [pl.BlockSpec((2, share, local), lambda i: (0, i, 0))]
-        + [whole(w) for w in merges]
+        + [part_spec((share, local), start) for _, start in mixes]
+        + [fixed_spec((width, local), start) for _, start in merges]
         + ([pl.BlockSpec(memory_space=pl.ANY), whole(earlier[1])] if earlier else []),
         out_specs=(
             pl.BlockSpec((share, width), lambda i: (i + first, 0)),
             pl.BlockSpec((share, width), lambda i: (0, 0)),
         ),
         out_shape=outs,
-        input_output_aliases={9: 0} if earlier else {},
+        input_output_aliases={11: 0} if earlier else {},
         compiler_params=limited(),
         name="merge_second" if earlier else "merge_first",
         cost_estimate=brief(),
-    )(tokens, norms, branch, *mixes, *merges, *earlier)
+    )(tokens, norms, branch, *[a for a, _ in (*mixes, *merges)], *earlier)
 
 
 def feed_rows(normed, ghidden, up, bias, act, part, plus=None):
@@ -619,7 +621,7 @@
 
 
 def middle_kernel(own, core, side, cotangent, resid, norms, *refs):
-    merges, (gresid, keep, send) = four(refs[:3]), refs[3:]
+    merges, (gresid, keep, send) = refs[:4], refs[4:]
     total = three(own, core, side)
     grad = cotangent[...].astype(jnp.float32) + norm_back(resid[...], norms[2:3, :], total)
     gresid[...] = grad
@@ -636,7 +638,7 @@
 
 def middle(own, core, side, cotangent, resid, norms, merges):
     share, width = resid.shape
-    local = merges[0].shape[1]
+    local = merges[0][0].shape[1]
     outs = (
         shaped((share, width), jnp.float32),
         shaped((2, share, local), jnp.bfloat16),
@@ -647,13 +649,14 @@
         middle_kernel,
         grid=(1,),
         in_specs=[whole_spec(own), whole_spec(core), whole_spec(side), mine]
-        + [whole_spec(a) for a in (resid, norms, *merges)],
+        + [whole_spec(a) for a in (resid, norms)]
+        + [fixed_spec((width, local), start) for _, start in merges],
         out_specs=[whole_spec(o) for o in outs],
         out_shape=outs,
         compiler_params=limited(),
         name="middle",
         cost_estimate=brief(),
-    )(own, core, side, cotangent, resid, norms, *merges)
+    )(own, core, side, cotangent, resid, norms, *[a for a, _ in merges])
 
 
 def last_kernel(own, core, side, tokens, gresid, norms, out):
@@ -684,7 +687,36 @@
     )(own, core, side, tokens, gresid, norms)
 
 
-def tail_kernel(total, hidden, decoder, joint):
+def plus_kernel(one, two, out):
+    out[...] = one[...] + two[...]
+
+
+def plus(one, two):
+    return pl.pallas_call(
+        plus_kernel,
+        out_shape=shaped(one.shape, one.dtype),
+        compiler_params=limited(),
+        name="plus",
+        cost_estimate=brief(),
+    )(one, two)
+
+
+def output_kernel(resid, own, core, side, branch, out):
+    out[...] = (resid[...] + three(own, core, side) + branch[1:2, :]).astype(jnp.bfloat16)
+
+
+def output_rows(resid, own, core, side, branch):
+    return pl.pallas_call(
+        output_kernel,
+        out_shape=shaped(resid.shape, jnp.bfloat16),
+        compiler_params=limited(),
+        name="output",
+        cost_estimate=brief(),
+    )(resid, own, core, side, branch)
+
+
+def tail_kernel(one, two, hidden, decoder, total, joint):
+    total[...] = one[...] + two[...]
     low = total[...].astype(jnp.bfloat16)
     held = hidden[...].astype(jnp.bfloat16)
     part = jnp.zeros(joint.shape, jnp.float32)
@@ -699,12 +731,13 @@
     joint[...] = jnp.where(row == PAD - 1, square, part)
 
 
-def update_kernel(joint, hidden, hidden_own, total, selected, selected_own, onehot, encoder, *refs):
+def update_kernel(joint_one, joint_two, hidden, hidden_own, total, selected, selected_own, onehot, encoder, *refs):
     table, enc, enc_bias, dec, dec_bias = (refs[i : i + 3] for i in range(0, 15, 3))
     norm_out, outs = refs[15], refs[16:]
     held = hidden[...]
     row = lax.broadcasted_iota(jnp.int32, held.shape, 0)
-    grad = jnp.where(row < PRE, joint[...], 0.0) * (1.0 - held * held)
+    joint = joint_one[...] + joint_two[...]
+    grad = jnp.where(row < PRE, joint, 0.0) * (1.0 - held * held)
     grad = grad.astype(jnp.bfloat16)
     square = joint[PAD - 1 : PAD, 0:1]
 
@@ -839,19 +872,25 @@
         projected, encoded, encoder_bias[None], decoder_full, decoder_bias
     )
 
-    def from_others(values, side):
-        return values, side, swap(jnp.stack([values, side]), "tensor", CORE)
-
     merge_side = after(swap(merge_own, "tensor", SIDE), mix_first)
     if small:
-        merge_side, up_far = after((merge_side, up_far))
-    merges = from_others(merge_own, merge_side)
-    mixes_first = from_others(mix_first, swap(mix_first, "tensor", SIDE))
-    proj_late = after(projected, mixes_first[1])
-    if small:
-        proj_late, down_near, down_pair_side, up_far = after(
-            (proj_late, down_near, down_pair_side, up_far)
+        merge_side, up_far, down_near, down_pair_side = after(
+            (merge_side, up_far, down_near, down_pair_side)
         )
+    mix_side = swap(mix_first, "tensor", SIDE)
+    half = rows // 2
+    both_cores = joined(merge_own, merge_side, mix_first, mix_side)
+    both_cores = swap(both_cores, "tensor", CORE)
+    merges = ((merge_own, 0), (both_cores, 0), (merge_side, 0), (both_cores, width))
+    mixes_first = (
+        (mix_first, 0),
+        (both_cores, 2 * width),
+        (mix_side, 0),
+        (both_cores, 2 * width + half),
+    )
+    proj_late = projected
+    if small:
+        proj_late = after(projected, down_near)
         down_near_side = swap(down_near, "dp", y)
         up_near = swap(joined(up_weight[None], up_far), "dp", z)
         up_far_side = swap(up_far, "dp", y)
@@ -866,12 +905,15 @@
         )
         up_near_side = swap(up_near, "dp", y)
     first_half = merge_half(tokens, norm_params, branch_late, mixes_first, merges)
-    mixes_second = from_others(mix_second, after(mix_side, first_half))
+    mix_side = after(mix_side, first_half)
+    if small:
+        mix_side, up_far_side = after((mix_side, up_far_side))
+    mix_cores = swap(joined(mix_second, mix_side), "tensor", CORE)
+    mixes_second = ((mix_second, 0), (mix_cores, 0), (mix_side, 0), (mix_cores, half))
     down_full, grad_hidden = down_back(after(cotangent, first_half), down)
     branch_late = after(branch_bias, grad_hidden)
     if small:
         encoder_far = swap(after(encoder_low, first_half), "dp", far)
-        branch_late, up_far_side = after((branch_late, up_far_side))
         up = (
             (up_weight[None], up_side, up_far, up_far_side, up_near, up_near_side),
             ((0,), (1,), (4,), (5,), (2, 6), (3, 7)),
@@ -935,41 +977,38 @@
         (keep, from_side, core_keep, core_side),
     )
     grad_first = attend_back(0, projected, grad_mix, log_sums, inner, grad_query)
-    prefix_total = grad_prefix + swap(grad_prefix, "dp", 1)
+    prefix_total = plus(grad_prefix, swap(grad_prefix, "dp", 1))
     grad_second = attend_back(
         1, projected, after(grad_mix, prefix_total), log_sums, inner, grad_query
     )
-    prefix_total = prefix_total + swap(prefix_total, "dp", 2)
+    prefix_total = plus(prefix_total, swap(prefix_total, "dp", 2))
     gprojs = after((grad_first, grad_second), prefix_total, out_from, out_core)
     back_both = swap(project_back((BOTH,), gprojs, attend_full), "tensor", CORE)
+    back_rest = project_back((CORE, OWN), gprojs, attend_full)
+    back_both = after(back_both, back_rest)
     back_send = project_back((SIDE,), gprojs, attend_full, back_both)
     back_from = swap(back_send, "tensor", SIDE)
     bits = 4
-    while bits < lax.axis_size("dp"):
-        prefix_total = prefix_total + after(swap(prefix_total, "dp", bits), back_send)
+    while bits < lax.axis_size("dp") // 2:
+        prefix_total = plus(prefix_total, swap(prefix_total, "dp", bits))
         bits *= 2
-    joint = pl.pallas_call(
+    prefix_rest = after(swap(prefix_total, "dp", bits), back_send)
+    prefix_total, joint = pl.pallas_call(
         tail_kernel,
-        out_shape=shaped((PAD, hidden_size), jnp.float32),
+        out_shape=(
+            shaped(grad_prefix.shape, jnp.float32),
+            shaped((PAD, hidden_size), jnp.float32),
+        ),
         compiler_params=limited(),
         name="tail",
         cost_estimate=brief(),
-    )(prefix_total, hidden, decoder_full)
-    joint = joint + swap(joint, "tensor", CORE)
-    back_rest = project_back((CORE, OWN), after(gprojs, back_send, prefix_total), attend_full)
+    )(prefix_total, prefix_rest, hidden, decoder_full)
+    joint = plus(joint, swap(joint, "tensor", CORE))
     joint_side = swap(joint, "tensor", SIDE)
     back_core = swap(back_rest, "tensor", CORE)
-    output = (
-        resid
-        + (
-            out_own.astype(jnp.float32)
-            + out_core.astype(jnp.float32)
-            + out_from.astype(jnp.float32)
-        )
-        + branch_bias[1]
-    )
+    output = output_rows(resid, out_own, out_core, out_from, branch_bias)
     input_grad = last(back_rest, back_core, back_from, tokens, grad_resid, norm_params)
-    joint = joint + after(joint_side, input_grad)
+    joint_side = after(joint_side, input_grad)
 
     params = [
         (prefix_table, first_table, second_table),
@@ -986,6 +1025,7 @@
         name="update",
     )(
         joint,
+        joint_side,
         hidden,
         hidden_own,
         prefix_total,
@@ -997,7 +1037,7 @@
     )
     for i in range(6, 9):
         new[i] = new[i][0]
-    return (output.astype(jnp.bfloat16), input_grad, grad_norm[0, 0], *new)
+    return (output, input_grad, grad_norm[0, 0], *new)
 
 
 def solution(mesh):

time: 191 us -> 179 us (0.937)
  waiting for transfers between devices: 78.8 us -> 66.6 us
    ppermute x42 -> x41, waiting for transfers between devices: 78.8 us -> 66.6 us  [swap(): return lax.ppermute(values, axis, [(i, i ^ bits) for i in range(size)])]
    ppermute x42 -> x41, starting transfers between devices: 47.1 us -> 48.5 us  [swap(): return lax.ppermute(values, axis, [(i, i ^ bits) for i in range(size)])]
  transfers between devices with their start and end apart: 42 -> 41, of which waited for: 21 -> 20; matrix products, arithmetic and copies ran while one was open for 5% -> 4% of each run, Pallas kernels for 22% -> 26%
where the time goes in v3:
time: 179 us
  waiting for transfers between devices  66.6 us (37%)
  Pallas kernels  51.2 us (29%)
  starting transfers between devices  48.5 us (27%)
  other arithmetic  5.99 us (3%)
  matrix products  4.1 us (2%)
    ppermute x41, waiting for transfers between devices, swap(): return lax.ppermute(values, axis, [(i, i ^ bits) for i in range(size)])  66.6 us
    ppermute x41, starting transfers between devices, swap(): return lax.ppermute(values, axis, [(i, i ^ bits) for i in range(size)])  48.5 us
    pallas_call x2, Pallas kernels, attend_back(): pl.pallas_call(functools.partial(attend_back_kernel, pair), grid=(1,), in...  11.4 us
    pallas_call x1, Pallas kernels, attend_second(): pl.pallas_call(functools.partial(attend_kernel, rows // 2), out_shape=out...  5.66 us
    pallas_call x3, Pallas kernels, feed(): pl.pallas_call(feed_kernel, grid=(1,), in_specs=[whole_spec(up), whole_sp...  5.48 us
    pallas_call x1, Pallas kernels, attend_first(): pl.pallas_call(attend_first_kernel, out_shape=outs, scratch_shapes=[pltpu...  4.9 us
    pallas_call x2, Pallas kernels, merge_half(): pl.pallas_call(functools.partial(merge_kernel, first), grid=(steps,), in_...  4.59 us
  transfers between devices with their start and end apart: 41, of which 20 were waited for; matrix products, arithmetic and copies ran while one was open for 4% of the time, Pallas kernels for 26%

profile of v3, /device:TPU:0, one launch (start us, length us, event | category | flops | bytes accessed | tf_op | source)
XLA Modules:
  0.0 178.7 jit_solution(4491325522013082419)
XLA Ops:
  2.8 4.1 %collective-permute-start.1 = (bf16[512,256]{1,0:T(8,128)(2,1)S(1)}, bf16[512,256]{1,0:T(8,128)(2,1)}, u32[]{:S(2)}, u32[]{:S(2)}) collective-permute-start(bf16[512,256]{1,0:T(8,128)(2,1)S(1)} %get-tuple-element.223), channel_id=1, source_target_pairs={{0,16},{4,20},{8,24},{12,28},{16,0},{20,4},{24,8},{28,12},{1,17},{... | collective-permute-start | bytes 786440 | tf_op jit(solution)/shard_map/ppermute | solution.py:84
  13.3 4.1 %collective-permute-done = bf16[160,256]{1,0:T(8,128)(2,1)S(1)} collective-permute-done((bf16[160,256]{1,0:T(8,128)(2,1)}, bf16[160,256]{1,0:T(8,128)(2,1)S(1)}, u32[]{:S(2)}, u32[]{:S(2)}) %collective-permute-start) | collective-permute-done | bytes 81952 | tf_op jit(solution)/shard_map/ppermute | solution.py:84
  20.7 3.6 %collective-permute-start.3 = (bf16[2,160,256]{2,1,0:T(8,128)(2,1)S(1)}, bf16[2,160,256]{2,1,0:T(8,128)(2,1)S(1)}, u32[]{:S(2)}, u32[]{:S(2)}) collective-permute-start(bf16[2,160,256]{2,1,0:T(8,128)(2,1)S(1)} %pad_maximum_fusion.9), channel_id=1, source_target_pairs={{0,16},{4,20},{8,24},{12,28},{16,0},{20,4},{24,8},{28,12},{1,17},{... | collective-permute-start | bytes 491528 | tf_op jit(solution)/shard_map/ppermute | solution.py:84
  25.7 10.9 %collective-permute-done.5.refs_1_ = bf16[2,512,256]{2,1,0:T(8,128)(2,1)S(1)} collective-permute-done((bf16[2,512,256]{2,1,0:T(8,128)(2,1)S(1)}, bf16[2,512,256]{2,1,0:T(8,128)(2,1)S(1)}, u32[]{:S(2)}, u32[]{:S(2)}) %collective-permute-start.5) | collective-permute-done | bytes 524320 | tf_op jit(solution)/shard_map/ppermute | solution.py:84
  39.9 3.3 %collective-permute-start.8 = (bf16[128,1024]{1,0:T(8,128)(2,1)S(1)}, bf16[128,1024]{1,0:T(8,128)(2,1)S(1)}, u32[]{:S(2)}, u32[]{:S(2)}) collective-permute-start(bf16[128,1024]{1,0:T(8,128)(2,1)S(1)} %copy-done.22), channel_id=1, source_target_pairs={{0,16},{4,20},{8,24},{12,28},{16,0},{20,4},{24,8},{28,12},{1,17},{... | collective-permute-start | bytes 786440 | tf_op jit(solution)/shard_map/ppermute | solution.py:84
  43.1 5.7 %collective-permute-done.7.refs_3_ = bf16[2,512,256]{2,1,0:T(8,128)(2,1)S(1)} collective-permute-done((bf16[2,512,256]{2,1,0:T(8,128)(2,1)S(1)}, bf16[2,512,256]{2,1,0:T(8,128)(2,1)S(1)}, u32[]{:S(2)}, u32[]{:S(2)}) %collective-permute-start.7) | collective-permute-done | bytes 524320 | tf_op jit(solution)/shard_map/ppermute | solution.py:84
  48.9 2.7 %project.1 = (bf16[3,1024,256]{2,1,0:T(8,128)(2,1)S(1)}, bf16[3,1024,256]{2,1,0:T(8,128)(2,1)S(1)}, bf16[2,512,256]{2,1,0:T(8,128)(2,1)S(1)}) custom-call(bf16[1024,1024]{1,0:T(8,128)(2,1)S(1)} %copy-done, f32[4,1024]{1,0:T(4,128)S(1)} %copy-done.5, f32[3,256]{1,0:T(4,128)S(1)} %copy-done.17, bf16[2,512,256]{2,1,0:T(8,128)(2,1)S(1)} %pad_maximum_fusion.1.refs_0_, ...), custom_call_target="tpu_custom_call" | custom-call | tf_op jit(solution)/shard_map/project/pallas_call | solution.py:187
  54.5 2.8 %collective-permute-start.11 = (bf16[2,128,1024]{2,1,0:T(8,128)(2,1)S(1)}, bf16[2,128,1024]{2,1,0:T(8,128)(2,1)S(1)}, u32[]{:S(2)}, u32[]{:S(2)}) collective-permute-start(bf16[2,128,1024]{2,1,0:T(8,128)(2,1)S(1)} %pad_maximum_fusion.2.refs_0_), channel_id=1, source_target_pairs={{0,8},{4,12},{8,0},{12,4},{16,24},{20,28},{24,16},{28,20},{1,9},{5... | collective-permute-start | bytes 1572872 | tf_op jit(solution)/shard_map/ppermute | solution.py:84
  57.8 2.7 %collective-permute-start.10 = (bf16[128,1024]{1,0:T(8,128)(2,1)S(1)}, bf16[128,1024]{1,0:T(8,128)(2,1)S(1)}, u32[]{:S(2)}, u32[]{:S(2)}) collective-permute-start(bf16[128,1024]{1,0:T(8,128)(2,1)S(1)} %copy-done.3), channel_id=1, source_target_pairs={{0,16},{4,20},{8,24},{12,28},{16,0},{20,4},{24,8},{28,12},{1,17},{... | collective-permute-start | bytes 786440 | tf_op jit(solution)/shard_map/ppermute | solution.py:84
  60.5 4.9 %attend_first.1 = (bf16[512,256]{1,0:T(8,128)(2,1)S(1)}, f32[512,128]{1,0:T(8,128)S(1)}, f32[16,512]{1,0:T(8,128)S(1)}, bf16[2,16,256]{2,1,0:T(8,128)(2,1)S(1)}) custom-call(bf16[3,1024,256]{2,1,0:T(8,128)(2,1)S(1)} %get-tuple-element.137.proj.query, f32[16,512]{1,0:T(8,128)S(1)} %get-tuple-element.130.encoded, f32[1,512]{1,0:T(1,128)S(1)} %bitcast.71, ...), custom_call_target="tpu_custom_call" | custom-call | tf_op jit(solution)/shard_map/attend_first/pallas_call | solution.py:286
  66.0 6.3 %collective-permute-done.10 = bf16[128,1024]{1,0:T(8,128)(2,1)S(1)} collective-permute-done((bf16[128,1024]{1,0:T(8,128)(2,1)S(1)}, bf16[128,1024]{1,0:T(8,128)(2,1)S(1)}, u32[]{:S(2)}, u32[]{:S(2)}) %collective-permute-start.10) | collective-permute-done | bytes 262176 | tf_op jit(solution)/shard_map/ppermute | solution.py:84
  76.9 5.7 %attend_second.1 = (bf16[512,256]{1,0:T(8,128)(2,1)S(1)}, f32[512,128]{1,0:T(8,128)S(1)}) custom-call(bf16[3,1024,256]{2,1,0:T(8,128)(2,1)S(1)} %get-tuple-element.137.proj.query, bf16[2,16,256]{2,1,0:T(8,128)(2,1)S(1)} %get-tuple-element.138.prefix), custom_call_target="tpu_custom_call" | custom-call | tf_op jit(solution)/shard_map/attend_second/pallas_call | solution.py:299
  84.1 3.9 %collective-permute-done.13.refs_3_ = bf16[2,128,1024]{2,1,0:T(8,128)(2,1)S(1)} collective-permute-done((bf16[2,128,1024]{2,1,0:T(8,128)(2,1)S(1)}, bf16[2,128,1024]{2,1,0:T(8,128)(2,1)S(1)}, u32[]{:S(2)}, u32[]{:S(2)}) %collective-permute-start.13) | collective-permute-done | bytes 524320 | tf_op jit(solution)/shard_map/ppermute | solution.py:84
  96.5 2.5 %down_back.1 = (bf16[1,1024,1024]{2,1,0:T(8,128)(2,1)S(1)}, bf16[1024,1024]{1,0:T(8,128)(2,1)S(1)}) custom-call(bf16[1024,1024]{1,0:T(8,128)(2,1)S(1)} %copy-done.1, bf16[2,128,1024]{2,1,0:T(8,128)(2,1)S(1)} %pad_maximum_fusion.2.refs_0_, bf16[2,128,1024]{2,1,0:T(8,128)(2,1)S(1)} %collective-permute-done.12.refs_1_, ...), custom_call_target="tpu_custom_call" | custom-call | tf_op jit(solution)/shard_map/down_back/pallas_call | solution.py:209
  103.7 3.9 %collective-permute-done.21.refs_5_ = bf16[2,128,1024]{2,1,0:T(8,128)(2,1)S(1)} collective-permute-done((bf16[2,128,1024]{2,1,0:T(8,128)(2,1)S(1)}, bf16[2,128,1024]{2,1,0:T(8,128)(2,1)S(1)}, u32[]{:S(2)}, u32[]{:S(2)}) %collective-permute-start.21) | collective-permute-done | bytes 524320 | tf_op jit(solution)/shard_map/ppermute | solution.py:84
  109.7 2.5 %collective-permute-start.24 = (bf16[2,128,512]{2,1,0:T(8,128)(2,1)S(1)}, bf16[2,128,512]{2,1,0:T(8,128)(2,1)S(1)}, u32[]{:S(2)}, u32[]{:S(2)}) collective-permute-start(bf16[2,128,512]{2,1,0:T(8,128)(2,1)S(1)} %pad_maximum_fusion.8), channel_id=1, source_target_pairs={{0,8},{4,12},{8,0},{12,4},{16,24},{20,28},{24,16},{28,20},{1,9},{5... | collective-permute-start | bytes 786440 | tf_op jit(solution)/shard_map/ppermute | solution.py:84
  121.7 6.5 %collective-permute-done.23.side = bf16[256,1024]{1,0:T(8,128)(2,1)S(1)} collective-permute-done((bf16[256,1024]{1,0:T(8,128)(2,1)S(1)}, bf16[256,1024]{1,0:T(8,128)(2,1)S(1)}, u32[]{:S(2)}, u32[]{:S(2)}) %collective-permute-start.23) | collective-permute-done | bytes 524320 | tf_op jit(solution)/shard_map/ppermute | solution.py:84
  131.8 2.8 %collective-permute-done.30.refs_1_ = bf16[4,128,512]{2,1,0:T(8,128)(2,1)S(1)} collective-permute-done((bf16[4,128,512]{2,1,0:T(8,128)(2,1)S(1)}, bf16[4,128,512]{2,1,0:T(8,128)(2,1)S(1)}, u32[]{:S(2)}, u32[]{:S(2)}) %collective-permute-start.30) | collective-permute-done | bytes 524320 | tf_op jit(solution)/shard_map/ppermute | solution.py:84
  135.5 3.3 %collective-permute-done.29.side = bf16[2,256,256]{2,1,0:T(8,128)(2,1)S(1)} collective-permute-done((bf16[2,256,256]{2,1,0:T(8,128)(2,1)S(1)}, bf16[2,256,256]{2,1,0:T(8,128)(2,1)S(1)}, u32[]{:S(2)}, u32[]{:S(2)}) %collective-permute-start.29) | collective-permute-done | bytes 262176 | tf_op jit(solution)/shard_map/ppermute | solution.py:84
  143.3 5.7 %attend_back.2.one = bf16[3,1024,128]{2,1,0:T(8,128)(2,1)S(1)} custom-call(bf16[3,1024,256]{2,1,0:T(8,128)(2,1)S(1)} %get-tuple-element.137.proj.query, bf16[1024,256]{1,0:T(8,128)(2,1)S(1)} %get-tuple-element.197.gmix, f32[8,1024]{1,0:T(8,128)S(1)} %get-tuple-element.193.log_sums, f32[8,1024]{1,0:T(8,128)S(1)} %get-tuple-element.194.inner, ...), custom_call_target="tpu_custom_call" | custom-call | flops 1610612736 | bytes 3932160 | tf_op jit(solution)/shard_map/attend_back/pallas_call | solution.py:428
  150.7 5.7 %attend_back.3.two = bf16[3,1024,128]{2,1,0:T(8,128)(2,1)S(1)} custom-call(bf16[3,1024,256]{2,1,0:T(8,128)(2,1)S(1)} %get-tuple-element.137.proj.query, bf16[1024,256]{1,0:T(8,128)(2,1)S(1)} %get-tuple-element.197.gmix, f32[8,1024]{1,0:T(8,128)S(1)} %get-tuple-element.193.log_sums, f32[8,1024]{1,0:T(8,128)S(1)} %get-tuple-element.194.inner, ...), custom_call_target="tpu_custom_call" | custom-call | flops 1610612736 | bytes 3932160 | tf_op jit(solution)/shard_map/attend_back/pallas_call | solution.py:428
  162.2 3.5 %collective-permute-done.38.two = f32[2,16,256]{2,1,0:T(8,128)S(1)} collective-permute-done((f32[2,16,256]{2,1,0:T(8,128)S(1)}, f32[2,16,256]{2,1,0:T(8,128)S(1)}, u32[]{:S(2)}, u32[]{:S(2)}) %collective-permute-start.38) | collective-permute-done | bytes 32800 | tf_op jit(solution)/shard_map/ppermute | solution.py:84
  169.6 4.4 %collective-permute-done.37.side = bf16[256,1024]{1,0:T(8,128)(2,1)S(1)} collective-permute-done((bf16[256,1024]{1,0:T(8,128)(2,1)S(1)}, bf16[256,1024]{1,0:T(8,128)(2,1)S(1)}, u32[]{:S(2)}, u32[]{:S(2)}) %collective-permute-start.37) | collective-permute-done | bytes 524320 | tf_op jit(solution)/shard_map/ppermute | solution.py:84
  175.9 2.6 %update.1 = (f32[1,1]{1,0:T(1,128)}, f32[10,1024]{1,0:T(8,128)}, f32[10,1024]{1,0:T(8,128)}, f32[10,1024]{1,0:T(8,128)}, f32[128,512]{1,0:T(8,128)}, /*index=5*/...) custom-call(f32[16,512]{1,0:T(8,128)S(1)} %plus.5.joint_one, ...), custom_call_target="tpu_custom_call" | custom-call | tf_op jit(solution)/shard_map/update/pallas_call | solution.py:1021
  (156 shorter events, 73.2 us)
Async XLA Ops:
  2.8 16.2 %collective-permute-start.1 = (bf16[512,256]{1,0:T(8,128)(2,1)S(1)}, bf16[512,256]{1,0:T(8,128)(2,1)}, u32[]{:S(2)}, u32[]{:S(2)}) collective-permute-start(bf16[512,256]{1,0:T(8,128)(2,1)S(1)} %get-tuple-element.223), channel_id=1, source_target_pairs={{0,16},{4,20},{8,24},{12,28},{16,0},{20,4},{24,8},{28,12},{1,17},{... | collective-permute-start | bytes 786440 | tf_op jit(solution)/shard_map/ppermute | solution.py:84
  6.9 12.0 %collective-permute-start.2 = (bf16[128,1024]{1,0:T(8,128)(2,1)}, bf16[128,1024]{1,0:T(8,128)(2,1)S(1)}, u32[]{:S(2)}, u32[]{:S(2)}) collective-permute-start(bf16[128,1024]{1,0:T(8,128)(2,1)} %param.33), channel_id=1, source_target_pairs={{0,4},{4,0},{8,12},{12,8},{16,20},{20,16},{24,28},{28,24},{1,5},{5... | collective-permute-start | bytes 786440 | tf_op jit(solution)/shard_map/ppermute | solution.py:84
  20.0 16.7 %collective-permute-start.5 = (bf16[2,512,256]{2,1,0:T(8,128)(2,1)S(1)}, bf16[2,512,256]{2,1,0:T(8,128)(2,1)S(1)}, u32[]{:S(2)}, u32[]{:S(2)}) collective-permute-start(bf16[2,512,256]{2,1,0:T(8,128)(2,1)S(1)} %pad_maximum_fusion.1.refs_0_), channel_id=1, source_target_pairs={{0,8},{4,12},{8,0},{12,4},{16,24},{20,28},{24,16},{28,20},{1,9},{5... | collective-permute-start | bytes 1572872 | tf_op jit(solution)/shard_map/ppermute | solution.py:84
  20.7 17.3 %collective-permute-start.3 = (bf16[2,160,256]{2,1,0:T(8,128)(2,1)S(1)}, bf16[2,160,256]{2,1,0:T(8,128)(2,1)S(1)}, u32[]{:S(2)}, u32[]{:S(2)}) collective-permute-start(bf16[2,160,256]{2,1,0:T(8,128)(2,1)S(1)} %pad_maximum_fusion.9), channel_id=1, source_target_pairs={{0,16},{4,20},{8,24},{12,28},{16,0},{20,4},{24,8},{28,12},{1,17},{... | collective-permute-start | bytes 491528 | tf_op jit(solution)/shard_map/ppermute | solution.py:84
  24.2 18.9 %collective-permute-start.6 = (bf16[2,512,256]{2,1,0:T(8,128)(2,1)S(1)}, bf16[2,512,256]{2,1,0:T(8,128)(2,1)S(1)}, u32[]{:S(2)}, u32[]{:S(2)}) collective-permute-start(bf16[2,512,256]{2,1,0:T(8,128)(2,1)S(1)} %pad_maximum_fusion.1.refs_0_), channel_id=1, source_target_pairs={{0,4},{4,0},{8,12},{12,8},{16,20},{20,16},{24,28},{28,24},{1,5},{5... | collective-permute-start | bytes 1572872 | tf_op jit(solution)/shard_map/ppermute | solution.py:84
  36.6 12.2 %collective-permute-start.7 = (bf16[2,512,256]{2,1,0:T(8,128)(2,1)S(1)}, bf16[2,512,256]{2,1,0:T(8,128)(2,1)S(1)}, u32[]{:S(2)}, u32[]{:S(2)}) collective-permute-start(bf16[2,512,256]{2,1,0:T(8,128)(2,1)S(1)} %collective-permute-done.5.refs_1_), channel_id=1, source_target_pairs={{0,4},{4,0},{8,12},{12,8},{16,20},{20,16},{24,28},{28,24},{1,5},{5... | collective-permute-start | bytes 1572872 | tf_op jit(solution)/shard_map/ppermute | solution.py:84
  38.0 14.8 %collective-permute-start.4 = (bf16[4,160,256]{2,1,0:T(8,128)(2,1)S(1)}, bf16[4,160,256]{2,1,0:T(8,128)(2,1)S(1)}, u32[]{:S(2)}, u32[]{:S(2)}) collective-permute-start(bf16[4,160,256]{2,1,0:T(8,128)(2,1)S(1)} %pad_maximum_fusion.6.refs_0_), channel_id=1, source_target_pairs={{0,8},{4,12},{8,0},{12,4},{16,24},{20,28},{24,16},{28,20},{1,9},{5... | collective-permute-start | bytes 983048 | tf_op jit(solution)/shard_map/ppermute | solution.py:84
  39.9 12.9 %collective-permute-start.8 = (bf16[128,1024]{1,0:T(8,128)(2,1)S(1)}, bf16[128,1024]{1,0:T(8,128)(2,1)S(1)}, u32[]{:S(2)}, u32[]{:S(2)}) collective-permute-start(bf16[128,1024]{1,0:T(8,128)(2,1)S(1)} %copy-done.22), channel_id=1, source_target_pairs={{0,16},{4,20},{8,24},{12,28},{16,0},{20,4},{24,8},{28,12},{1,17},{... | collective-permute-start | bytes 786440 | tf_op jit(solution)/shard_map/ppermute | solution.py:84
  52.9 13.1 %collective-permute-start.9 = (bf16[1024,256]{1,0:T(8,128)(2,1)S(1)}, bf16[1024,256]{1,0:T(8,128)(2,1)S(1)}, u32[]{:S(2)}, u32[]{:S(2)}) collective-permute-start(bf16[1024,256]{1,0:T(8,128)(2,1)S(1)} %get-tuple-element.129.refs_4_.refs_0_), channel_id=1, source_target_pairs={{0,2},{1,3},{2,0},{3,1},{4,6},{5,7},{6,4},{7,5},{8,10},{9,11},{10,... | collective-permute-start | bytes 1572872 | tf_op jit(solution)/shard_map/ppermute | solution.py:84
  54.5 18.5 %collective-permute-start.11 = (bf16[2,128,1024]{2,1,0:T(8,128)(2,1)S(1)}, bf16[2,128,1024]{2,1,0:T(8,128)(2,1)S(1)}, u32[]{:S(2)}, u32[]{:S(2)}) collective-permute-start(bf16[2,128,1024]{2,1,0:T(8,128)(2,1)S(1)} %pad_maximum_fusion.2.refs_0_), channel_id=1, source_target_pairs={{0,8},{4,12},{8,0},{12,4},{16,24},{20,28},{24,16},{28,20},{1,9},{5... | collective-permute-start | bytes 1572872 | tf_op jit(solution)/shard_map/ppermute | solution.py:84
  57.3 15.7 %collective-permute-start.12 = (bf16[2,128,1024]{2,1,0:T(8,128)(2,1)S(1)}, bf16[2,128,1024]{2,1,0:T(8,128)(2,1)S(1)}, u32[]{:S(2)}, u32[]{:S(2)}) collective-permute-start(bf16[2,128,1024]{2,1,0:T(8,128)(2,1)S(1)} %pad_maximum_fusion.2.refs_0_), channel_id=1, source_target_pairs={{0,4},{4,0},{8,12},{12,8},{16,20},{20,16},{24,28},{28,24},{1,5},{5... | collective-permute-start | bytes 1572872 | tf_op jit(solution)/shard_map/ppermute | solution.py:84
  57.8 14.5 %collective-permute-start.10 = (bf16[128,1024]{1,0:T(8,128)(2,1)S(1)}, bf16[128,1024]{1,0:T(8,128)(2,1)S(1)}, u32[]{:S(2)}, u32[]{:S(2)}) collective-permute-start(bf16[128,1024]{1,0:T(8,128)(2,1)S(1)} %copy-done.3), channel_id=1, source_target_pairs={{0,16},{4,20},{8,24},{12,28},{16,0},{20,4},{24,8},{28,12},{1,17},{... | collective-permute-start | bytes 786440 | tf_op jit(solution)/shard_map/ppermute | solution.py:84
  73.1 16.0 %collective-permute-start.16 = (bf16[3072,256]{1,0:T(8,128)(2,1)S(1)}, bf16[3072,256]{1,0:T(8,128)(2,1)S(1)}, u32[]{:S(2)}, u32[]{:S(2)}) collective-permute-start(bf16[3072,256]{1,0:T(8,128)(2,1)S(1)} %pad_maximum_fusion), channel_id=1, source_target_pairs={{0,1},{1,0},{2,3},{3,2},{4,5},{5,4},{6,7},{7,6},{8,9},{9,8},{10,11... | collective-permute-start | bytes 4718600 | tf_op jit(solution)/shard_map/ppermute | solution.py:84
  73.2 14.9 %collective-permute-start.13 = (bf16[2,128,1024]{2,1,0:T(8,128)(2,1)S(1)}, bf16[2,128,1024]{2,1,0:T(8,128)(2,1)S(1)}, u32[]{:S(2)}, u32[]{:S(2)}) collective-permute-start(bf16[2,128,1024]{2,1,0:T(8,128)(2,1)S(1)} %collective-permute-done.11.refs_2_), channel_id=1, source_target_pairs={{0,4},{4,0},{8,12},{12,8},{16,20},{20,16},{24,28},{28,24},{1,5},{5... | collective-permute-start | bytes 1572872 | tf_op jit(solution)/shard_map/ppermute | solution.py:84
  74.4 14.7 %collective-permute-start.14 = (bf16[2,128,1024]{2,1,0:T(8,128)(2,1)S(1)}, bf16[2,128,1024]{2,1,0:T(8,128)(2,1)S(1)}, u32[]{:S(2)}, u32[]{:S(2)}) collective-permute-start(bf16[2,128,1024]{2,1,0:T(8,128)(2,1)S(1)} %pad_maximum_fusion.3), channel_id=1, source_target_pairs={{0,8},{4,12},{8,0},{12,4},{16,24},{20,28},{24,16},{28,20},{1,9},{5... | collective-permute-start | bytes 1572872 | tf_op jit(solution)/shard_map/ppermute | solution.py:84
  83.1 10.0 %collective-permute-start.18 = (bf16[1,128,1024]{2,1,0:T(8,128)(2,1)S(1)}, bf16[1,128,1024]{2,1,0:T(8,128)(2,1)S(1)}, u32[]{:S(2)}, u32[]{:S(2)}) collective-permute-start(bf16[1,128,1024]{2,1,0:T(8,128)(2,1)S(1)} %bitcast.64), channel_id=1, source_target_pairs={{0,4},{4,0},{8,12},{12,8},{16,20},{20,16},{24,28},{28,24},{1,5},{5... | collective-permute-start | bytes 786440 | tf_op jit(solution)/shard_map/ppermute | solution.py:84
  93.3 14.3 %collective-permute-start.21 = (bf16[2,128,1024]{2,1,0:T(8,128)(2,1)S(1)}, bf16[2,128,1024]{2,1,0:T(8,128)(2,1)S(1)}, u32[]{:S(2)}, u32[]{:S(2)}) collective-permute-start(bf16[2,128,1024]{2,1,0:T(8,128)(2,1)S(1)} %collective-permute-done.14.refs_4_), channel_id=1, source_target_pairs={{0,4},{4,0},{8,12},{12,8},{16,20},{20,16},{24,28},{28,24},{1,5},{5... | collective-permute-start | bytes 1572872 | tf_op jit(solution)/shard_map/ppermute | solution.py:84
  114.1 14.1 %collective-permute-start.23 = (bf16[256,1024]{1,0:T(8,128)(2,1)S(1)}, bf16[256,1024]{1,0:T(8,128)(2,1)S(1)}, u32[]{:S(2)}, u32[]{:S(2)}) collective-permute-start(bf16[256,1024]{1,0:T(8,128)(2,1)S(1)} %get-tuple-element.162), channel_id=1, source_target_pairs={{0,2},{1,3},{2,0},{3,1},{4,6},{5,7},{6,4},{7,5},{8,10},{9,11},{10,... | collective-permute-start | bytes 1572872 | tf_op jit(solution)/shard_map/ppermute | solution.py:84
  120.0 14.8 %collective-permute-start.27 = (bf16[256,1024]{1,0:T(8,128)(2,1)S(1)}, bf16[256,1024]{1,0:T(8,128)(2,1)S(1)}, u32[]{:S(2)}, u32[]{:S(2)}) collective-permute-start(bf16[256,1024]{1,0:T(8,128)(2,1)S(1)} %fusion.8), channel_id=1, source_target_pairs={{0,1},{1,0},{2,3},{3,2},{4,5},{5,4},{6,7},{7,6},{8,9},{9,8},{10,11... | collective-permute-start | bytes 1572872 | tf_op jit(solution)/shard_map/ppermute | solution.py:84
  120.6 14.0 %collective-permute-start.30 = (bf16[4,128,512]{2,1,0:T(8,128)(2,1)S(1)}, bf16[4,128,512]{2,1,0:T(8,128)(2,1)S(1)}, u32[]{:S(2)}, u32[]{:S(2)}) collective-permute-start(bf16[4,128,512]{2,1,0:T(8,128)(2,1)S(1)} %pad_maximum_fusion.5.refs_0_), channel_id=1, source_target_pairs={{0,4},{4,0},{8,12},{12,8},{16,20},{20,16},{24,28},{28,24},{1,5},{5... | collective-permute-start | bytes 1572872 | tf_op jit(solution)/shard_map/ppermute | solution.py:84
  138.8 17.6 %collective-permute-start.25 = (bf16[256,1024]{1,0:T(8,128)(2,1)S(1)}, bf16[256,1024]{1,0:T(8,128)(2,1)S(1)}, u32[]{:S(2)}, u32[]{:S(2)}) collective-permute-start(bf16[256,1024]{1,0:T(8,128)(2,1)S(1)} %fusion.14), channel_id=1, source_target_pairs={{0,1},{1,0},{2,3},{3,2},{4,5},{5,4},{6,7},{7,6},{8,9},{9,8},{10,11... | collective-permute-start | bytes 1572872 | tf_op jit(solution)/shard_map/ppermute | solution.py:84
  139.3 17.1 %collective-permute-start.28 = (bf16[256,1024]{1,0:T(8,128)(2,1)S(1)}, bf16[256,1024]{1,0:T(8,128)(2,1)S(1)}, u32[]{:S(2)}, u32[]{:S(2)}) collective-permute-start(bf16[256,1024]{1,0:T(8,128)(2,1)S(1)} %add_convert_fusion), channel_id=1, source_target_pairs={{0,2},{1,3},{2,0},{3,1},{4,6},{5,7},{6,4},{7,5},{8,10},{9,11},{10,... | collective-permute-start | bytes 1572872 | tf_op jit(solution)/shard_map/ppermute | solution.py:84
  158.5 11.1 %collective-permute-start.35 = (bf16[512,1024]{1,0:T(8,128)(2,1)S(1)}, bf16[512,1024]{1,0:T(8,128)(2,1)S(1)}, u32[]{:S(2)}, u32[]{:S(2)}) collective-permute-start(bf16[512,1024]{1,0:T(8,128)(2,1)S(1)} %project_back.3.own), channel_id=1, source_target_pairs={{0,1},{1,0},{2,3},{3,2},{4,5},{5,4},{6,7},{7,6},{8,9},{9,8},{10,11... | collective-permute-start | bytes 3145736 | tf_op jit(solution)/shard_map/ppermute | solution.py:84
  159.7 14.4 %collective-permute-start.37 = (bf16[256,1024]{1,0:T(8,128)(2,1)S(1)}, bf16[256,1024]{1,0:T(8,128)(2,1)S(1)}, u32[]{:S(2)}, u32[]{:S(2)}) collective-permute-start(bf16[256,1024]{1,0:T(8,128)(2,1)S(1)} %project_back.5), channel_id=1, source_target_pairs={{0,2},{1,3},{2,0},{3,1},{4,6},{5,7},{6,4},{7,5},{8,10},{9,11},{10,... | collective-permute-start | bytes 1572872 | tf_op jit(solution)/shard_map/ppermute | solution.py:84
  (40 other events, 406.7 us)

commit v4 on v3

--- a/solution.py
+++ b/solution.py
@@ -699,6 +699,23 @@
         name="plus",
         cost_estimate=brief(),
     )(one, two)
+
+
+def down_rows_kernel(act, down, *refs):
+    total = dot(act[...], down[0], NT)
+    for one in refs[:-1]:
+        total = total + one[...].astype(jnp.float32)
+    refs[-1][...] = total.astype(jnp.bfloat16)
+
+
+def down_rows(act, down, *rest):
+    return pl.pallas_call(
+        down_rows_kernel,
+        out_shape=shaped((act.shape[0], down.shape[1]), jnp.bfloat16),
+        compiler_params=limited(),
+        name="down_rows",
+        cost_estimate=brief(),
+    )(act, down, *rest)
 
 
 def output_kernel(resid, own, core, side, branch, out):
@@ -921,16 +938,8 @@
     normed, resid = merge_half(
         tokens, norm_params, branch_late, mixes_second, merges, after(first_half, grad_hidden)
     )
-    if small:
-        normed = after(normed, encoder_far)
-
-    def branch(act, *plus):
-        part = lax.dot_general(
-            act, down_full[0], (((1,), (1,)), ((), ())), preferred_element_type=jnp.float32
-        )
-        for one in plus:
-            part = part + one.astype(jnp.float32)
-        return part.astype(jnp.bfloat16)
+    def branch(act, *rest):
+        return down_rows(act, down_full, *rest)
 
     bias = up_bias[None]
     if small:
@@ -946,16 +955,15 @@
     up_core = swap(up_core, "tensor", CORE)
     act_own, up_own = feed(OWN, after(normed, act_core), grad_hidden, up_full, bias)
     out_both = branch(after(act_both, act_own))
-    up_from = after(up_from, out_both)
+    out_core = branch(after(act_core, act_own))
+    out_own = branch(act_own)
+    up_from = after(up_from, out_both, out_core, out_own)
     if small:
         encoder_near = after(encoder_near, act_own)
         encoder_quad = joined(encoder_pair, encoder_near)
         encoder_side = swap(encoder_quad, "dp", y)
         encoder = ((encoder_quad, encoder_side), ((0, 4, 2, 6), (1, 5, 3, 7)))
         up_from = after(up_from, encoder_near)
-    out_core = branch(after(act_core, up_from))
-    out_own = branch(after(act_own, up_from))
-    up_core = after(up_core, out_own, out_core)
     grad_resid, keep, send = middle(up_own, up_core, up_from, cotangent, resid, norm_params, merges)
     out_both = swap(out_both, "tensor", CORE)
     from_side = swap(send, "tensor", SIDE)

time: 179 us -> 178 us (level)
  Pallas kernels: 51.2 us -> 54.2 us
  matrix products: 4.1 us -> 1.12 us
    pallas_call x0 -> x4, Pallas kernels: none -> 2.98 us  [down_rows(): pl.pallas_call(down_rows_kernel, out_shape=shaped((act.shape[0], down.sha...]
    dot_general x4 -> x0, matrix products: 2.97 us -> none  [branch(): lax.dot_general(act, down_full[0], (((1,), (1,)), ((), ())), preferred_el...]
  transfers between devices with their start and end apart: 41 -> 41, of which waited for: 20 -> 20; matrix products, arithmetic and copies ran while one was open for 4% -> 3% of each run, Pallas kernels for 26% -> 28%
where the time goes in v4:
time: 178 us; the launch traced here: 177 us
  waiting for transfers between devices  65.5 us (37%)
  Pallas kernels  54.2 us (30%)
  starting transfers between devices  48.1 us (27%)
  other arithmetic  5.99 us (3%)
    ppermute x41, waiting for transfers between devices, swap(): return lax.ppermute(values, axis, [(i, i ^ bits) for i in range(size)])  65.5 us
    ppermute x41, starting transfers between devices, swap(): return lax.ppermute(values, axis, [(i, i ^ bits) for i in range(size)])  48.1 us
    pallas_call x2, Pallas kernels, attend_back(): pl.pallas_call(functools.partial(attend_back_kernel, pair), grid=(1,), in...  11.4 us
    pallas_call x1, Pallas kernels, attend_second(): pl.pallas_call(functools.partial(attend_kernel, rows // 2), out_shape=out...  5.63 us
    pallas_call x3, Pallas kernels, feed(): pl.pallas_call(feed_kernel, grid=(1,), in_specs=[whole_spec(up), whole_sp...  5.5 us
    pallas_call x1, Pallas kernels, attend_first(): pl.pallas_call(attend_first_kernel, out_shape=outs, scratch_shapes=[pltpu...  4.88 us
    pallas_call x2, Pallas kernels, merge_half(): pl.pallas_call(functools.partial(merge_kernel, first), grid=(steps,), in_...  4.6 us
  transfers between devices with their start and end apart: 41, of which 20 were waited for; matrix products, arithmetic and copies ran while one was open for 3% of the time, Pallas kernels for 28%

profile of v4, /device:TPU:0, one launch (start us, length us, event | category | flops | bytes accessed | tf_op | source)
XLA Modules:
  0.0 177.2 jit_solution(9112447384407794394)
XLA Ops:
  2.8 4.1 %collective-permute-start.1 = (bf16[512,256]{1,0:T(8,128)(2,1)S(1)}, bf16[512,256]{1,0:T(8,128)(2,1)}, u32[]{:S(2)}, u32[]{:S(2)}) collective-permute-start(bf16[512,256]{1,0:T(8,128)(2,1)S(1)} %get-tuple-element.217), channel_id=1, source_target_pairs={{0,16},{4,20},{8,24},{12,28},{16,0},{20,4},{24,8},{28,12},{1,17},{... | collective-permute-start | bytes 786440 | tf_op jit(solution)/shard_map/ppermute | solution.py:84
  13.3 4.1 %collective-permute-done = bf16[160,256]{1,0:T(8,128)(2,1)S(1)} collective-permute-done((bf16[160,256]{1,0:T(8,128)(2,1)}, bf16[160,256]{1,0:T(8,128)(2,1)S(1)}, u32[]{:S(2)}, u32[]{:S(2)}) %collective-permute-start) | collective-permute-done | bytes 81952 | tf_op jit(solution)/shard_map/ppermute | solution.py:84
  20.7 3.6 %collective-permute-start.3 = (bf16[2,160,256]{2,1,0:T(8,128)(2,1)S(1)}, bf16[2,160,256]{2,1,0:T(8,128)(2,1)S(1)}, u32[]{:S(2)}, u32[]{:S(2)}) collective-permute-start(bf16[2,160,256]{2,1,0:T(8,128)(2,1)S(1)} %pad_maximum_fusion.9), channel_id=1, source_target_pairs={{0,16},{4,20},{8,24},{12,28},{16,0},{20,4},{24,8},{28,12},{1,17},{... | collective-permute-start | bytes 491528 | tf_op jit(solution)/shard_map/ppermute | solution.py:84
  25.7 10.9 %collective-permute-done.5.refs_1_ = bf16[2,512,256]{2,1,0:T(8,128)(2,1)S(1)} collective-permute-done((bf16[2,512,256]{2,1,0:T(8,128)(2,1)S(1)}, bf16[2,512,256]{2,1,0:T(8,128)(2,1)S(1)}, u32[]{:S(2)}, u32[]{:S(2)}) %collective-permute-start.5) | collective-permute-done | bytes 524320 | tf_op jit(solution)/shard_map/ppermute | solution.py:84
  39.9 3.3 %collective-permute-start.8 = (bf16[128,1024]{1,0:T(8,128)(2,1)S(1)}, bf16[128,1024]{1,0:T(8,128)(2,1)S(1)}, u32[]{:S(2)}, u32[]{:S(2)}) collective-permute-start(bf16[128,1024]{1,0:T(8,128)(2,1)S(1)} %copy-done.22), channel_id=1, source_target_pairs={{0,16},{4,20},{8,24},{12,28},{16,0},{20,4},{24,8},{28,12},{1,17},{... | collective-permute-start | bytes 786440 | tf_op jit(solution)/shard_map/ppermute | solution.py:84
  43.1 5.7 %collective-permute-done.7.refs_3_ = bf16[2,512,256]{2,1,0:T(8,128)(2,1)S(1)} collective-permute-done((bf16[2,512,256]{2,1,0:T(8,128)(2,1)S(1)}, bf16[2,512,256]{2,1,0:T(8,128)(2,1)S(1)}, u32[]{:S(2)}, u32[]{:S(2)}) %collective-permute-start.7) | collective-permute-done | bytes 524320 | tf_op jit(solution)/shard_map/ppermute | solution.py:84
  48.9 2.7 %project.1 = (bf16[3,1024,256]{2,1,0:T(8,128)(2,1)S(1)}, bf16[3,1024,256]{2,1,0:T(8,128)(2,1)S(1)}, bf16[2,512,256]{2,1,0:T(8,128)(2,1)S(1)}) custom-call(bf16[1024,1024]{1,0:T(8,128)(2,1)S(1)} %copy-done, f32[4,1024]{1,0:T(4,128)S(1)} %copy-done.5, f32[3,256]{1,0:T(4,128)S(1)} %copy-done.17, bf16[2,512,256]{2,1,0:T(8,128)(2,1)S(1)} %pad_maximum_fusion.1.refs_0_, ...), custom_call_target="tpu_custom_call" | custom-call | tf_op jit(solution)/shard_map/project/pallas_call | solution.py:187
  54.5 2.8 %collective-permute-start.11 = (bf16[2,128,1024]{2,1,0:T(8,128)(2,1)S(1)}, bf16[2,128,1024]{2,1,0:T(8,128)(2,1)S(1)}, u32[]{:S(2)}, u32[]{:S(2)}) collective-permute-start(bf16[2,128,1024]{2,1,0:T(8,128)(2,1)S(1)} %pad_maximum_fusion.2.refs_0_), channel_id=1, source_target_pairs={{0,8},{4,12},{8,0},{12,4},{16,24},{20,28},{24,16},{28,20},{1,9},{5... | collective-permute-start | bytes 1572872 | tf_op jit(solution)/shard_map/ppermute | solution.py:84
  57.8 2.7 %collective-permute-start.10 = (bf16[128,1024]{1,0:T(8,128)(2,1)S(1)}, bf16[128,1024]{1,0:T(8,128)(2,1)S(1)}, u32[]{:S(2)}, u32[]{:S(2)}) collective-permute-start(bf16[128,1024]{1,0:T(8,128)(2,1)S(1)} %copy-done.3), channel_id=1, source_target_pairs={{0,16},{4,20},{8,24},{12,28},{16,0},{20,4},{24,8},{28,12},{1,17},{... | collective-permute-start | bytes 786440 | tf_op jit(solution)/shard_map/ppermute | solution.py:84
  60.5 4.9 %attend_first.1 = (bf16[512,256]{1,0:T(8,128)(2,1)S(1)}, f32[512,128]{1,0:T(8,128)S(1)}, f32[16,512]{1,0:T(8,128)S(1)}, bf16[2,16,256]{2,1,0:T(8,128)(2,1)S(1)}) custom-call(bf16[3,1024,256]{2,1,0:T(8,128)(2,1)S(1)} %get-tuple-element.134.proj.query, f32[16,512]{1,0:T(8,128)S(1)} %get-tuple-element.127.encoded, f32[1,512]{1,0:T(1,128)S(1)} %bitcast.50, ...), custom_call_target="tpu_custom_call" | custom-call | tf_op jit(solution)/shard_map/attend_first/pallas_call | solution.py:286
  66.0 6.3 %collective-permute-done.10 = bf16[128,1024]{1,0:T(8,128)(2,1)S(1)} collective-permute-done((bf16[128,1024]{1,0:T(8,128)(2,1)S(1)}, bf16[128,1024]{1,0:T(8,128)(2,1)S(1)}, u32[]{:S(2)}, u32[]{:S(2)}) %collective-permute-start.10) | collective-permute-done | bytes 262176 | tf_op jit(solution)/shard_map/ppermute | solution.py:84
  76.9 5.6 %attend_second.1 = (bf16[512,256]{1,0:T(8,128)(2,1)S(1)}, f32[512,128]{1,0:T(8,128)S(1)}) custom-call(bf16[3,1024,256]{2,1,0:T(8,128)(2,1)S(1)} %get-tuple-element.134.proj.query, bf16[2,16,256]{2,1,0:T(8,128)(2,1)S(1)} %get-tuple-element.135.prefix), custom_call_target="tpu_custom_call" | custom-call | tf_op jit(solution)/shard_map/attend_second/pallas_call | solution.py:299
  84.1 3.9 %collective-permute-done.13.refs_3_ = bf16[2,128,1024]{2,1,0:T(8,128)(2,1)S(1)} collective-permute-done((bf16[2,128,1024]{2,1,0:T(8,128)(2,1)S(1)}, bf16[2,128,1024]{2,1,0:T(8,128)(2,1)S(1)}, u32[]{:S(2)}, u32[]{:S(2)}) %collective-permute-start.13) | collective-permute-done | bytes 524320 | tf_op jit(solution)/shard_map/ppermute | solution.py:84
  96.5 2.5 %down_back.1 = (bf16[1,1024,1024]{2,1,0:T(8,128)(2,1)S(1)}, bf16[1024,1024]{1,0:T(8,128)(2,1)S(1)}) custom-call(bf16[1024,1024]{1,0:T(8,128)(2,1)S(1)} %copy-done.1, bf16[2,128,1024]{2,1,0:T(8,128)(2,1)S(1)} %pad_maximum_fusion.2.refs_0_, bf16[2,128,1024]{2,1,0:T(8,128)(2,1)S(1)} %collective-permute-done.12.refs_1_, ...), custom_call_target="tpu_custom_call" | custom-call | tf_op jit(solution)/shard_map/down_back/pallas_call | solution.py:209
  103.7 3.9 %collective-permute-done.21.refs_5_ = bf16[2,128,1024]{2,1,0:T(8,128)(2,1)S(1)} collective-permute-done((bf16[2,128,1024]{2,1,0:T(8,128)(2,1)S(1)}, bf16[2,128,1024]{2,1,0:T(8,128)(2,1)S(1)}, u32[]{:S(2)}, u32[]{:S(2)}) %collective-permute-start.21) | collective-permute-done | bytes 524320 | tf_op jit(solution)/shard_map/ppermute | solution.py:84
  109.7 2.5 %collective-permute-start.26 = (bf16[2,128,512]{2,1,0:T(8,128)(2,1)S(1)}, bf16[2,128,512]{2,1,0:T(8,128)(2,1)S(1)}, u32[]{:S(2)}, u32[]{:S(2)}) collective-permute-start(bf16[2,128,512]{2,1,0:T(8,128)(2,1)S(1)} %pad_maximum_fusion.8), channel_id=1, source_target_pairs={{0,8},{4,12},{8,0},{12,4},{16,24},{20,28},{24,16},{28,20},{1,9},{5... | collective-permute-start | bytes 786440 | tf_op jit(solution)/shard_map/ppermute | solution.py:84
  122.7 5.5 %collective-permute-done.25.side = bf16[256,1024]{1,0:T(8,128)(2,1)S(1)} collective-permute-done((bf16[256,1024]{1,0:T(8,128)(2,1)S(1)}, bf16[256,1024]{1,0:T(8,128)(2,1)S(1)}, u32[]{:S(2)}, u32[]{:S(2)}) %collective-permute-start.25) | collective-permute-done | bytes 524320 | tf_op jit(solution)/shard_map/ppermute | solution.py:84
  130.3 2.8 %collective-permute-done.30.refs_1_ = bf16[4,128,512]{2,1,0:T(8,128)(2,1)S(1)} collective-permute-done((bf16[4,128,512]{2,1,0:T(8,128)(2,1)S(1)}, bf16[4,128,512]{2,1,0:T(8,128)(2,1)S(1)}, u32[]{:S(2)}, u32[]{:S(2)}) %collective-permute-start.30) | collective-permute-done | bytes 524320 | tf_op jit(solution)/shard_map/ppermute | solution.py:84
  134.0 3.3 %collective-permute-done.29.side = bf16[2,256,256]{2,1,0:T(8,128)(2,1)S(1)} collective-permute-done((bf16[2,256,256]{2,1,0:T(8,128)(2,1)S(1)}, bf16[2,256,256]{2,1,0:T(8,128)(2,1)S(1)}, u32[]{:S(2)}, u32[]{:S(2)}) %collective-permute-start.29) | collective-permute-done | bytes 262176 | tf_op jit(solution)/shard_map/ppermute | solution.py:84
  141.8 5.7 %attend_back.2.one = bf16[3,1024,128]{2,1,0:T(8,128)(2,1)S(1)} custom-call(bf16[3,1024,256]{2,1,0:T(8,128)(2,1)S(1)} %get-tuple-element.134.proj.query, bf16[1024,256]{1,0:T(8,128)(2,1)S(1)} %get-tuple-element.191.gmix, f32[8,1024]{1,0:T(8,128)S(1)} %get-tuple-element.187.log_sums, f32[8,1024]{1,0:T(8,128)S(1)} %get-tuple-element.188.inner, ...), custom_call_target="tpu_custom_call" | custom-call | flops 1610612736 | bytes 3932160 | tf_op jit(solution)/shard_map/attend_back/pallas_call | solution.py:428
  149.2 5.7 %attend_back.3.two = bf16[3,1024,128]{2,1,0:T(8,128)(2,1)S(1)} custom-call(bf16[3,1024,256]{2,1,0:T(8,128)(2,1)S(1)} %get-tuple-element.134.proj.query, bf16[1024,256]{1,0:T(8,128)(2,1)S(1)} %get-tuple-element.191.gmix, f32[8,1024]{1,0:T(8,128)S(1)} %get-tuple-element.187.log_sums, f32[8,1024]{1,0:T(8,128)S(1)} %get-tuple-element.188.inner, ...), custom_call_target="tpu_custom_call" | custom-call | flops 1610612736 | bytes 3932160 | tf_op jit(solution)/shard_map/attend_back/pallas_call | solution.py:428
  160.8 3.5 %collective-permute-done.38.two = f32[2,16,256]{2,1,0:T(8,128)S(1)} collective-permute-done((f32[2,16,256]{2,1,0:T(8,128)S(1)}, f32[2,16,256]{2,1,0:T(8,128)S(1)}, u32[]{:S(2)}, u32[]{:S(2)}) %collective-permute-start.38) | collective-permute-done | bytes 32800 | tf_op jit(solution)/shard_map/ppermute | solution.py:84
  168.1 4.4 %collective-permute-done.37.side = bf16[256,1024]{1,0:T(8,128)(2,1)S(1)} collective-permute-done((bf16[256,1024]{1,0:T(8,128)(2,1)S(1)}, bf16[256,1024]{1,0:T(8,128)(2,1)S(1)}, u32[]{:S(2)}, u32[]{:S(2)}) %collective-permute-start.37) | collective-permute-done | bytes 524320 | tf_op jit(solution)/shard_map/ppermute | solution.py:84
  174.4 2.6 %update.1 = (f32[1,1]{1,0:T(1,128)}, f32[10,1024]{1,0:T(8,128)}, f32[10,1024]{1,0:T(8,128)}, f32[10,1024]{1,0:T(8,128)}, f32[128,512]{1,0:T(8,128)}, /*index=5*/...) custom-call(f32[16,512]{1,0:T(8,128)S(1)} %plus.5.joint_one, ...), custom_call_target="tpu_custom_call" | custom-call | tf_op jit(solution)/shard_map/update/pallas_call | solution.py:1029
  (156 shorter events, 72.6 us)
Async XLA Ops:
  2.8 16.2 %collective-permute-start.1 = (bf16[512,256]{1,0:T(8,128)(2,1)S(1)}, bf16[512,256]{1,0:T(8,128)(2,1)}, u32[]{:S(2)}, u32[]{:S(2)}) collective-permute-start(bf16[512,256]{1,0:T(8,128)(2,1)S(1)} %get-tuple-element.217), channel_id=1, source_target_pairs={{0,16},{4,20},{8,24},{12,28},{16,0},{20,4},{24,8},{28,12},{1,17},{... | collective-permute-start | bytes 786440 | tf_op jit(solution)/shard_map/ppermute | solution.py:84
  6.9 12.0 %collective-permute-start.2 = (bf16[128,1024]{1,0:T(8,128)(2,1)}, bf16[128,1024]{1,0:T(8,128)(2,1)S(1)}, u32[]{:S(2)}, u32[]{:S(2)}) collective-permute-start(bf16[128,1024]{1,0:T(8,128)(2,1)} %param.33), channel_id=1, source_target_pairs={{0,4},{4,0},{8,12},{12,8},{16,20},{20,16},{24,28},{28,24},{1,5},{5... | collective-permute-start | bytes 786440 | tf_op jit(solution)/shard_map/ppermute | solution.py:84
  20.0 16.7 %collective-permute-start.5 = (bf16[2,512,256]{2,1,0:T(8,128)(2,1)S(1)}, bf16[2,512,256]{2,1,0:T(8,128)(2,1)S(1)}, u32[]{:S(2)}, u32[]{:S(2)}) collective-permute-start(bf16[2,512,256]{2,1,0:T(8,128)(2,1)S(1)} %pad_maximum_fusion.1.refs_0_), channel_id=1, source_target_pairs={{0,8},{4,12},{8,0},{12,4},{16,24},{20,28},{24,16},{28,20},{1,9},{5... | collective-permute-start | bytes 1572872 | tf_op jit(solution)/shard_map/ppermute | solution.py:84
  20.7 17.3 %collective-permute-start.3 = (bf16[2,160,256]{2,1,0:T(8,128)(2,1)S(1)}, bf16[2,160,256]{2,1,0:T(8,128)(2,1)S(1)}, u32[]{:S(2)}, u32[]{:S(2)}) collective-permute-start(bf16[2,160,256]{2,1,0:T(8,128)(2,1)S(1)} %pad_maximum_fusion.9), channel_id=1, source_target_pairs={{0,16},{4,20},{8,24},{12,28},{16,0},{20,4},{24,8},{28,12},{1,17},{... | collective-permute-start | bytes 491528 | tf_op jit(solution)/shard_map/ppermute | solution.py:84
  24.2 18.9 %collective-permute-start.6 = (bf16[2,512,256]{2,1,0:T(8,128)(2,1)S(1)}, bf16[2,512,256]{2,1,0:T(8,128)(2,1)S(1)}, u32[]{:S(2)}, u32[]{:S(2)}) collective-permute-start(bf16[2,512,256]{2,1,0:T(8,128)(2,1)S(1)} %pad_maximum_fusion.1.refs_0_), channel_id=1, source_target_pairs={{0,4},{4,0},{8,12},{12,8},{16,20},{20,16},{24,28},{28,24},{1,5},{5... | collective-permute-start | bytes 1572872 | tf_op jit(solution)/shard_map/ppermute | solution.py:84
  36.6 12.2 %collective-permute-start.7 = (bf16[2,512,256]{2,1,0:T(8,128)(2,1)S(1)}, bf16[2,512,256]{2,1,0:T(8,128)(2,1)S(1)}, u32[]{:S(2)}, u32[]{:S(2)}) collective-permute-start(bf16[2,512,256]{2,1,0:T(8,128)(2,1)S(1)} %collective-permute-done.5.refs_1_), channel_id=1, source_target_pairs={{0,4},{4,0},{8,12},{12,8},{16,20},{20,16},{24,28},{28,24},{1,5},{5... | collective-permute-start | bytes 1572872 | tf_op jit(solution)/shard_map/ppermute | solution.py:84
  38.0 14.8 %collective-permute-start.4 = (bf16[4,160,256]{2,1,0:T(8,128)(2,1)S(1)}, bf16[4,160,256]{2,1,0:T(8,128)(2,1)S(1)}, u32[]{:S(2)}, u32[]{:S(2)}) collective-permute-start(bf16[4,160,256]{2,1,0:T(8,128)(2,1)S(1)} %pad_maximum_fusion.6.refs_0_), channel_id=1, source_target_pairs={{0,8},{4,12},{8,0},{12,4},{16,24},{20,28},{24,16},{28,20},{1,9},{5... | collective-permute-start | bytes 983048 | tf_op jit(solution)/shard_map/ppermute | solution.py:84
  39.9 12.9 %collective-permute-start.8 = (bf16[128,1024]{1,0:T(8,128)(2,1)S(1)}, bf16[128,1024]{1,0:T(8,128)(2,1)S(1)}, u32[]{:S(2)}, u32[]{:S(2)}) collective-permute-start(bf16[128,1024]{1,0:T(8,128)(2,1)S(1)} %copy-done.22), channel_id=1, source_target_pairs={{0,16},{4,20},{8,24},{12,28},{16,0},{20,4},{24,8},{28,12},{1,17},{... | collective-permute-start | bytes 786440 | tf_op jit(solution)/shard_map/ppermute | solution.py:84
  52.9 13.1 %collective-permute-start.9 = (bf16[1024,256]{1,0:T(8,128)(2,1)S(1)}, bf16[1024,256]{1,0:T(8,128)(2,1)S(1)}, u32[]{:S(2)}, u32[]{:S(2)}) collective-permute-start(bf16[1024,256]{1,0:T(8,128)(2,1)S(1)} %get-tuple-element.126.refs_4_.refs_0_), channel_id=1, source_target_pairs={{0,2},{1,3},{2,0},{3,1},{4,6},{5,7},{6,4},{7,5},{8,10},{9,11},{10,... | collective-permute-start | bytes 1572872 | tf_op jit(solution)/shard_map/ppermute | solution.py:84
  54.5 18.5 %collective-permute-start.11 = (bf16[2,128,1024]{2,1,0:T(8,128)(2,1)S(1)}, bf16[2,128,1024]{2,1,0:T(8,128)(2,1)S(1)}, u32[]{:S(2)}, u32[]{:S(2)}) collective-permute-start(bf16[2,128,1024]{2,1,0:T(8,128)(2,1)S(1)} %pad_maximum_fusion.2.refs_0_), channel_id=1, source_target_pairs={{0,8},{4,12},{8,0},{12,4},{16,24},{20,28},{24,16},{28,20},{1,9},{5... | collective-permute-start | bytes 1572872 | tf_op jit(solution)/shard_map/ppermute | solution.py:84
  57.3 15.7 %collective-permute-start.12 = (bf16[2,128,1024]{2,1,0:T(8,128)(2,1)S(1)}, bf16[2,128,1024]{2,1,0:T(8,128)(2,1)S(1)}, u32[]{:S(2)}, u32[]{:S(2)}) collective-permute-start(bf16[2,128,1024]{2,1,0:T(8,128)(2,1)S(1)} %pad_maximum_fusion.2.refs_0_), channel_id=1, source_target_pairs={{0,4},{4,0},{8,12},{12,8},{16,20},{20,16},{24,28},{28,24},{1,5},{5... | collective-permute-start | bytes 1572872 | tf_op jit(solution)/shard_map/ppermute | solution.py:84
  57.8 14.5 %collective-permute-start.10 = (bf16[128,1024]{1,0:T(8,128)(2,1)S(1)}, bf16[128,1024]{1,0:T(8,128)(2,1)S(1)}, u32[]{:S(2)}, u32[]{:S(2)}) collective-permute-start(bf16[128,1024]{1,0:T(8,128)(2,1)S(1)} %copy-done.3), channel_id=1, source_target_pairs={{0,16},{4,20},{8,24},{12,28},{16,0},{20,4},{24,8},{28,12},{1,17},{... | collective-permute-start | bytes 786440 | tf_op jit(solution)/shard_map/ppermute | solution.py:84
  73.1 16.0 %collective-permute-start.16 = (bf16[3072,256]{1,0:T(8,128)(2,1)S(1)}, bf16[3072,256]{1,0:T(8,128)(2,1)S(1)}, u32[]{:S(2)}, u32[]{:S(2)}) collective-permute-start(bf16[3072,256]{1,0:T(8,128)(2,1)S(1)} %pad_maximum_fusion), channel_id=1, source_target_pairs={{0,1},{1,0},{2,3},{3,2},{4,5},{5,4},{6,7},{7,6},{8,9},{9,8},{10,11... | collective-permute-start | bytes 4718600 | tf_op jit(solution)/shard_map/ppermute | solution.py:84
  73.2 14.9 %collective-permute-start.13 = (bf16[2,128,1024]{2,1,0:T(8,128)(2,1)S(1)}, bf16[2,128,1024]{2,1,0:T(8,128)(2,1)S(1)}, u32[]{:S(2)}, u32[]{:S(2)}) collective-permute-start(bf16[2,128,1024]{2,1,0:T(8,128)(2,1)S(1)} %collective-permute-done.11.refs_2_), channel_id=1, source_target_pairs={{0,4},{4,0},{8,12},{12,8},{16,20},{20,16},{24,28},{28,24},{1,5},{5... | collective-permute-start | bytes 1572872 | tf_op jit(solution)/shard_map/ppermute | solution.py:84
  74.4 14.7 %collective-permute-start.14 = (bf16[2,128,1024]{2,1,0:T(8,128)(2,1)S(1)}, bf16[2,128,1024]{2,1,0:T(8,128)(2,1)S(1)}, u32[]{:S(2)}, u32[]{:S(2)}) collective-permute-start(bf16[2,128,1024]{2,1,0:T(8,128)(2,1)S(1)} %pad_maximum_fusion.3), channel_id=1, source_target_pairs={{0,8},{4,12},{8,0},{12,4},{16,24},{20,28},{24,16},{28,20},{1,9},{5... | collective-permute-start | bytes 1572872 | tf_op jit(solution)/shard_map/ppermute | solution.py:84
  93.3 14.3 %collective-permute-start.21 = (bf16[2,128,1024]{2,1,0:T(8,128)(2,1)S(1)}, bf16[2,128,1024]{2,1,0:T(8,128)(2,1)S(1)}, u32[]{:S(2)}, u32[]{:S(2)}) collective-permute-start(bf16[2,128,1024]{2,1,0:T(8,128)(2,1)S(1)} %collective-permute-done.14.refs_4_), channel_id=1, source_target_pairs={{0,4},{4,0},{8,12},{12,8},{16,20},{20,16},{24,28},{28,24},{1,5},{5... | collective-permute-start | bytes 1572872 | tf_op jit(solution)/shard_map/ppermute | solution.py:84
  114.1 14.1 %collective-permute-start.25 = (bf16[256,1024]{1,0:T(8,128)(2,1)S(1)}, bf16[256,1024]{1,0:T(8,128)(2,1)S(1)}, u32[]{:S(2)}, u32[]{:S(2)}) collective-permute-start(bf16[256,1024]{1,0:T(8,128)(2,1)S(1)} %get-tuple-element.158), channel_id=1, source_target_pairs={{0,2},{1,3},{2,0},{3,1},{4,6},{5,7},{6,4},{7,5},{8,10},{9,11},{10,... | collective-permute-start | bytes 1572872 | tf_op jit(solution)/shard_map/ppermute | solution.py:84
  116.5 11.7 %collective-permute-start.24 = (bf16[256,1024]{1,0:T(8,128)(2,1)S(1)}, bf16[256,1024]{1,0:T(8,128)(2,1)S(1)}, u32[]{:S(2)}, u32[]{:S(2)}) collective-permute-start(bf16[256,1024]{1,0:T(8,128)(2,1)S(1)} %get-tuple-element.167), channel_id=1, source_target_pairs={{0,1},{1,0},{2,3},{3,2},{4,5},{5,4},{6,7},{7,6},{8,9},{9,8},{10,11... | collective-permute-start | bytes 1572872 | tf_op jit(solution)/shard_map/ppermute | solution.py:84
  119.3 13.8 %collective-permute-start.30 = (bf16[4,128,512]{2,1,0:T(8,128)(2,1)S(1)}, bf16[4,128,512]{2,1,0:T(8,128)(2,1)S(1)}, u32[]{:S(2)}, u32[]{:S(2)}) collective-permute-start(bf16[4,128,512]{2,1,0:T(8,128)(2,1)S(1)} %pad_maximum_fusion.5.refs_0_), channel_id=1, source_target_pairs={{0,4},{4,0},{8,12},{12,8},{16,20},{20,16},{24,28},{28,24},{1,5},{5... | collective-permute-start | bytes 1572872 | tf_op jit(solution)/shard_map/ppermute | solution.py:84
  121.1 12.1 %collective-permute-start.27 = (bf16[256,1024]{1,0:T(8,128)(2,1)S(1)}, bf16[256,1024]{1,0:T(8,128)(2,1)S(1)}, u32[]{:S(2)}, u32[]{:S(2)}) collective-permute-start(bf16[256,1024]{1,0:T(8,128)(2,1)S(1)} %down_rows.6), channel_id=1, source_target_pairs={{0,1},{1,0},{2,3},{3,2},{4,5},{5,4},{6,7},{7,6},{8,9},{9,8},{10,11... | collective-permute-start | bytes 1572872 | tf_op jit(solution)/shard_map/ppermute | solution.py:84
  137.3 17.6 %collective-permute-start.23 = (bf16[256,1024]{1,0:T(8,128)(2,1)S(1)}, bf16[256,1024]{1,0:T(8,128)(2,1)S(1)}, u32[]{:S(2)}, u32[]{:S(2)}) collective-permute-start(bf16[256,1024]{1,0:T(8,128)(2,1)S(1)} %down_rows.5), channel_id=1, source_target_pairs={{0,1},{1,0},{2,3},{3,2},{4,5},{5,4},{6,7},{7,6},{8,9},{9,8},{10,11... | collective-permute-start | bytes 1572872 | tf_op jit(solution)/shard_map/ppermute | solution.py:84
  137.8 17.1 %collective-permute-start.28 = (bf16[256,1024]{1,0:T(8,128)(2,1)S(1)}, bf16[256,1024]{1,0:T(8,128)(2,1)S(1)}, u32[]{:S(2)}, u32[]{:S(2)}) collective-permute-start(bf16[256,1024]{1,0:T(8,128)(2,1)S(1)} %down_rows.7), channel_id=1, source_target_pairs={{0,2},{1,3},{2,0},{3,1},{4,6},{5,7},{6,4},{7,5},{8,10},{9,11},{10,... | collective-permute-start | bytes 1572872 | tf_op jit(solution)/shard_map/ppermute | solution.py:84
  157.1 11.1 %collective-permute-start.35 = (bf16[512,1024]{1,0:T(8,128)(2,1)S(1)}, bf16[512,1024]{1,0:T(8,128)(2,1)S(1)}, u32[]{:S(2)}, u32[]{:S(2)}) collective-permute-start(bf16[512,1024]{1,0:T(8,128)(2,1)S(1)} %project_back.3.own), channel_id=1, source_target_pairs={{0,1},{1,0},{2,3},{3,2},{4,5},{5,4},{6,7},{7,6},{8,9},{9,8},{10,11... | collective-permute-start | bytes 3145736 | tf_op jit(solution)/shard_map/ppermute | solution.py:84
  158.2 14.4 %collective-permute-start.37 = (bf16[256,1024]{1,0:T(8,128)(2,1)S(1)}, bf16[256,1024]{1,0:T(8,128)(2,1)S(1)}, u32[]{:S(2)}, u32[]{:S(2)}) collective-permute-start(bf16[256,1024]{1,0:T(8,128)(2,1)S(1)} %project_back.5), channel_id=1, source_target_pairs={{0,2},{1,3},{2,0},{3,1},{4,6},{5,7},{6,4},{7,5},{8,10},{9,11},{10,... | collective-permute-start | bytes 1572872 | tf_op jit(solution)/shard_map/ppermute | solution.py:84
  (40 other events, 407.1 us)

commit v5 on v4

--- a/solution.py
+++ b/solution.py
@@ -891,8 +891,10 @@
 
     merge_side = after(swap(merge_own, "tensor", SIDE), mix_first)
     if small:
-        merge_side, up_far, down_near, down_pair_side = after(
-            (merge_side, up_far, down_near, down_pair_side)
+        up_far = after(up_far, mix_first)
+        up_far_side = swap(up_far, "dp", y)
+        merge_side, up_far_side, down_near, down_pair_side = after(
+            (merge_side, up_far_side, down_near, down_pair_side)
         )
     mix_side = swap(mix_first, "tensor", SIDE)
     half = rows // 2
@@ -910,21 +912,19 @@
         proj_late = after(projected, down_near)
         down_near_side = swap(down_near, "dp", y)
         up_near = swap(joined(up_weight[None], up_far), "dp", z)
-        up_far_side = swap(up_far, "dp", y)
     mix_second, sums_second = attend_second(proj_late, prefix)
     mix_side = swap(mix_second, "tensor", SIDE)
     branch_late = branch_bias
     if small:
-        branch_late, down_near_side, up_near = after((branch_bias, down_near_side, up_near), mix_second)
+        branch_late, down_near_side, up_near, mix_side = after(
+            (branch_bias, down_near_side, up_near, mix_side), mix_second
+        )
         down = (
             (down_pair, down_pair_side, down_near, down_near_side),
             ((0, 4), (1, 5), (2, 6), (3, 7)),
         )
         up_near_side = swap(up_near, "dp", y)
     first_half = merge_half(tokens, norm_params, branch_late, mixes_first, merges)
-    mix_side = after(mix_side, first_half)
-    if small:
-        mix_side, up_far_side = after((mix_side, up_far_side))
     mix_cores = swap(joined(mix_second, mix_side), "tensor", CORE)
     mixes_second = ((mix_second, 0), (mix_cores, 0), (mix_side, 0), (mix_cores, half))
     down_full, grad_hidden = down_back(after(cotangent, first_half), down)

time: 178 us -> 176 us (0.989)
  waiting for transfers between devices: 65.5 us -> 62.8 us
    ppermute x41, waiting for transfers between devices: 65.5 us -> 62.8 us  [swap(): return lax.ppermute(values, axis, [(i, i ^ bits) for i in range(size)])]
where the time goes in v5:
time: 176 us
  waiting for transfers between devices  62.8 us (36%)
  Pallas kernels  54.2 us (31%)
  starting transfers between devices  49 us (28%)
  other arithmetic  5.99 us (3%)
    ppermute x41, waiting for transfers between devices, swap(): return lax.ppermute(values, axis, [(i, i ^ bits) for i in range(size)])  62.8 us
    ppermute x41, starting transfers between devices, swap(): return lax.ppermute(values, axis, [(i, i ^ bits) for i in range(size)])  49 us
    pallas_call x2, Pallas kernels, attend_back(): pl.pallas_call(functools.partial(attend_back_kernel, pair), grid=(1,), in...  11.4 us
    pallas_call x1, Pallas kernels, attend_second(): pl.pallas_call(functools.partial(attend_kernel, rows // 2), out_shape=out...  5.66 us
    pallas_call x3, Pallas kernels, feed(): pl.pallas_call(feed_kernel, grid=(1,), in_specs=[whole_spec(up), whole_sp...  5.5 us
    pallas_call x1, Pallas kernels, attend_first(): pl.pallas_call(attend_first_kernel, out_shape=outs, scratch_shapes=[pltpu...  4.9 us
    pallas_call x2, Pallas kernels, merge_half(): pl.pallas_call(functools.partial(merge_kernel, first), grid=(steps,), in_...  4.58 us
  transfers between devices with their start and end apart: 41, of which 20 were waited for; matrix products, arithmetic and copies ran while one was open for 3% of the time, Pallas kernels for 28%

profile of v5, /device:TPU:0, one launch (start us, length us, event | category | flops | bytes accessed | tf_op | source)
XLA Modules:
  0.0 175.5 jit_solution(629348814284548103)
XLA Ops:
  2.8 4.1 %collective-permute-start.1 = (bf16[512,256]{1,0:T(8,128)(2,1)S(1)}, bf16[512,256]{1,0:T(8,128)(2,1)}, u32[]{:S(2)}, u32[]{:S(2)}) collective-permute-start(bf16[512,256]{1,0:T(8,128)(2,1)S(1)} %get-tuple-element.215), channel_id=1, source_target_pairs={{0,16},{4,20},{8,24},{12,28},{16,0},{20,4},{24,8},{28,12},{1,17},{... | collective-permute-start | bytes 786440 | tf_op jit(solution)/shard_map/ppermute | solution.py:84
  13.3 4.1 %collective-permute-done = bf16[160,256]{1,0:T(8,128)(2,1)S(1)} collective-permute-done((bf16[160,256]{1,0:T(8,128)(2,1)}, bf16[160,256]{1,0:T(8,128)(2,1)S(1)}, u32[]{:S(2)}, u32[]{:S(2)}) %collective-permute-start) | collective-permute-done | bytes 81952 | tf_op jit(solution)/shard_map/ppermute | solution.py:84
  20.7 3.6 %collective-permute-start.3 = (bf16[2,160,256]{2,1,0:T(8,128)(2,1)S(1)}, bf16[2,160,256]{2,1,0:T(8,128)(2,1)S(1)}, u32[]{:S(2)}, u32[]{:S(2)}) collective-permute-start(bf16[2,160,256]{2,1,0:T(8,128)(2,1)S(1)} %pad_maximum_fusion.9), channel_id=1, source_target_pairs={{0,16},{4,20},{8,24},{12,28},{16,0},{20,4},{24,8},{28,12},{1,17},{... | collective-permute-start | bytes 491528 | tf_op jit(solution)/shard_map/ppermute | solution.py:84
  25.7 10.9 %collective-permute-done.5.refs_1_ = bf16[2,512,256]{2,1,0:T(8,128)(2,1)S(1)} collective-permute-done((bf16[2,512,256]{2,1,0:T(8,128)(2,1)S(1)}, bf16[2,512,256]{2,1,0:T(8,128)(2,1)S(1)}, u32[]{:S(2)}, u32[]{:S(2)}) %collective-permute-start.5) | collective-permute-done | bytes 524320 | tf_op jit(solution)/shard_map/ppermute | solution.py:84
  39.9 3.3 %collective-permute-start.8 = (bf16[128,1024]{1,0:T(8,128)(2,1)S(1)}, bf16[128,1024]{1,0:T(8,128)(2,1)S(1)}, u32[]{:S(2)}, u32[]{:S(2)}) collective-permute-start(bf16[128,1024]{1,0:T(8,128)(2,1)S(1)} %copy-done.22), channel_id=1, source_target_pairs={{0,16},{4,20},{8,24},{12,28},{16,0},{20,4},{24,8},{28,12},{1,17},{... | collective-permute-start | bytes 786440 | tf_op jit(solution)/shard_map/ppermute | solution.py:84
  43.1 5.7 %collective-permute-done.7.refs_3_ = bf16[2,512,256]{2,1,0:T(8,128)(2,1)S(1)} collective-permute-done((bf16[2,512,256]{2,1,0:T(8,128)(2,1)S(1)}, bf16[2,512,256]{2,1,0:T(8,128)(2,1)S(1)}, u32[]{:S(2)}, u32[]{:S(2)}) %collective-permute-start.7) | collective-permute-done | bytes 524320 | tf_op jit(solution)/shard_map/ppermute | solution.py:84
  48.9 2.7 %project.1 = (bf16[3,1024,256]{2,1,0:T(8,128)(2,1)S(1)}, bf16[3,1024,256]{2,1,0:T(8,128)(2,1)S(1)}, bf16[2,512,256]{2,1,0:T(8,128)(2,1)S(1)}) custom-call(bf16[1024,1024]{1,0:T(8,128)(2,1)S(1)} %copy-done, f32[4,1024]{1,0:T(4,128)S(1)} %copy-done.5, f32[3,256]{1,0:T(4,128)S(1)} %copy-done.17, bf16[2,512,256]{2,1,0:T(8,128)(2,1)S(1)} %pad_maximum_fusion.1.refs_0_, ...), custom_call_target="tpu_custom_call" | custom-call | tf_op jit(solution)/shard_map/project/pallas_call | solution.py:187
  54.4 2.6 %collective-permute-start.10 = (bf16[128,1024]{1,0:T(8,128)(2,1)S(1)}, bf16[128,1024]{1,0:T(8,128)(2,1)S(1)}, u32[]{:S(2)}, u32[]{:S(2)}) collective-permute-start(bf16[128,1024]{1,0:T(8,128)(2,1)S(1)} %copy-done.3), channel_id=1, source_target_pairs={{0,16},{4,20},{8,24},{12,28},{16,0},{20,4},{24,8},{28,12},{1,17},{... | collective-permute-start | bytes 786440 | tf_op jit(solution)/shard_map/ppermute | solution.py:84
  60.5 4.9 %attend_first.1 = (bf16[512,256]{1,0:T(8,128)(2,1)S(1)}, f32[512,128]{1,0:T(8,128)S(1)}, f32[16,512]{1,0:T(8,128)S(1)}, bf16[2,16,256]{2,1,0:T(8,128)(2,1)S(1)}) custom-call(bf16[3,1024,256]{2,1,0:T(8,128)(2,1)S(1)} %get-tuple-element.133.proj.query, f32[16,512]{1,0:T(8,128)S(1)} %get-tuple-element.126.encoded, f32[1,512]{1,0:T(1,128)S(1)} %bitcast.50, ...), custom_call_target="tpu_custom_call" | custom-call | tf_op jit(solution)/shard_map/attend_first/pallas_call | solution.py:286
  69.9 6.7 %collective-permute-done.11.refs_3_ = bf16[1,128,1024]{2,1,0:T(8,128)(2,1)S(1)} collective-permute-done((bf16[1,128,1024]{2,1,0:T(8,128)(2,1)S(1)}, bf16[1,128,1024]{2,1,0:T(8,128)(2,1)S(1)}, u32[]{:S(2)}, u32[]{:S(2)}) %collective-permute-start.11) | collective-permute-done | bytes 262176 | tf_op jit(solution)/shard_map/ppermute | solution.py:84
  78.5 5.7 %attend_second.1 = (bf16[512,256]{1,0:T(8,128)(2,1)S(1)}, f32[512,128]{1,0:T(8,128)S(1)}) custom-call(bf16[3,1024,256]{2,1,0:T(8,128)(2,1)S(1)} %get-tuple-element.133.proj.query, bf16[2,16,256]{2,1,0:T(8,128)(2,1)S(1)} %get-tuple-element.134.prefix), custom_call_target="tpu_custom_call" | custom-call | tf_op jit(solution)/shard_map/attend_second/pallas_call | solution.py:299
  84.8 6.5 %collective-permute-done.15.refs_4_ = bf16[2,128,1024]{2,1,0:T(8,128)(2,1)S(1)} collective-permute-done((bf16[2,128,1024]{2,1,0:T(8,128)(2,1)S(1)}, bf16[2,128,1024]{2,1,0:T(8,128)(2,1)S(1)}, u32[]{:S(2)}, u32[]{:S(2)}) %collective-permute-start.15) | collective-permute-done | bytes 524320 | tf_op jit(solution)/shard_map/ppermute | solution.py:84
  96.3 3.4 %collective-permute-start.20 = (bf16[128,512]{1,0:T(8,128)(2,1)S(1)}, bf16[128,512]{1,0:T(8,128)(2,1)S(1)}, u32[]{:S(2)}, u32[]{:S(2)}) collective-permute-start(bf16[128,512]{1,0:T(8,128)(2,1)S(1)} %convert_element_type.19), channel_id=1, source_target_pairs={{0,16},{4,20},{8,24},{12,28},{16,0},{20,4},{24,8},{28,12},{1,17},{... | collective-permute-start | bytes 393224 | tf_op jit(solution)/shard_map/ppermute | solution.py:84
  99.7 2.5 %down_back.1 = (bf16[1,1024,1024]{2,1,0:T(8,128)(2,1)S(1)}, bf16[1024,1024]{1,0:T(8,128)(2,1)S(1)}) custom-call(bf16[1024,1024]{1,0:T(8,128)(2,1)S(1)} %copy-done.1, bf16[2,128,1024]{2,1,0:T(8,128)(2,1)S(1)} %pad_maximum_fusion.2.refs_0_, bf16[2,128,1024]{2,1,0:T(8,128)(2,1)S(1)} %collective-permute-done.13.refs_1_, ...), custom_call_target="tpu_custom_call" | custom-call | tf_op jit(solution)/shard_map/down_back/pallas_call | solution.py:209
  102.3 2.4 %merge_second.1 = (bf16[1024,1024]{1,0:T(8,128)(2,1)S(1)}, f32[256,1024]{1,0:T(8,128)S(1)}) custom-call(bf16[1024,1024]{1,0:T(8,128)(2,1)S(1)} %copy-done, f32[4,1024]{1,0:T(4,128)S(1)} %copy-done.5, f32[2,1024]{1,0:T(2,128)S(1)} %copy-done.11, bf16[512,256]{1,0:T(8,128)(2,1)S(1)} %get-tuple-element.135.refs_0_.mix_second, ...), custom_call_target="tpu_custom_call", output_to_operand_aliasing={{0}: (11, {})} | custom-call | tf_op jit(solution)/shard_map/merge_second/pallas_call | solution.py:486
  121.7 5.0 %collective-permute-done.25.side = bf16[256,1024]{1,0:T(8,128)(2,1)S(1)} collective-permute-done((bf16[256,1024]{1,0:T(8,128)(2,1)S(1)}, bf16[256,1024]{1,0:T(8,128)(2,1)S(1)}, u32[]{:S(2)}, u32[]{:S(2)}) %collective-permute-start.25) | collective-permute-done | bytes 524320 | tf_op jit(solution)/shard_map/ppermute | solution.py:84
  128.8 2.7 %collective-permute-done.30.refs_1_ = bf16[4,128,512]{2,1,0:T(8,128)(2,1)S(1)} collective-permute-done((bf16[4,128,512]{2,1,0:T(8,128)(2,1)S(1)}, bf16[4,128,512]{2,1,0:T(8,128)(2,1)S(1)}, u32[]{:S(2)}, u32[]{:S(2)}) %collective-permute-start.30) | collective-permute-done | bytes 524320 | tf_op jit(solution)/shard_map/ppermute | solution.py:84
  132.4 3.3 %collective-permute-done.29.side = bf16[2,256,256]{2,1,0:T(8,128)(2,1)S(1)} collective-permute-done((bf16[2,256,256]{2,1,0:T(8,128)(2,1)S(1)}, bf16[2,256,256]{2,1,0:T(8,128)(2,1)S(1)}, u32[]{:S(2)}, u32[]{:S(2)}) %collective-permute-start.29) | collective-permute-done | bytes 262176 | tf_op jit(solution)/shard_map/ppermute | solution.py:84
  140.8 5.7 %attend_back.2.one = bf16[3,1024,128]{2,1,0:T(8,128)(2,1)S(1)} custom-call(bf16[3,1024,256]{2,1,0:T(8,128)(2,1)S(1)} %get-tuple-element.133.proj.query, bf16[1024,256]{1,0:T(8,128)(2,1)S(1)} %get-tuple-element.189.gmix, f32[8,1024]{1,0:T(8,128)S(1)} %get-tuple-element.185.log_sums, f32[8,1024]{1,0:T(8,128)S(1)} %get-tuple-element.186.inner, ...), custom_call_target="tpu_custom_call" | custom-call | flops 1610612736 | bytes 3932160 | tf_op jit(solution)/shard_map/attend_back/pallas_call | solution.py:428
  147.5 5.7 %attend_back.3.two = bf16[3,1024,128]{2,1,0:T(8,128)(2,1)S(1)} custom-call(bf16[3,1024,256]{2,1,0:T(8,128)(2,1)S(1)} %get-tuple-element.133.proj.query, bf16[1024,256]{1,0:T(8,128)(2,1)S(1)} %get-tuple-element.189.gmix, f32[8,1024]{1,0:T(8,128)S(1)} %get-tuple-element.185.log_sums, f32[8,1024]{1,0:T(8,128)S(1)} %get-tuple-element.186.inner, ...), custom_call_target="tpu_custom_call" | custom-call | flops 1610612736 | bytes 3932160 | tf_op jit(solution)/shard_map/attend_back/pallas_call | solution.py:428
  157.6 2.8 %collective-permute-start.38 = (f32[2,16,256]{2,1,0:T(8,128)S(1)}, f32[2,16,256]{2,1,0:T(8,128)S(1)}, u32[]{:S(2)}, u32[]{:S(2)}) collective-permute-start(f32[2,16,256]{2,1,0:T(8,128)S(1)} %plus.4.one), channel_id=1, source_target_pairs={{0,16},{4,20},{8,24},{12,28},{16,0},{20,4},{24,8},{28,12},{1,17},{... | collective-permute-start | bytes 98312 | tf_op jit(solution)/shard_map/ppermute | solution.py:84
  160.3 2.4 %collective-permute-done.38.two = f32[2,16,256]{2,1,0:T(8,128)S(1)} collective-permute-done((f32[2,16,256]{2,1,0:T(8,128)S(1)}, f32[2,16,256]{2,1,0:T(8,128)S(1)}, u32[]{:S(2)}, u32[]{:S(2)}) %collective-permute-start.38) | collective-permute-done | bytes 32800 | tf_op jit(solution)/shard_map/ppermute | solution.py:84
  166.6 4.3 %collective-permute-done.37.side = bf16[256,1024]{1,0:T(8,128)(2,1)S(1)} collective-permute-done((bf16[256,1024]{1,0:T(8,128)(2,1)S(1)}, bf16[256,1024]{1,0:T(8,128)(2,1)S(1)}, u32[]{:S(2)}, u32[]{:S(2)}) %collective-permute-start.37) | collective-permute-done | bytes 524320 | tf_op jit(solution)/shard_map/ppermute | solution.py:84
  172.7 2.6 %update.1 = (f32[1,1]{1,0:T(1,128)}, f32[10,1024]{1,0:T(8,128)}, f32[10,1024]{1,0:T(8,128)}, f32[10,1024]{1,0:T(8,128)}, f32[128,512]{1,0:T(8,128)}, /*index=5*/...) custom-call(f32[16,512]{1,0:T(8,128)S(1)} %plus.5.joint_one, ...), custom_call_target="tpu_custom_call" | custom-call | tf_op jit(solution)/shard_map/update/pallas_call | solution.py:1029
  (156 shorter events, 70.5 us)
Async XLA Ops:
  2.8 16.2 %collective-permute-start.1 = (bf16[512,256]{1,0:T(8,128)(2,1)S(1)}, bf16[512,256]{1,0:T(8,128)(2,1)}, u32[]{:S(2)}, u32[]{:S(2)}) collective-permute-start(bf16[512,256]{1,0:T(8,128)(2,1)S(1)} %get-tuple-element.215), channel_id=1, source_target_pairs={{0,16},{4,20},{8,24},{12,28},{16,0},{20,4},{24,8},{28,12},{1,17},{... | collective-permute-start | bytes 786440 | tf_op jit(solution)/shard_map/ppermute | solution.py:84
  6.9 12.0 %collective-permute-start.2 = (bf16[128,1024]{1,0:T(8,128)(2,1)}, bf16[128,1024]{1,0:T(8,128)(2,1)S(1)}, u32[]{:S(2)}, u32[]{:S(2)}) collective-permute-start(bf16[128,1024]{1,0:T(8,128)(2,1)} %param.33), channel_id=1, source_target_pairs={{0,4},{4,0},{8,12},{12,8},{16,20},{20,16},{24,28},{28,24},{1,5},{5... | collective-permute-start | bytes 786440 | tf_op jit(solution)/shard_map/ppermute | solution.py:84
  20.0 16.7 %collective-permute-start.5 = (bf16[2,512,256]{2,1,0:T(8,128)(2,1)S(1)}, bf16[2,512,256]{2,1,0:T(8,128)(2,1)S(1)}, u32[]{:S(2)}, u32[]{:S(2)}) collective-permute-start(bf16[2,512,256]{2,1,0:T(8,128)(2,1)S(1)} %pad_maximum_fusion.1.refs_0_), channel_id=1, source_target_pairs={{0,8},{4,12},{8,0},{12,4},{16,24},{20,28},{24,16},{28,20},{1,9},{5... | collective-permute-start | bytes 1572872 | tf_op jit(solution)/shard_map/ppermute | solution.py:84
  20.7 17.3 %collective-permute-start.3 = (bf16[2,160,256]{2,1,0:T(8,128)(2,1)S(1)}, bf16[2,160,256]{2,1,0:T(8,128)(2,1)S(1)}, u32[]{:S(2)}, u32[]{:S(2)}) collective-permute-start(bf16[2,160,256]{2,1,0:T(8,128)(2,1)S(1)} %pad_maximum_fusion.9), channel_id=1, source_target_pairs={{0,16},{4,20},{8,24},{12,28},{16,0},{20,4},{24,8},{28,12},{1,17},{... | collective-permute-start | bytes 491528 | tf_op jit(solution)/shard_map/ppermute | solution.py:84
  24.2 18.9 %collective-permute-start.6 = (bf16[2,512,256]{2,1,0:T(8,128)(2,1)S(1)}, bf16[2,512,256]{2,1,0:T(8,128)(2,1)S(1)}, u32[]{:S(2)}, u32[]{:S(2)}) collective-permute-start(bf16[2,512,256]{2,1,0:T(8,128)(2,1)S(1)} %pad_maximum_fusion.1.refs_0_), channel_id=1, source_target_pairs={{0,4},{4,0},{8,12},{12,8},{16,20},{20,16},{24,28},{28,24},{1,5},{5... | collective-permute-start | bytes 1572872 | tf_op jit(solution)/shard_map/ppermute | solution.py:84
  36.6 12.2 %collective-permute-start.7 = (bf16[2,512,256]{2,1,0:T(8,128)(2,1)S(1)}, bf16[2,512,256]{2,1,0:T(8,128)(2,1)S(1)}, u32[]{:S(2)}, u32[]{:S(2)}) collective-permute-start(bf16[2,512,256]{2,1,0:T(8,128)(2,1)S(1)} %collective-permute-done.5.refs_1_), channel_id=1, source_target_pairs={{0,4},{4,0},{8,12},{12,8},{16,20},{20,16},{24,28},{28,24},{1,5},{5... | collective-permute-start | bytes 1572872 | tf_op jit(solution)/shard_map/ppermute | solution.py:84
  38.0 14.8 %collective-permute-start.4 = (bf16[4,160,256]{2,1,0:T(8,128)(2,1)S(1)}, bf16[4,160,256]{2,1,0:T(8,128)(2,1)S(1)}, u32[]{:S(2)}, u32[]{:S(2)}) collective-permute-start(bf16[4,160,256]{2,1,0:T(8,128)(2,1)S(1)} %pad_maximum_fusion.6.refs_0_), channel_id=1, source_target_pairs={{0,8},{4,12},{8,0},{12,4},{16,24},{20,28},{24,16},{28,20},{1,9},{5... | collective-permute-start | bytes 983048 | tf_op jit(solution)/shard_map/ppermute | solution.py:84
  39.9 12.9 %collective-permute-start.8 = (bf16[128,1024]{1,0:T(8,128)(2,1)S(1)}, bf16[128,1024]{1,0:T(8,128)(2,1)S(1)}, u32[]{:S(2)}, u32[]{:S(2)}) collective-permute-start(bf16[128,1024]{1,0:T(8,128)(2,1)S(1)} %copy-done.22), channel_id=1, source_target_pairs={{0,16},{4,20},{8,24},{12,28},{16,0},{20,4},{24,8},{28,12},{1,17},{... | collective-permute-start | bytes 786440 | tf_op jit(solution)/shard_map/ppermute | solution.py:84
  52.9 17.0 %collective-permute-start.9 = (bf16[1024,256]{1,0:T(8,128)(2,1)S(1)}, bf16[1024,256]{1,0:T(8,128)(2,1)S(1)}, u32[]{:S(2)}, u32[]{:S(2)}) collective-permute-start(bf16[1024,256]{1,0:T(8,128)(2,1)S(1)} %get-tuple-element.125.refs_4_.refs_0_), channel_id=1, source_target_pairs={{0,2},{1,3},{2,0},{3,1},{4,6},{5,7},{6,4},{7,5},{8,10},{9,11},{10,... | collective-permute-start | bytes 1572872 | tf_op jit(solution)/shard_map/ppermute | solution.py:84
  54.4 13.1 %collective-permute-start.10 = (bf16[128,1024]{1,0:T(8,128)(2,1)S(1)}, bf16[128,1024]{1,0:T(8,128)(2,1)S(1)}, u32[]{:S(2)}, u32[]{:S(2)}) collective-permute-start(bf16[128,1024]{1,0:T(8,128)(2,1)S(1)} %copy-done.3), channel_id=1, source_target_pairs={{0,16},{4,20},{8,24},{12,28},{16,0},{20,4},{24,8},{28,12},{1,17},{... | collective-permute-start | bytes 786440 | tf_op jit(solution)/shard_map/ppermute | solution.py:84
  57.1 19.5 %collective-permute-start.12 = (bf16[2,128,1024]{2,1,0:T(8,128)(2,1)S(1)}, bf16[2,128,1024]{2,1,0:T(8,128)(2,1)S(1)}, u32[]{:S(2)}, u32[]{:S(2)}) collective-permute-start(bf16[2,128,1024]{2,1,0:T(8,128)(2,1)S(1)} %pad_maximum_fusion.2.refs_0_), channel_id=1, source_target_pairs={{0,8},{4,12},{8,0},{12,4},{16,24},{20,28},{24,16},{28,20},{1,9},{5... | collective-permute-start | bytes 1572872 | tf_op jit(solution)/shard_map/ppermute | solution.py:84
  59.0 17.6 %collective-permute-start.13 = (bf16[2,128,1024]{2,1,0:T(8,128)(2,1)S(1)}, bf16[2,128,1024]{2,1,0:T(8,128)(2,1)S(1)}, u32[]{:S(2)}, u32[]{:S(2)}) collective-permute-start(bf16[2,128,1024]{2,1,0:T(8,128)(2,1)S(1)} %pad_maximum_fusion.2.refs_0_), channel_id=1, source_target_pairs={{0,4},{4,0},{8,12},{12,8},{16,20},{20,16},{24,28},{28,24},{1,5},{5... | collective-permute-start | bytes 1572872 | tf_op jit(solution)/shard_map/ppermute | solution.py:84
  76.8 17.4 %collective-permute-start.18 = (bf16[3072,256]{1,0:T(8,128)(2,1)S(1)}, bf16[3072,256]{1,0:T(8,128)(2,1)S(1)}, u32[]{:S(2)}, u32[]{:S(2)}) collective-permute-start(bf16[3072,256]{1,0:T(8,128)(2,1)S(1)} %pad_maximum_fusion), channel_id=1, source_target_pairs={{0,1},{1,0},{2,3},{3,2},{4,5},{5,4},{6,7},{7,6},{8,9},{9,8},{10,11... | collective-permute-start | bytes 4718600 | tf_op jit(solution)/shard_map/ppermute | solution.py:84
  76.9 14.4 %collective-permute-start.15 = (bf16[2,128,1024]{2,1,0:T(8,128)(2,1)S(1)}, bf16[2,128,1024]{2,1,0:T(8,128)(2,1)S(1)}, u32[]{:S(2)}, u32[]{:S(2)}) collective-permute-start(bf16[2,128,1024]{2,1,0:T(8,128)(2,1)S(1)} %pad_maximum_fusion.3), channel_id=1, source_target_pairs={{0,8},{4,12},{8,0},{12,4},{16,24},{20,28},{24,16},{28,20},{1,9},{5... | collective-permute-start | bytes 1572872 | tf_op jit(solution)/shard_map/ppermute | solution.py:84
  78.0 14.4 %collective-permute-start.14 = (bf16[2,128,1024]{2,1,0:T(8,128)(2,1)S(1)}, bf16[2,128,1024]{2,1,0:T(8,128)(2,1)S(1)}, u32[]{:S(2)}, u32[]{:S(2)}) collective-permute-start(bf16[2,128,1024]{2,1,0:T(8,128)(2,1)S(1)} %collective-permute-done.12.refs_2_), channel_id=1, source_target_pairs={{0,4},{4,0},{8,12},{12,8},{16,20},{20,16},{24,28},{28,24},{1,5},{5... | collective-permute-start | bytes 1572872 | tf_op jit(solution)/shard_map/ppermute | solution.py:84
  92.5 14.3 %collective-permute-start.21 = (bf16[2,128,1024]{2,1,0:T(8,128)(2,1)S(1)}, bf16[2,128,1024]{2,1,0:T(8,128)(2,1)S(1)}, u32[]{:S(2)}, u32[]{:S(2)}) collective-permute-start(bf16[2,128,1024]{2,1,0:T(8,128)(2,1)S(1)} %collective-permute-done.15.refs_4_), channel_id=1, source_target_pairs={{0,4},{4,0},{8,12},{12,8},{16,20},{20,16},{24,28},{28,24},{1,5},{5... | collective-permute-start | bytes 1572872 | tf_op jit(solution)/shard_map/ppermute | solution.py:84
  112.7 14.0 %collective-permute-start.25 = (bf16[256,1024]{1,0:T(8,128)(2,1)S(1)}, bf16[256,1024]{1,0:T(8,128)(2,1)S(1)}, u32[]{:S(2)}, u32[]{:S(2)}) collective-permute-start(bf16[256,1024]{1,0:T(8,128)(2,1)S(1)} %get-tuple-element.156), channel_id=1, source_target_pairs={{0,2},{1,3},{2,0},{3,1},{4,6},{5,7},{6,4},{7,5},{8,10},{9,11},{10,... | collective-permute-start | bytes 1572872 | tf_op jit(solution)/shard_map/ppermute | solution.py:84
  115.1 11.6 %collective-permute-start.24 = (bf16[256,1024]{1,0:T(8,128)(2,1)S(1)}, bf16[256,1024]{1,0:T(8,128)(2,1)S(1)}, u32[]{:S(2)}, u32[]{:S(2)}) collective-permute-start(bf16[256,1024]{1,0:T(8,128)(2,1)S(1)} %get-tuple-element.165), channel_id=1, source_target_pairs={{0,1},{1,0},{2,3},{3,2},{4,5},{5,4},{6,7},{7,6},{8,9},{9,8},{10,11... | collective-permute-start | bytes 1572872 | tf_op jit(solution)/shard_map/ppermute | solution.py:84
  117.8 13.7 %collective-permute-start.30 = (bf16[4,128,512]{2,1,0:T(8,128)(2,1)S(1)}, bf16[4,128,512]{2,1,0:T(8,128)(2,1)S(1)}, u32[]{:S(2)}, u32[]{:S(2)}) collective-permute-start(bf16[4,128,512]{2,1,0:T(8,128)(2,1)S(1)} %pad_maximum_fusion.5.refs_0_), channel_id=1, source_target_pairs={{0,4},{4,0},{8,12},{12,8},{16,20},{20,16},{24,28},{28,24},{1,5},{5... | collective-permute-start | bytes 1572872 | tf_op jit(solution)/shard_map/ppermute | solution.py:84
  120.2 11.4 %collective-permute-start.27 = (bf16[256,1024]{1,0:T(8,128)(2,1)S(1)}, bf16[256,1024]{1,0:T(8,128)(2,1)S(1)}, u32[]{:S(2)}, u32[]{:S(2)}) collective-permute-start(bf16[256,1024]{1,0:T(8,128)(2,1)S(1)} %down_rows.6), channel_id=1, source_target_pairs={{0,1},{1,0},{2,3},{3,2},{4,5},{5,4},{6,7},{7,6},{8,9},{9,8},{10,11... | collective-permute-start | bytes 1572872 | tf_op jit(solution)/shard_map/ppermute | solution.py:84
  135.7 17.5 %collective-permute-start.23 = (bf16[256,1024]{1,0:T(8,128)(2,1)S(1)}, bf16[256,1024]{1,0:T(8,128)(2,1)S(1)}, u32[]{:S(2)}, u32[]{:S(2)}) collective-permute-start(bf16[256,1024]{1,0:T(8,128)(2,1)S(1)} %down_rows.5), channel_id=1, source_target_pairs={{0,1},{1,0},{2,3},{3,2},{4,5},{5,4},{6,7},{7,6},{8,9},{9,8},{10,11... | collective-permute-start | bytes 1572872 | tf_op jit(solution)/shard_map/ppermute | solution.py:84
  136.3 17.0 %collective-permute-start.28 = (bf16[256,1024]{1,0:T(8,128)(2,1)S(1)}, bf16[256,1024]{1,0:T(8,128)(2,1)S(1)}, u32[]{:S(2)}, u32[]{:S(2)}) collective-permute-start(bf16[256,1024]{1,0:T(8,128)(2,1)S(1)} %down_rows.7), channel_id=1, source_target_pairs={{0,2},{1,3},{2,0},{3,1},{4,6},{5,7},{6,4},{7,5},{8,10},{9,11},{10,... | collective-permute-start | bytes 1572872 | tf_op jit(solution)/shard_map/ppermute | solution.py:84
  155.4 15.5 %collective-permute-start.35 = (bf16[512,1024]{1,0:T(8,128)(2,1)S(1)}, bf16[512,1024]{1,0:T(8,128)(2,1)S(1)}, u32[]{:S(2)}, u32[]{:S(2)}) collective-permute-start(bf16[512,1024]{1,0:T(8,128)(2,1)S(1)} %project_back.3.own), channel_id=1, source_target_pairs={{0,1},{1,0},{2,3},{3,2},{4,5},{5,4},{6,7},{7,6},{8,9},{9,8},{10,11... | collective-permute-start | bytes 3145736 | tf_op jit(solution)/shard_map/ppermute | solution.py:84
  156.5 14.4 %collective-permute-start.37 = (bf16[256,1024]{1,0:T(8,128)(2,1)S(1)}, bf16[256,1024]{1,0:T(8,128)(2,1)S(1)}, u32[]{:S(2)}, u32[]{:S(2)}) collective-permute-start(bf16[256,1024]{1,0:T(8,128)(2,1)S(1)} %project_back.5), channel_id=1, source_target_pairs={{0,2},{1,3},{2,0},{3,1},{4,6},{5,7},{6,4},{7,5},{8,10},{9,11},{10,... | collective-permute-start | bytes 1572872 | tf_op jit(solution)/shard_map/ppermute | solution.py:84
  (40 other events, 402.2 us)

commit v6 on v5

--- a/solution.py
+++ b/solution.py
@@ -989,18 +989,18 @@
     grad_second = attend_back(
         1, projected, after(grad_mix, prefix_total), log_sums, inner, grad_query
     )
-    prefix_total = plus(prefix_total, swap(prefix_total, "dp", 2))
-    gprojs = after((grad_first, grad_second), prefix_total, out_from, out_core)
+    gprojs = after((grad_first, grad_second), out_from, out_core)
     back_both = swap(project_back((BOTH,), gprojs, attend_full), "tensor", CORE)
     back_rest = project_back((CORE, OWN), gprojs, attend_full)
     back_both = after(back_both, back_rest)
     back_send = project_back((SIDE,), gprojs, attend_full, back_both)
     back_from = swap(back_send, "tensor", SIDE)
+    prefix_total = plus(prefix_total, after(swap(prefix_total, "dp", 2), back_send))
     bits = 4
     while bits < lax.axis_size("dp") // 2:
         prefix_total = plus(prefix_total, swap(prefix_total, "dp", bits))
         bits *= 2
-    prefix_rest = after(swap(prefix_total, "dp", bits), back_send)
+    prefix_rest = swap(prefix_total, "dp", bits)
     prefix_total, joint = pl.pallas_call(
         tail_kernel,
         out_shape=(

time: 176 us -> 175 us (level)
  transfers between devices with their start and end apart: 41 -> 41, of which waited for: 20 -> 21; matrix products, arithmetic and copies ran while one was open for 3% -> 3% of each run, Pallas kernels for 28% -> 28%
where the time goes in v6:
time: 175 us
  waiting for transfers between devices  61.3 us (35%)
  Pallas kernels  54.2 us (31%)
  starting transfers between devices  49.6 us (28%)
  other arithmetic  5.99 us (3%)
    ppermute x41, waiting for transfers between devices, swap(): return lax.ppermute(values, axis, [(i, i ^ bits) for i in range(size)])  61.3 us
    ppermute x41, starting transfers between devices, swap(): return lax.ppermute(values, axis, [(i, i ^ bits) for i in range(size)])  49.6 us
    pallas_call x2, Pallas kernels, attend_back(): pl.pallas_call(functools.partial(attend_back_kernel, pair), grid=(1,), in...  11.4 us
    pallas_call x1, Pallas kernels, attend_second(): pl.pallas_call(functools.partial(attend_kernel, rows // 2), out_shape=out...  5.66 us
    pallas_call x3, Pallas kernels, feed(): pl.pallas_call(feed_kernel, grid=(1,), in_specs=[whole_spec(up), whole_sp...  5.5 us
    pallas_call x1, Pallas kernels, attend_first(): pl.pallas_call(attend_first_kernel, out_shape=outs, scratch_shapes=[pltpu...  4.9 us
    pallas_call x2, Pallas kernels, merge_half(): pl.pallas_call(functools.partial(merge_kernel, first), grid=(steps,), in_...  4.58 us
  transfers between devices with their start and end apart: 41, of which 21 were waited for; matrix products, arithmetic and copies ran while one was open for 3% of the time, Pallas kernels for 28%

profile of v6, /device:TPU:0, one launch (start us, length us, event | category | flops | bytes accessed | tf_op | source)
XLA Modules:
  0.0 174.6 jit_solution(11097847675431498440)
XLA Ops:
  2.8 4.1 %collective-permute-start.1 = (bf16[512,256]{1,0:T(8,128)(2,1)S(1)}, bf16[512,256]{1,0:T(8,128)(2,1)}, u32[]{:S(2)}, u32[]{:S(2)}) collective-permute-start(bf16[512,256]{1,0:T(8,128)(2,1)S(1)} %get-tuple-element.215), channel_id=1, source_target_pairs={{0,16},{4,20},{8,24},{12,28},{16,0},{20,4},{24,8},{28,12},{1,17},{... | collective-permute-start | bytes 786440 | tf_op jit(solution)/shard_map/ppermute | solution.py:84
  13.3 4.1 %collective-permute-done = bf16[160,256]{1,0:T(8,128)(2,1)S(1)} collective-permute-done((bf16[160,256]{1,0:T(8,128)(2,1)}, bf16[160,256]{1,0:T(8,128)(2,1)S(1)}, u32[]{:S(2)}, u32[]{:S(2)}) %collective-permute-start) | collective-permute-done | bytes 81952 | tf_op jit(solution)/shard_map/ppermute | solution.py:84
  20.7 3.6 %collective-permute-start.3 = (bf16[2,160,256]{2,1,0:T(8,128)(2,1)S(1)}, bf16[2,160,256]{2,1,0:T(8,128)(2,1)S(1)}, u32[]{:S(2)}, u32[]{:S(2)}) collective-permute-start(bf16[2,160,256]{2,1,0:T(8,128)(2,1)S(1)} %pad_maximum_fusion.9), channel_id=1, source_target_pairs={{0,16},{4,20},{8,24},{12,28},{16,0},{20,4},{24,8},{28,12},{1,17},{... | collective-permute-start | bytes 491528 | tf_op jit(solution)/shard_map/ppermute | solution.py:84
  25.7 10.9 %collective-permute-done.5.refs_1_ = bf16[2,512,256]{2,1,0:T(8,128)(2,1)S(1)} collective-permute-done((bf16[2,512,256]{2,1,0:T(8,128)(2,1)S(1)}, bf16[2,512,256]{2,1,0:T(8,128)(2,1)S(1)}, u32[]{:S(2)}, u32[]{:S(2)}) %collective-permute-start.5) | collective-permute-done | bytes 524320 | tf_op jit(solution)/shard_map/ppermute | solution.py:84
  39.9 3.3 %collective-permute-start.8 = (bf16[128,1024]{1,0:T(8,128)(2,1)S(1)}, bf16[128,1024]{1,0:T(8,128)(2,1)S(1)}, u32[]{:S(2)}, u32[]{:S(2)}) collective-permute-start(bf16[128,1024]{1,0:T(8,128)(2,1)S(1)} %copy-done.22), channel_id=1, source_target_pairs={{0,16},{4,20},{8,24},{12,28},{16,0},{20,4},{24,8},{28,12},{1,17},{... | collective-permute-start | bytes 786440 | tf_op jit(solution)/shard_map/ppermute | solution.py:84
  43.1 5.7 %collective-permute-done.7.refs_3_ = bf16[2,512,256]{2,1,0:T(8,128)(2,1)S(1)} collective-permute-done((bf16[2,512,256]{2,1,0:T(8,128)(2,1)S(1)}, bf16[2,512,256]{2,1,0:T(8,128)(2,1)S(1)}, u32[]{:S(2)}, u32[]{:S(2)}) %collective-permute-start.7) | collective-permute-done | bytes 524320 | tf_op jit(solution)/shard_map/ppermute | solution.py:84
  48.9 2.7 %project.1 = (bf16[3,1024,256]{2,1,0:T(8,128)(2,1)S(1)}, bf16[3,1024,256]{2,1,0:T(8,128)(2,1)S(1)}, bf16[2,512,256]{2,1,0:T(8,128)(2,1)S(1)}) custom-call(bf16[1024,1024]{1,0:T(8,128)(2,1)S(1)} %copy-done, f32[4,1024]{1,0:T(4,128)S(1)} %copy-done.5, f32[3,256]{1,0:T(4,128)S(1)} %copy-done.17, bf16[2,512,256]{2,1,0:T(8,128)(2,1)S(1)} %pad_maximum_fusion.1.refs_0_, ...), custom_call_target="tpu_custom_call" | custom-call | tf_op jit(solution)/shard_map/project/pallas_call | solution.py:187
  54.4 2.6 %collective-permute-start.10 = (bf16[128,1024]{1,0:T(8,128)(2,1)S(1)}, bf16[128,1024]{1,0:T(8,128)(2,1)S(1)}, u32[]{:S(2)}, u32[]{:S(2)}) collective-permute-start(bf16[128,1024]{1,0:T(8,128)(2,1)S(1)} %copy-done.3), channel_id=1, source_target_pairs={{0,16},{4,20},{8,24},{12,28},{16,0},{20,4},{24,8},{28,12},{1,17},{... | collective-permute-start | bytes 786440 | tf_op jit(solution)/shard_map/ppermute | solution.py:84
  60.5 4.9 %attend_first.1 = (bf16[512,256]{1,0:T(8,128)(2,1)S(1)}, f32[512,128]{1,0:T(8,128)S(1)}, f32[16,512]{1,0:T(8,128)S(1)}, bf16[2,16,256]{2,1,0:T(8,128)(2,1)S(1)}) custom-call(bf16[3,1024,256]{2,1,0:T(8,128)(2,1)S(1)} %get-tuple-element.133.proj.query, f32[16,512]{1,0:T(8,128)S(1)} %get-tuple-element.126.encoded, f32[1,512]{1,0:T(1,128)S(1)} %bitcast.50, ...), custom_call_target="tpu_custom_call" | custom-call | tf_op jit(solution)/shard_map/attend_first/pallas_call | solution.py:286
  69.9 6.7 %collective-permute-done.11.refs_3_ = bf16[1,128,1024]{2,1,0:T(8,128)(2,1)S(1)} collective-permute-done((bf16[1,128,1024]{2,1,0:T(8,128)(2,1)S(1)}, bf16[1,128,1024]{2,1,0:T(8,128)(2,1)S(1)}, u32[]{:S(2)}, u32[]{:S(2)}) %collective-permute-start.11) | collective-permute-done | bytes 262176 | tf_op jit(solution)/shard_map/ppermute | solution.py:84
  78.5 5.7 %attend_second.1 = (bf16[512,256]{1,0:T(8,128)(2,1)S(1)}, f32[512,128]{1,0:T(8,128)S(1)}) custom-call(bf16[3,1024,256]{2,1,0:T(8,128)(2,1)S(1)} %get-tuple-element.133.proj.query, bf16[2,16,256]{2,1,0:T(8,128)(2,1)S(1)} %get-tuple-element.134.prefix), custom_call_target="tpu_custom_call" | custom-call | tf_op jit(solution)/shard_map/attend_second/pallas_call | solution.py:299
  84.8 6.5 %collective-permute-done.15.refs_4_ = bf16[2,128,1024]{2,1,0:T(8,128)(2,1)S(1)} collective-permute-done((bf16[2,128,1024]{2,1,0:T(8,128)(2,1)S(1)}, bf16[2,128,1024]{2,1,0:T(8,128)(2,1)S(1)}, u32[]{:S(2)}, u32[]{:S(2)}) %collective-permute-start.15) | collective-permute-done | bytes 524320 | tf_op jit(solution)/shard_map/ppermute | solution.py:84
  96.3 3.4 %collective-permute-start.20 = (bf16[128,512]{1,0:T(8,128)(2,1)S(1)}, bf16[128,512]{1,0:T(8,128)(2,1)S(1)}, u32[]{:S(2)}, u32[]{:S(2)}) collective-permute-start(bf16[128,512]{1,0:T(8,128)(2,1)S(1)} %convert_element_type.19), channel_id=1, source_target_pairs={{0,16},{4,20},{8,24},{12,28},{16,0},{20,4},{24,8},{28,12},{1,17},{... | collective-permute-start | bytes 393224 | tf_op jit(solution)/shard_map/ppermute | solution.py:84
  99.7 2.5 %down_back.1 = (bf16[1,1024,1024]{2,1,0:T(8,128)(2,1)S(1)}, bf16[1024,1024]{1,0:T(8,128)(2,1)S(1)}) custom-call(bf16[1024,1024]{1,0:T(8,128)(2,1)S(1)} %copy-done.1, bf16[2,128,1024]{2,1,0:T(8,128)(2,1)S(1)} %pad_maximum_fusion.2.refs_0_, bf16[2,128,1024]{2,1,0:T(8,128)(2,1)S(1)} %collective-permute-done.13.refs_1_, ...), custom_call_target="tpu_custom_call" | custom-call | tf_op jit(solution)/shard_map/down_back/pallas_call | solution.py:209
  102.3 2.4 %merge_second.1 = (bf16[1024,1024]{1,0:T(8,128)(2,1)S(1)}, f32[256,1024]{1,0:T(8,128)S(1)}) custom-call(bf16[1024,1024]{1,0:T(8,128)(2,1)S(1)} %copy-done, f32[4,1024]{1,0:T(4,128)S(1)} %copy-done.5, f32[2,1024]{1,0:T(2,128)S(1)} %copy-done.11, bf16[512,256]{1,0:T(8,128)(2,1)S(1)} %get-tuple-element.135.refs_0_.mix_second, ...), custom_call_target="tpu_custom_call", output_to_operand_aliasing={{0}: (11, {})} | custom-call | tf_op jit(solution)/shard_map/merge_second/pallas_call | solution.py:486
  121.7 5.0 %collective-permute-done.25.side = bf16[256,1024]{1,0:T(8,128)(2,1)S(1)} collective-permute-done((bf16[256,1024]{1,0:T(8,128)(2,1)S(1)}, bf16[256,1024]{1,0:T(8,128)(2,1)S(1)}, u32[]{:S(2)}, u32[]{:S(2)}) %collective-permute-start.25) | collective-permute-done | bytes 524320 | tf_op jit(solution)/shard_map/ppermute | solution.py:84
  128.8 2.7 %collective-permute-done.30.refs_1_ = bf16[4,128,512]{2,1,0:T(8,128)(2,1)S(1)} collective-permute-done((bf16[4,128,512]{2,1,0:T(8,128)(2,1)S(1)}, bf16[4,128,512]{2,1,0:T(8,128)(2,1)S(1)}, u32[]{:S(2)}, u32[]{:S(2)}) %collective-permute-start.30) | collective-permute-done | bytes 524320 | tf_op jit(solution)/shard_map/ppermute | solution.py:84
  132.4 3.3 %collective-permute-done.29.side = bf16[2,256,256]{2,1,0:T(8,128)(2,1)S(1)} collective-permute-done((bf16[2,256,256]{2,1,0:T(8,128)(2,1)S(1)}, bf16[2,256,256]{2,1,0:T(8,128)(2,1)S(1)}, u32[]{:S(2)}, u32[]{:S(2)}) %collective-permute-start.29) | collective-permute-done | bytes 262176 | tf_op jit(solution)/shard_map/ppermute | solution.py:84
  140.8 5.7 %attend_back.2.one = bf16[3,1024,128]{2,1,0:T(8,128)(2,1)S(1)} custom-call(bf16[3,1024,256]{2,1,0:T(8,128)(2,1)S(1)} %get-tuple-element.133.proj.query, bf16[1024,256]{1,0:T(8,128)(2,1)S(1)} %get-tuple-element.189.gmix, f32[8,1024]{1,0:T(8,128)S(1)} %get-tuple-element.185.log_sums, f32[8,1024]{1,0:T(8,128)S(1)} %get-tuple-element.186.inner, ...), custom_call_target="tpu_custom_call" | custom-call | flops 1610612736 | bytes 3932160 | tf_op jit(solution)/shard_map/attend_back/pallas_call | solution.py:428
  146.5 5.7 %attend_back.3.two = bf16[3,1024,128]{2,1,0:T(8,128)(2,1)S(1)} custom-call(bf16[3,1024,256]{2,1,0:T(8,128)(2,1)S(1)} %get-tuple-element.133.proj.query, bf16[1024,256]{1,0:T(8,128)(2,1)S(1)} %get-tuple-element.189.gmix, f32[8,1024]{1,0:T(8,128)S(1)} %get-tuple-element.185.log_sums, f32[8,1024]{1,0:T(8,128)S(1)} %get-tuple-element.186.inner, ...), custom_call_target="tpu_custom_call" | custom-call | flops 1610612736 | bytes 3932160 | tf_op jit(solution)/shard_map/attend_back/pallas_call | solution.py:428
  157.5 2.9 %collective-permute-done.37.two = f32[2,16,256]{2,1,0:T(8,128)S(1)} collective-permute-done((f32[2,16,256]{2,1,0:T(8,128)S(1)}, f32[2,16,256]{2,1,0:T(8,128)S(1)}, u32[]{:S(2)}, u32[]{:S(2)}) %collective-permute-start.37) | collective-permute-done | bytes 32800 | tf_op jit(solution)/shard_map/ppermute | solution.py:84
  160.4 3.4 %collective-permute-start.38 = (f32[2,16,256]{2,1,0:T(8,128)S(1)}, f32[2,16,256]{2,1,0:T(8,128)S(1)}, u32[]{:S(2)}, u32[]{:S(2)}) collective-permute-start(f32[2,16,256]{2,1,0:T(8,128)S(1)} %plus.4.one), channel_id=1, source_target_pairs={{0,16},{4,20},{8,24},{12,28},{16,0},{20,4},{24,8},{28,12},{1,17},{... | collective-permute-start | bytes 98312 | tf_op jit(solution)/shard_map/ppermute | solution.py:84
  163.8 2.2 %collective-permute-done.38.two = f32[2,16,256]{2,1,0:T(8,128)S(1)} collective-permute-done((f32[2,16,256]{2,1,0:T(8,128)S(1)}, f32[2,16,256]{2,1,0:T(8,128)S(1)}, u32[]{:S(2)}, u32[]{:S(2)}) %collective-permute-start.38) | collective-permute-done | bytes 32800 | tf_op jit(solution)/shard_map/ppermute | solution.py:84
  171.8 2.6 %update.1 = (f32[1,1]{1,0:T(1,128)}, f32[10,1024]{1,0:T(8,128)}, f32[10,1024]{1,0:T(8,128)}, f32[10,1024]{1,0:T(8,128)}, f32[128,512]{1,0:T(8,128)}, /*index=5*/...) custom-call(f32[16,512]{1,0:T(8,128)S(1)} %plus.5.joint_one, ...), custom_call_target="tpu_custom_call" | custom-call | tf_op jit(solution)/shard_map/update/pallas_call | solution.py:1029
  (156 shorter events, 70.5 us)
Async XLA Ops:
  2.8 16.2 %collective-permute-start.1 = (bf16[512,256]{1,0:T(8,128)(2,1)S(1)}, bf16[512,256]{1,0:T(8,128)(2,1)}, u32[]{:S(2)}, u32[]{:S(2)}) collective-permute-start(bf16[512,256]{1,0:T(8,128)(2,1)S(1)} %get-tuple-element.215), channel_id=1, source_target_pairs={{0,16},{4,20},{8,24},{12,28},{16,0},{20,4},{24,8},{28,12},{1,17},{... | collective-permute-start | bytes 786440 | tf_op jit(solution)/shard_map/ppermute | solution.py:84
  6.9 12.0 %collective-permute-start.2 = (bf16[128,1024]{1,0:T(8,128)(2,1)}, bf16[128,1024]{1,0:T(8,128)(2,1)S(1)}, u32[]{:S(2)}, u32[]{:S(2)}) collective-permute-start(bf16[128,1024]{1,0:T(8,128)(2,1)} %param.33), channel_id=1, source_target_pairs={{0,4},{4,0},{8,12},{12,8},{16,20},{20,16},{24,28},{28,24},{1,5},{5... | collective-permute-start | bytes 786440 | tf_op jit(solution)/shard_map/ppermute | solution.py:84
  20.0 16.7 %collective-permute-start.5 = (bf16[2,512,256]{2,1,0:T(8,128)(2,1)S(1)}, bf16[2,512,256]{2,1,0:T(8,128)(2,1)S(1)}, u32[]{:S(2)}, u32[]{:S(2)}) collective-permute-start(bf16[2,512,256]{2,1,0:T(8,128)(2,1)S(1)} %pad_maximum_fusion.1.refs_0_), channel_id=1, source_target_pairs={{0,8},{4,12},{8,0},{12,4},{16,24},{20,28},{24,16},{28,20},{1,9},{5... | collective-permute-start | bytes 1572872 | tf_op jit(solution)/shard_map/ppermute | solution.py:84
  20.7 17.3 %collective-permute-start.3 = (bf16[2,160,256]{2,1,0:T(8,128)(2,1)S(1)}, bf16[2,160,256]{2,1,0:T(8,128)(2,1)S(1)}, u32[]{:S(2)}, u32[]{:S(2)}) collective-permute-start(bf16[2,160,256]{2,1,0:T(8,128)(2,1)S(1)} %pad_maximum_fusion.9), channel_id=1, source_target_pairs={{0,16},{4,20},{8,24},{12,28},{16,0},{20,4},{24,8},{28,12},{1,17},{... | collective-permute-start | bytes 491528 | tf_op jit(solution)/shard_map/ppermute | solution.py:84
  24.2 18.9 %collective-permute-start.6 = (bf16[2,512,256]{2,1,0:T(8,128)(2,1)S(1)}, bf16[2,512,256]{2,1,0:T(8,128)(2,1)S(1)}, u32[]{:S(2)}, u32[]{:S(2)}) collective-permute-start(bf16[2,512,256]{2,1,0:T(8,128)(2,1)S(1)} %pad_maximum_fusion.1.refs_0_), channel_id=1, source_target_pairs={{0,4},{4,0},{8,12},{12,8},{16,20},{20,16},{24,28},{28,24},{1,5},{5... | collective-permute-start | bytes 1572872 | tf_op jit(solution)/shard_map/ppermute | solution.py:84
  36.6 12.2 %collective-permute-start.7 = (bf16[2,512,256]{2,1,0:T(8,128)(2,1)S(1)}, bf16[2,512,256]{2,1,0:T(8,128)(2,1)S(1)}, u32[]{:S(2)}, u32[]{:S(2)}) collective-permute-start(bf16[2,512,256]{2,1,0:T(8,128)(2,1)S(1)} %collective-permute-done.5.refs_1_), channel_id=1, source_target_pairs={{0,4},{4,0},{8,12},{12,8},{16,20},{20,16},{24,28},{28,24},{1,5},{5... | collective-permute-start | bytes 1572872 | tf_op jit(solution)/shard_map/ppermute | solution.py:84
  38.0 14.8 %collective-permute-start.4 = (bf16[4,160,256]{2,1,0:T(8,128)(2,1)S(1)}, bf16[4,160,256]{2,1,0:T(8,128)(2,1)S(1)}, u32[]{:S(2)}, u32[]{:S(2)}) collective-permute-start(bf16[4,160,256]{2,1,0:T(8,128)(2,1)S(1)} %pad_maximum_fusion.6.refs_0_), channel_id=1, source_target_pairs={{0,8},{4,12},{8,0},{12,4},{16,24},{20,28},{24,16},{28,20},{1,9},{5... | collective-permute-start | bytes 983048 | tf_op jit(solution)/shard_map/ppermute | solution.py:84
  39.9 12.9 %collective-permute-start.8 = (bf16[128,1024]{1,0:T(8,128)(2,1)S(1)}, bf16[128,1024]{1,0:T(8,128)(2,1)S(1)}, u32[]{:S(2)}, u32[]{:S(2)}) collective-permute-start(bf16[128,1024]{1,0:T(8,128)(2,1)S(1)} %copy-done.22), channel_id=1, source_target_pairs={{0,16},{4,20},{8,24},{12,28},{16,0},{20,4},{24,8},{28,12},{1,17},{... | collective-permute-start | bytes 786440 | tf_op jit(solution)/shard_map/ppermute | solution.py:84
  52.9 17.0 %collective-permute-start.9 = (bf16[1024,256]{1,0:T(8,128)(2,1)S(1)}, bf16[1024,256]{1,0:T(8,128)(2,1)S(1)}, u32[]{:S(2)}, u32[]{:S(2)}) collective-permute-start(bf16[1024,256]{1,0:T(8,128)(2,1)S(1)} %get-tuple-element.125.refs_4_.refs_0_), channel_id=1, source_target_pairs={{0,2},{1,3},{2,0},{3,1},{4,6},{5,7},{6,4},{7,5},{8,10},{9,11},{10,... | collective-permute-start | bytes 1572872 | tf_op jit(solution)/shard_map/ppermute | solution.py:84
  54.4 13.1 %collective-permute-start.10 = (bf16[128,1024]{1,0:T(8,128)(2,1)S(1)}, bf16[128,1024]{1,0:T(8,128)(2,1)S(1)}, u32[]{:S(2)}, u32[]{:S(2)}) collective-permute-start(bf16[128,1024]{1,0:T(8,128)(2,1)S(1)} %copy-done.3), channel_id=1, source_target_pairs={{0,16},{4,20},{8,24},{12,28},{16,0},{20,4},{24,8},{28,12},{1,17},{... | collective-permute-start | bytes 786440 | tf_op jit(solution)/shard_map/ppermute | solution.py:84
  57.1 19.5 %collective-permute-start.12 = (bf16[2,128,1024]{2,1,0:T(8,128)(2,1)S(1)}, bf16[2,128,1024]{2,1,0:T(8,128)(2,1)S(1)}, u32[]{:S(2)}, u32[]{:S(2)}) collective-permute-start(bf16[2,128,1024]{2,1,0:T(8,128)(2,1)S(1)} %pad_maximum_fusion.2.refs_0_), channel_id=1, source_target_pairs={{0,8},{4,12},{8,0},{12,4},{16,24},{20,28},{24,16},{28,20},{1,9},{5... | collective-permute-start | bytes 1572872 | tf_op jit(solution)/shard_map/ppermute | solution.py:84
  59.0 17.6 %collective-permute-start.13 = (bf16[2,128,1024]{2,1,0:T(8,128)(2,1)S(1)}, bf16[2,128,1024]{2,1,0:T(8,128)(2,1)S(1)}, u32[]{:S(2)}, u32[]{:S(2)}) collective-permute-start(bf16[2,128,1024]{2,1,0:T(8,128)(2,1)S(1)} %pad_maximum_fusion.2.refs_0_), channel_id=1, source_target_pairs={{0,4},{4,0},{8,12},{12,8},{16,20},{20,16},{24,28},{28,24},{1,5},{5... | collective-permute-start | bytes 1572872 | tf_op jit(solution)/shard_map/ppermute | solution.py:84
  76.8 17.4 %collective-permute-start.18 = (bf16[3072,256]{1,0:T(8,128)(2,1)S(1)}, bf16[3072,256]{1,0:T(8,128)(2,1)S(1)}, u32[]{:S(2)}, u32[]{:S(2)}) collective-permute-start(bf16[3072,256]{1,0:T(8,128)(2,1)S(1)} %pad_maximum_fusion), channel_id=1, source_target_pairs={{0,1},{1,0},{2,3},{3,2},{4,5},{5,4},{6,7},{7,6},{8,9},{9,8},{10,11... | collective-permute-start | bytes 4718600 | tf_op jit(solution)/shard_map/ppermute | solution.py:84
  76.9 14.4 %collective-permute-start.15 = (bf16[2,128,1024]{2,1,0:T(8,128)(2,1)S(1)}, bf16[2,128,1024]{2,1,0:T(8,128)(2,1)S(1)}, u32[]{:S(2)}, u32[]{:S(2)}) collective-permute-start(bf16[2,128,1024]{2,1,0:T(8,128)(2,1)S(1)} %pad_maximum_fusion.3), channel_id=1, source_target_pairs={{0,8},{4,12},{8,0},{12,4},{16,24},{20,28},{24,16},{28,20},{1,9},{5... | collective-permute-start | bytes 1572872 | tf_op jit(solution)/shard_map/ppermute | solution.py:84
  78.0 14.4 %collective-permute-start.14 = (bf16[2,128,1024]{2,1,0:T(8,128)(2,1)S(1)}, bf16[2,128,1024]{2,1,0:T(8,128)(2,1)S(1)}, u32[]{:S(2)}, u32[]{:S(2)}) collective-permute-start(bf16[2,128,1024]{2,1,0:T(8,128)(2,1)S(1)} %collective-permute-done.12.refs_2_), channel_id=1, source_target_pairs={{0,4},{4,0},{8,12},{12,8},{16,20},{20,16},{24,28},{28,24},{1,5},{5... | collective-permute-start | bytes 1572872 | tf_op jit(solution)/shard_map/ppermute | solution.py:84
  92.5 14.3 %collective-permute-start.21 = (bf16[2,128,1024]{2,1,0:T(8,128)(2,1)S(1)}, bf16[2,128,1024]{2,1,0:T(8,128)(2,1)S(1)}, u32[]{:S(2)}, u32[]{:S(2)}) collective-permute-start(bf16[2,128,1024]{2,1,0:T(8,128)(2,1)S(1)} %collective-permute-done.15.refs_4_), channel_id=1, source_target_pairs={{0,4},{4,0},{8,12},{12,8},{16,20},{20,16},{24,28},{28,24},{1,5},{5... | collective-permute-start | bytes 1572872 | tf_op jit(solution)/shard_map/ppermute | solution.py:84
  112.7 14.0 %collective-permute-start.25 = (bf16[256,1024]{1,0:T(8,128)(2,1)S(1)}, bf16[256,1024]{1,0:T(8,128)(2,1)S(1)}, u32[]{:S(2)}, u32[]{:S(2)}) collective-permute-start(bf16[256,1024]{1,0:T(8,128)(2,1)S(1)} %get-tuple-element.156), channel_id=1, source_target_pairs={{0,2},{1,3},{2,0},{3,1},{4,6},{5,7},{6,4},{7,5},{8,10},{9,11},{10,... | collective-permute-start | bytes 1572872 | tf_op jit(solution)/shard_map/ppermute | solution.py:84
  115.1 11.6 %collective-permute-start.24 = (bf16[256,1024]{1,0:T(8,128)(2,1)S(1)}, bf16[256,1024]{1,0:T(8,128)(2,1)S(1)}, u32[]{:S(2)}, u32[]{:S(2)}) collective-permute-start(bf16[256,1024]{1,0:T(8,128)(2,1)S(1)} %get-tuple-element.165), channel_id=1, source_target_pairs={{0,1},{1,0},{2,3},{3,2},{4,5},{5,4},{6,7},{7,6},{8,9},{9,8},{10,11... | collective-permute-start | bytes 1572872 | tf_op jit(solution)/shard_map/ppermute | solution.py:84
  117.8 13.7 %collective-permute-start.30 = (bf16[4,128,512]{2,1,0:T(8,128)(2,1)S(1)}, bf16[4,128,512]{2,1,0:T(8,128)(2,1)S(1)}, u32[]{:S(2)}, u32[]{:S(2)}) collective-permute-start(bf16[4,128,512]{2,1,0:T(8,128)(2,1)S(1)} %pad_maximum_fusion.5.refs_0_), channel_id=1, source_target_pairs={{0,4},{4,0},{8,12},{12,8},{16,20},{20,16},{24,28},{28,24},{1,5},{5... | collective-permute-start | bytes 1572872 | tf_op jit(solution)/shard_map/ppermute | solution.py:84
  120.2 11.4 %collective-permute-start.27 = (bf16[256,1024]{1,0:T(8,128)(2,1)S(1)}, bf16[256,1024]{1,0:T(8,128)(2,1)S(1)}, u32[]{:S(2)}, u32[]{:S(2)}) collective-permute-start(bf16[256,1024]{1,0:T(8,128)(2,1)S(1)} %down_rows.6), channel_id=1, source_target_pairs={{0,1},{1,0},{2,3},{3,2},{4,5},{5,4},{6,7},{7,6},{8,9},{9,8},{10,11... | collective-permute-start | bytes 1572872 | tf_op jit(solution)/shard_map/ppermute | solution.py:84
  135.7 16.4 %collective-permute-start.23 = (bf16[256,1024]{1,0:T(8,128)(2,1)S(1)}, bf16[256,1024]{1,0:T(8,128)(2,1)S(1)}, u32[]{:S(2)}, u32[]{:S(2)}) collective-permute-start(bf16[256,1024]{1,0:T(8,128)(2,1)S(1)} %down_rows.5), channel_id=1, source_target_pairs={{0,1},{1,0},{2,3},{3,2},{4,5},{5,4},{6,7},{7,6},{8,9},{9,8},{10,11... | collective-permute-start | bytes 1572872 | tf_op jit(solution)/shard_map/ppermute | solution.py:84
  136.3 15.9 %collective-permute-start.28 = (bf16[256,1024]{1,0:T(8,128)(2,1)S(1)}, bf16[256,1024]{1,0:T(8,128)(2,1)S(1)}, u32[]{:S(2)}, u32[]{:S(2)}) collective-permute-start(bf16[256,1024]{1,0:T(8,128)(2,1)S(1)} %down_rows.7), channel_id=1, source_target_pairs={{0,2},{1,3},{2,0},{3,1},{4,6},{5,7},{6,4},{7,5},{8,10},{9,11},{10,... | collective-permute-start | bytes 1572872 | tf_op jit(solution)/shard_map/ppermute | solution.py:84
  154.3 15.6 %collective-permute-start.34 = (bf16[512,1024]{1,0:T(8,128)(2,1)S(1)}, bf16[512,1024]{1,0:T(8,128)(2,1)S(1)}, u32[]{:S(2)}, u32[]{:S(2)}) collective-permute-start(bf16[512,1024]{1,0:T(8,128)(2,1)S(1)} %project_back.3.own), channel_id=1, source_target_pairs={{0,1},{1,0},{2,3},{3,2},{4,5},{5,4},{6,7},{7,6},{8,9},{9,8},{10,11... | collective-permute-start | bytes 3145736 | tf_op jit(solution)/shard_map/ppermute | solution.py:84
  155.4 14.4 %collective-permute-start.36 = (bf16[256,1024]{1,0:T(8,128)(2,1)S(1)}, bf16[256,1024]{1,0:T(8,128)(2,1)S(1)}, u32[]{:S(2)}, u32[]{:S(2)}) collective-permute-start(bf16[256,1024]{1,0:T(8,128)(2,1)S(1)} %project_back.5), channel_id=1, source_target_pairs={{0,2},{1,3},{2,0},{3,1},{4,6},{5,7},{6,4},{7,5},{8,10},{9,11},{10,... | collective-permute-start | bytes 1572872 | tf_op jit(solution)/shard_map/ppermute | solution.py:84
  (40 other events, 396.2 us)
